TPU v7x, 256 devices: a whole 4x4x8 slice. The times are simulated.
256 devices in a mesh: leaf: 64 (over x, z, core), cols: 4 (over y).
Axes of the slice: x: 4, y: 4, z: 8, core: 2. Of those that a mesh axis runs over, the one named last changes fastest.
Arguments:
- samples: bfloat16 [2048, 131072], P('cols', 'leaf'), may hold values from -6 to 6
- order_perm: int32 [131072], P('leaf'), may hold values from 0 to 131071, as said below
- leaf_factor: bfloat16 [128, 1024, 1024], P('leaf'), may hold values from -0.1875 to 0.1875
- bases: bfloat16 [7, 64, 131072], P(None, None, 'leaf'), may hold values from -110 to 110
- coupling: float32 [7, 64, 64, 64], P(None, 'leaf'), may hold values from -1 to 1, as said below
- ranks: int32 [7, 128], replicated, may hold values from 16 to 64
Outputs:
- transformed: float32 [2048, 131072], P('cols', 'leaf')
Inputs may be any that keep to these rules, and one draw needn't show every extreme that they name: `order_perm`: each aligned block of 2048 positions holds a permutation of the same block's indices. coupling[l, d] equals coupling[l, e] whenever d and e lie in the same level-l node, that is d // 2**l == e // 2**l.
All inputs are finite; a program needn't handle non-finite values.
Results may differ from a plain program's by a relative error of at most 0.0003.
Values sent between devices are 32-bit elements; how exact they have to be, the bound alone decides.
No kernel may reach another device: no remote copies, remote signals or barrier semaphores. Data moves between devices by JAX's collectives and lax.ppermute only.
A program may use at most 128 MiB of HBM per device.

v0:
```python
import math

import jax
import jax.numpy as jnp
from jax import lax
from jax.sharding import PartitionSpec as P

HIGH = lax.Precision.HIGHEST


def from_everyone(array, axis):
    copies = jnp.broadcast_to(array, (lax.axis_size(axis), *array.shape))
    return lax.all_to_all(copies, axis, split_axis=0, concat_axis=0, tiled=True)


def taken_together(array, axis):
    return from_everyone(array, axis).sum(axis=0)


def from_partner(array, axis, stride):
    return lax.ppermute(array, axis, [(i, i ^ 1 << stride) for i in range(lax.axis_size(axis))])


def chol_apply(system, right_side):
    lower_factor = jnp.linalg.cholesky(system)
    middle = lax.linalg.triangular_solve(lower_factor, right_side, left_side=True, lower=True)
    return lax.linalg.triangular_solve(
        lower_factor, middle, left_side=True, lower=True, transpose_a=True
    )


def coupled(coupling_now, gram_other, proj_other):
    rank_width = coupling_now.shape[-1]
    inner = jnp.matmul(coupling_now, gram_other, precision=HIGH)
    system = jnp.eye(rank_width, dtype=jnp.float32) + jnp.matmul(
        inner, coupling_now.T, precision=HIGH
    )
    return chol_apply(system, jnp.matmul(coupling_now, proj_other, precision=HIGH))


def rank_mask(rank_value, rank_width, scale):
    return (jnp.arange(rank_width, dtype=jnp.int32) < rank_value).astype(jnp.float32) * scale


def project(basis, field):
    return lax.dot_general(basis, field, (((1,), (1,)), ((), ())), precision=HIGH)


def expand(update, basis):
    return lax.dot_general(update, basis, (((0,), (0,)), ((), ())), precision=HIGH)


def local(samples, order_perm, leaf_factor, bases, coupling, ranks):
    dev_index = lax.axis_index("leaf")
    row_count = samples.shape[1]
    rank_width = bases.shape[1]
    leaf_rows = leaf_factor.shape[1]
    levels = bases.shape[0]
    local_order = order_perm - dev_index * row_count
    permuted = jnp.take(samples, local_order, axis=1)
    first_half = jnp.dot(
        permuted[:, :leaf_rows], leaf_factor[0], preferred_element_type=jnp.float32
    )
    second_half = jnp.dot(
        permuted[:, leaf_rows:], leaf_factor[1], preferred_element_type=jnp.float32
    )
    col_parts = lax.axis_size("cols")
    quarter = row_count // col_parts
    quarter_start = lax.axis_index("cols") * quarter
    slab = lax.dynamic_slice_in_dim(bases, quarter_start, quarter, 2).astype(jnp.float32)
    raw_grams = jnp.einsum("lrc,lsc->lrs", slab, slab, precision=HIGH)
    which_leaf = quarter_start // leaf_rows
    raw_first = raw_grams[0] * (which_leaf == 0).astype(jnp.float32)
    raw_second = raw_grams[0] * (which_leaf == 1).astype(jnp.float32)
    raw_all = jnp.concatenate([raw_first[None], raw_second[None], raw_grams[1:]], axis=0)
    grams = taken_together(raw_all, "cols")
    scale_zero = 1.0 / math.sqrt(leaf_rows)
    mask_first = rank_mask(ranks[0, 2 * dev_index], rank_width, scale_zero)
    mask_second = rank_mask(ranks[0, 2 * dev_index + 1], rank_width, scale_zero)
    base_zero = bases[0].astype(jnp.float32)
    basis_first = base_zero[:, :leaf_rows] * mask_first[:, None]
    basis_second = base_zero[:, leaf_rows:] * mask_second[:, None]
    proj_first = project(basis_first, first_half)
    proj_second = project(basis_second, second_half)
    gram_first = grams[0] * (mask_first[:, None] * mask_first[None, :])
    gram_second = grams[1] * (mask_second[:, None] * mask_second[None, :])
    coupling_zero = coupling[0, 0]
    update_first = coupled(coupling_zero, gram_second, proj_second)
    update_second = coupled(coupling_zero.T, gram_first, proj_first)
    first_half = first_half - expand(update_first, basis_first)
    second_half = second_half - expand(update_second, basis_second)
    field = jnp.concatenate([first_half, second_half], axis=1)
    all_grams = lax.all_gather(grams[2:][None], "leaf", axis=0, tiled=True)
    for tree_level in range(1, levels):
        child_span = 2 ** (tree_level - 1)
        child_index = dev_index // child_span
        is_second = child_index % 2
        sibling_index = child_index + 1 - 2 * is_second
        scale = 1.0 / math.sqrt(leaf_rows * 2**tree_level)
        mask_mine = rank_mask(ranks[tree_level, child_index * 2**tree_level], rank_width, scale)
        mask_other = rank_mask(ranks[tree_level, sibling_index * 2**tree_level], rank_width, scale)
        basis = bases[tree_level].astype(jnp.float32) * mask_mine[:, None]
        proj_mine = project(basis, field)
        payload = proj_mine
        for bit_pos in range(tree_level - 1):
            payload = payload + from_partner(payload, "leaf", bit_pos)
        received = from_partner(payload, "leaf", tree_level - 1)
        level_slab = lax.dynamic_slice_in_dim(
            all_grams[:, tree_level - 1], sibling_index * child_span, child_span, 0
        )
        gram_raw = jnp.sum(level_slab, axis=0)
        gram_other = gram_raw * (mask_other[:, None] * mask_other[None, :])
        coupling_now = coupling[tree_level, 0]
        rotated = jnp.where(is_second == 1, coupling_now.T, coupling_now)
        update = coupled(rotated, gram_other, received)
        field = field - expand(update, basis)
    return field


def solution(mesh):
    in_specs = (
        P("cols", "leaf"),
        P("leaf"),
        P("leaf", None, None),
        P(None, None, "leaf"),
        P(None, "leaf", None, None),
        P(),
    )
    out_specs = P("cols", "leaf")
    return jax.shard_map(local, mesh=mesh, in_specs=in_specs, out_specs=out_specs, check_vma=False)
```

profile of v0, /device:TPU:16, one launch (start us, length us, event | category | flops | bytes accessed | tf_op | source)
XLA Modules:
  0.0 352.3 jit_solution(13387176542879933447)
XLA Ops:
  8.8 11.4 %all_to_all.5 = f32[4,1,32768]{2,1,0:T(1,128)S(1)} all-to-all(f32[4,1,32768]{2,1,0:T(1,128)S(1)} %reshape.319), channel_id=1, replica_groups=mesh['leaf'=64,'cols'=4] {'cols'}, dimensions={0} | all-to-all | bytes 1048576 | tf_op jit(solution)/shard_map/all_to_all | solution.py:13
  28.0 9.2 %gather_fusion = bf16[2048,512]{1,0:T(8,128)(2,1)} fusion(bf16[512,2048]{0,1:T(8,128)(2,1)S(1)} %copy.53, s32[2048]{0:T(1024)S(1)} %fusion.161), kind=kCustom, calls=%fused_computation | custom fusion | bytes 4202496 | tf_op jit(solution)/shard_map/jit(_take)/gather | solution.py:60
  57.1 5.8 %cholesky.134 = f32[64,64]{1,0:T(8,128)S(1)} custom-call(f32[64,64]{1,0:T(8,128)S(1)} %fusion.113), custom_call_target="Cholesky" | custom-call | tf_op jit(solution)/shard_map/jit(cholesky)/cholesky | solution.py:25
  64.3 4.9 %custom-call.23 = f32[1,64,64]{1,2,0:T(8,128)S(1)} custom-call(f32[1,64,64]{2,1,0:T(8,128)S(1)} %fusion.59), custom_call_target="InvertDiagBlocksLowerTriangular" | custom-call | tf_op jit(solution)/shard_map/triangular_solve/custom-call.2 | solution.py:27
  69.9 5.8 %cholesky.145 = f32[64,64]{1,0:T(8,128)S(1)} custom-call(f32[64,64]{1,0:T(8,128)S(1)} %fusion.108), custom_call_target="Cholesky" | custom-call | tf_op jit(solution)/shard_map/jit(cholesky)/cholesky | solution.py:25
  77.1 4.9 %custom-call.25 = f32[1,64,64]{1,2,0:T(8,128)S(1)} custom-call(f32[1,64,64]{2,1,0:T(8,128)S(1)} %fusion.60), custom_call_target="InvertDiagBlocksLowerTriangular" | custom-call | tf_op jit(solution)/shard_map/triangular_solve/custom-call.2 | solution.py:27
  89.1 5.3 %fusion.1 = f32[64,512]{1,0:T(8,128)S(1)} fusion(f32[512,1024]{1,0:T(8,128)S(1)} %convolution_subtract_fusion.5, f32[512,1024]{1,0:T(8,128)S(1)} %convolution_subtract_fusion.6, f32[64]{0:T(128)S(1)} %compare_select_fusion.11, bf16[7,64,2048]{2,1,0:T(8,128)(2,1)} %param.14), kind=kOutput, calls=%fused_computation.3 | convolution fusion | flops 806617088 | bytes 4587776 | tf_op jit(solution)/shard_map/dot_general | solution.py:46
  96.4 20.8 %all-gather.3.cloned.1.call-done = f32[384,64,64]{2,1,0:T(8,128)} async-done(((f32[6,64,64]{2,1,0:T(8,128)}), f32[384,64,64]{2,1,0:T(8,128)}) %all-gather.3.cloned.1.call-update) | async-done | bytes 6291472 | tf_op jit(solution)/shard_map/all_gather | solution.py:93
  117.2 9.2 %fusion.165 = (f32[64,1,64,64]{3,2,1,0:T(8,128)}, f32[64,1,64,64]{3,2,1,0:T(8,128)}, f32[64,1,64,64]{3,2,1,0:T(8,128)}, f32[64,1,64,64]{3,2,1,0:T(8,128)S(1)}, f...) fusion(f32[64,6,64,64]{3,2,1,0:T(8,128)} %bitcast.317), kind=kLoop, calls=%fused_computation.280 | loop fusion | bytes 12582912 | tf_op jit(solution)/shard_map/slice | solution.py:109
  128.3 5.8 %cholesky.167 = f32[64,64]{1,0:T(8,128)S(1)} custom-call(f32[64,64]{1,0:T(8,128)S(1)} %fusion.97), custom_call_target="Cholesky" | custom-call | tf_op jit(solution)/shard_map/jit(cholesky)/cholesky | solution.py:25
  135.5 5.8 %cholesky.156 = f32[64,64]{1,0:T(8,128)S(1)} custom-call(f32[64,64]{1,0:T(8,128)S(1)} %fusion.102), custom_call_target="Cholesky" | custom-call | tf_op jit(solution)/shard_map/jit(cholesky)/cholesky | solution.py:25
  142.6 4.9 %custom-call.27 = f32[1,64,64]{1,2,0:T(8,128)S(1)} custom-call(f32[1,64,64]{2,1,0:T(8,128)S(1)} %fusion.61), custom_call_target="InvertDiagBlocksLowerTriangular" | custom-call | tf_op jit(solution)/shard_map/triangular_solve/custom-call.2 | solution.py:27
  148.2 5.6 %fusion = f32[512,2048]{1,0:T(8,128)S(1)} fusion(f32[512,1024]{1,0:T(8,128)} %copy-done.5, f32[512,1024]{1,0:T(8,128)S(1)} %convolution_subtract_fusion.6, f32[64,512]{1,0:T(8,128)S(1)} %fusion.100, f32[64]{0:T(128)S(1)} %compare_select_fusion.11, bf16[7,64,2048]{2,1,0:T(8,128)(2,1)} %param.14), kind=kOutput, calls=%fused_computation.2 | convolution fusion | flops 807665664 | bytes 8782080 | tf_op jit(solution)/shard_map/dot_general | solution.py:50
  153.7 5.5 %fusion.14 = f32[64,512]{1,0:T(8,128)S(1)} fusion(f32[512,2048]{1,0:T(8,128)S(1)} %fusion, f32[64]{0:T(128)S(1)} %compare_select_fusion.9, bf16[7,64,2048]{2,1,0:T(8,128)(2,1)} %param.14), kind=kOutput, calls=%fused_computation.40 | convolution fusion | flops 805568512 | bytes 4587776 | tf_op jit(solution)/shard_map/dot_general | solution.py:46
  159.6 5.8 %cholesky.178 = f32[64,64]{1,0:T(8,128)S(1)} custom-call(f32[64,64]{1,0:T(8,128)S(1)} %fusion.92), custom_call_target="Cholesky" | custom-call | tf_op jit(solution)/shard_map/jit(cholesky)/cholesky | solution.py:25
  168.4 4.9 %custom-call.29 = f32[1,64,64]{1,2,0:T(8,128)S(1)} custom-call(f32[1,64,64]{2,1,0:T(8,128)S(1)} %fusion.62), custom_call_target="InvertDiagBlocksLowerTriangular" | custom-call | tf_op jit(solution)/shard_map/triangular_solve/custom-call.2 | solution.py:27
  174.2 5.7 %convolution_subtract_fusion.4 = f32[512,2048]{1,0:T(8,128)S(1)} fusion(f32[512,2048]{1,0:T(8,128)} %copy-done.4, f32[64,512]{1,0:T(8,128)S(1)} %fusion.95, f32[64]{0:T(128)S(1)} %compare_select_fusion.9, bf16[7,64,2048]{2,1,0:T(8,128)(2,1)S(1)} %copy-done.9), kind=kOutput, calls=%fused_computation.8 | convolution fusion | flops 806617088 | bytes 8782336 | tf_op jit(solution)/shard_map/dot_general | solution.py:50
  194.9 6.9 %collective-permute-done.5 = f32[64,512]{1,0:T(8,128)S(1)} collective-permute-done((f32[64,512]{1,0:T(8,128)S(1)}, f32[64,512]{1,0:T(8,128)S(1)}, u32[]{:S(2)}, u32[]{:S(2)}) %collective-permute-start.5) | collective-permute-done | bytes 131104 | tf_op jit(solution)/shard_map/ppermute | solution.py:21
  202.7 5.7 %convolution_subtract_fusion.3 = f32[512,2048]{1,0:T(8,128)S(1)} fusion(f32[512,2048]{1,0:T(8,128)} %copy-done.3, f32[64,512]{1,0:T(8,128)S(1)} %fusion.90, f32[64]{0:T(128)S(1)} %compare_select_fusion.7, bf16[7,64,2048]{2,1,0:T(8,128)(2,1)S(1)} %copy-done.9), kind=kOutput, calls=%fused_computation.7 | convolution fusion | flops 806617088 | bytes 8782336 | tf_op jit(solution)/shard_map/dot_general | solution.py:50
  214.2 5.8 %cholesky.189 = f32[64,64]{1,0:T(8,128)S(1)} custom-call(f32[64,64]{1,0:T(8,128)S(1)} %fusion.87), custom_call_target="Cholesky" | custom-call | tf_op jit(solution)/shard_map/jit(cholesky)/cholesky | solution.py:25
  224.0 5.7 %collective-permute-done.8 = f32[64,512]{1,0:T(8,128)S(1)} collective-permute-done((f32[64,512]{1,0:T(8,128)S(1)}, f32[64,512]{1,0:T(8,128)S(1)}, u32[]{:S(2)}, u32[]{:S(2)}) %collective-permute-start.8) | collective-permute-done | bytes 131104 | tf_op jit(solution)/shard_map/ppermute | solution.py:21
  233.0 4.9 %custom-call.33 = f32[1,64,64]{1,2,0:T(8,128)S(1)} custom-call(f32[1,64,64]{2,1,0:T(8,128)S(1)} %fusion.64), custom_call_target="InvertDiagBlocksLowerTriangular" | custom-call | tf_op jit(solution)/shard_map/triangular_solve/custom-call.2 | solution.py:27
  241.3 5.9 %convolution_subtract_fusion.2 = f32[512,2048]{1,0:T(8,128)S(1)} fusion(f32[512,2048]{1,0:T(8,128)} %copy-done.2, f32[64,512]{1,0:T(8,128)S(1)} %fusion.85, f32[64]{0:T(128)S(1)} %compare_select_fusion.5, bf16[7,64,2048]{2,1,0:T(8,128)(2,1)S(1)} %copy-done.9), kind=kOutput, calls=%fused_computation.6 | convolution fusion | flops 806617088 | bytes 8782336 | tf_op jit(solution)/shard_map/dot_general | solution.py:50
  253.2 5.3 %collective-permute-done.11 = f32[64,512]{1,0:T(8,128)S(1)} collective-permute-done((f32[64,512]{1,0:T(8,128)S(1)}, f32[64,512]{1,0:T(8,128)S(1)}, u32[]{:S(2)}, u32[]{:S(2)}) %collective-permute-start.11) | collective-permute-done | bytes 131104 | tf_op jit(solution)/shard_map/ppermute | solution.py:21
  259.6 5.8 %cholesky.200 = f32[64,64]{1,0:T(8,128)S(1)} custom-call(f32[64,64]{1,0:T(8,128)S(1)} %fusion.82), custom_call_target="Cholesky" | custom-call | tf_op jit(solution)/shard_map/jit(cholesky)/cholesky | solution.py:25
  271.3 8.0 %collective-permute-done.13 = f32[64,512]{1,0:T(8,128)S(1)} collective-permute-done((f32[64,512]{1,0:T(8,128)S(1)}, f32[64,512]{1,0:T(8,128)S(1)}, u32[]{:S(2)}, u32[]{:S(2)}) %collective-permute-start.13) | collective-permute-done | bytes 131104 | tf_op jit(solution)/shard_map/ppermute | solution.py:21
  280.3 4.9 %custom-call.35 = f32[1,64,64]{1,2,0:T(8,128)S(1)} custom-call(f32[1,64,64]{2,1,0:T(8,128)S(1)} %fusion.65), custom_call_target="InvertDiagBlocksLowerTriangular" | custom-call | tf_op jit(solution)/shard_map/triangular_solve/custom-call.2 | solution.py:27
  286.0 5.7 %convolution_subtract_fusion.1 = f32[512,2048]{1,0:T(8,128)S(1)} fusion(f32[512,2048]{1,0:T(8,128)} %copy-done.1, f32[64,512]{1,0:T(8,128)S(1)} %fusion.80, f32[64]{0:T(128)S(1)} %compare_select_fusion.3, bf16[7,64,2048]{2,1,0:T(8,128)(2,1)S(1)} %copy-done.9), kind=kOutput, calls=%fused_computation.5 | convolution fusion | flops 806617088 | bytes 8782336 | tf_op jit(solution)/shard_map/dot_general | solution.py:50
  298.4 5.6 %collective-permute-done.16 = f32[64,512]{1,0:T(8,128)S(1)} collective-permute-done((f32[64,512]{1,0:T(8,128)S(1)}, f32[64,512]{1,0:T(8,128)S(1)}, u32[]{:S(2)}, u32[]{:S(2)}) %collective-permute-start.16) | collective-permute-done | bytes 131104 | tf_op jit(solution)/shard_map/ppermute | solution.py:21
  305.3 7.6 %collective-permute-done.17 = f32[64,512]{1,0:T(8,128)S(1)} collective-permute-done((f32[64,512]{1,0:T(8,128)S(1)}, f32[64,512]{1,0:T(8,128)S(1)}, u32[]{:S(2)}, u32[]{:S(2)}) %collective-permute-start.17) | collective-permute-done | bytes 131104 | tf_op jit(solution)/shard_map/ppermute | solution.py:21
  315.9 5.8 %cholesky.211 = f32[64,64]{1,0:T(8,128)S(1)} custom-call(f32[64,64]{1,0:T(8,128)S(1)} %fusion.77), custom_call_target="Cholesky" | custom-call | tf_op jit(solution)/shard_map/jit(cholesky)/cholesky | solution.py:25
  338.6 6.7 %convolution_subtract_fusion = f32[512,2048]{1,0:T(8,128)} fusion(f32[512,2048]{1,0:T(8,128)} %copy-done, f32[64,512]{1,0:T(8,128)S(1)} %fusion.75, f32[64]{0:T(128)S(1)} %compare_select_fusion.1, bf16[7,64,2048]{2,1,0:T(8,128)(2,1)S(1)} %copy-done.9), kind=kOutput, calls=%fused_computation.4 | convolution fusion | flops 806617088 | bytes 8782336 | tf_op jit(solution)/shard_map/dot_general | solution.py:50
  (217 shorter events, 125.5 us)
Async XLA Ops:
  6.5 110.6 %all-gather.3.cloned.1.call-start = ((), (), s32[]{:S(2)}) async-start(), calls=%async_computation.1 | async-start | bytes 12779520 | tf_op jit(solution)/shard_map/all_gather | solution.py:93
  28.0 9.2 %copy-start.12 = (s32[7,128]{1,0:T(8,128)S(1)}, s32[7,128]{1,0:T(8,128)}, u32[]{:S(2)}) copy-start(s32[7,128]{1,0:T(8,128)} %param.16) | copy-start | bytes 10756
  49.0 4.9 %copy-start.6 = (f32[512,1024]{1,0:T(8,128)}, f32[512,1024]{1,0:T(8,128)S(1)}, u32[]{:S(2)}) copy-start(f32[512,1024]{1,0:T(8,128)S(1)} %fusion.2) | copy-start | bytes 6291460
  83.2 3.7 %copy-start.7 = (f32[512,1024]{1,0:T(8,128)S(1)}, f32[512,1024]{1,0:T(8,128)}, u32[]{:S(2)}) copy-start(f32[512,1024]{1,0:T(8,128)} %copy-done.6) | copy-start | bytes 6291460
  89.1 5.4 %copy-start.5 = (f32[512,1024]{1,0:T(8,128)}, f32[512,1024]{1,0:T(8,128)S(1)}, u32[]{:S(2)}) copy-start(f32[512,1024]{1,0:T(8,128)S(1)} %convolution_subtract_fusion.5) | copy-start | bytes 6291460
  94.5 1.6 collective-permute-start
  153.7 5.5 %copy-start.4 = (f32[512,2048]{1,0:T(8,128)}, f32[512,2048]{1,0:T(8,128)S(1)}, u32[]{:S(2)}) copy-start(f32[512,2048]{1,0:T(8,128)S(1)} %fusion) | copy-start | bytes 12582916
  153.7 20.4 %copy-start.9 = (bf16[7,64,2048]{2,1,0:T(8,128)(2,1)S(1)}, bf16[7,64,2048]{2,1,0:T(8,128)(2,1)}, u32[]{:S(2)}) copy-start(bf16[7,64,2048]{2,1,0:T(8,128)(2,1)} %param.14) | copy-start | bytes 5505028
  159.3 6.9 %collective-permute-start.1 = (f32[64,512]{1,0:T(8,128)S(1)}, f32[64,512]{1,0:T(8,128)S(1)}, u32[]{:S(2)}, u32[]{:S(2)}) collective-permute-start(f32[64,512]{1,0:T(8,128)S(1)} %fusion.14), channel_id=1, source_target_pairs={{0,4},{4,0},{8,12},{12,8},{16,20},{20,16},{24,28},{28,24},{32,36},... | collective-permute-start | bytes 393224 | tf_op jit(solution)/shard_map/ppermute | solution.py:21
  166.2 7.1 %collective-permute-start.2 = (f32[64,512]{1,0:T(8,128)S(1)}, f32[64,512]{1,0:T(8,128)S(1)}, u32[]{:S(2)}, u32[]{:S(2)}) collective-permute-start(f32[64,512]{1,0:T(8,128)S(1)} %add.215), channel_id=1, source_target_pairs={{0,8},{4,12},{8,0},{12,4},{16,24},{20,28},{24,16},{28,20},{32,40},... | collective-permute-start | bytes 393224 | tf_op jit(solution)/shard_map/ppermute | solution.py:21
  179.8 4.2 %copy-start.3 = (f32[512,2048]{1,0:T(8,128)}, f32[512,2048]{1,0:T(8,128)S(1)}, u32[]{:S(2)}) copy-start(f32[512,2048]{1,0:T(8,128)S(1)} %convolution_subtract_fusion.4) | copy-start | bytes 12582916
  184.0 1.4 collective-permute-start.3
  185.5 7.2 %collective-permute-start.4 = (f32[64,512]{1,0:T(8,128)S(1)}, f32[64,512]{1,0:T(8,128)S(1)}, u32[]{:S(2)}, u32[]{:S(2)}) collective-permute-start(f32[64,512]{1,0:T(8,128)S(1)} %add.222), channel_id=1, source_target_pairs={{0,8},{4,12},{8,0},{12,4},{16,24},{20,28},{24,16},{28,20},{32,40},... | collective-permute-start | bytes 393224 | tf_op jit(solution)/shard_map/ppermute | solution.py:21
  192.7 9.1 %collective-permute-start.5 = (f32[64,512]{1,0:T(8,128)S(1)}, f32[64,512]{1,0:T(8,128)S(1)}, u32[]{:S(2)}, u32[]{:S(2)}) collective-permute-start(f32[64,512]{1,0:T(8,128)S(1)} %add.223), channel_id=1, source_target_pairs={{0,16},{4,20},{8,24},{12,28},{16,0},{20,4},{24,8},{28,12},{32,48},... | collective-permute-start | bytes 393224 | tf_op jit(solution)/shard_map/ppermute | solution.py:21
  208.4 4.2 %copy-start.2 = (f32[512,2048]{1,0:T(8,128)}, f32[512,2048]{1,0:T(8,128)S(1)}, u32[]{:S(2)}) copy-start(f32[512,2048]{1,0:T(8,128)S(1)} %convolution_subtract_fusion.3) | copy-start | bytes 12582916
  212.6 1.4 collective-permute-start.6
  214.0 6.0 %collective-permute-start.7 = (f32[64,512]{1,0:T(8,128)S(1)}, f32[64,512]{1,0:T(8,128)S(1)}, u32[]{:S(2)}, u32[]{:S(2)}) collective-permute-start(f32[64,512]{1,0:T(8,128)S(1)} %add.230), channel_id=1, source_target_pairs={{0,8},{4,12},{8,0},{12,4},{16,24},{20,28},{24,16},{28,20},{32,40},... | collective-permute-start | bytes 393224 | tf_op jit(solution)/shard_map/ppermute | solution.py:21
  220.1 9.6 %collective-permute-start.8 = (f32[64,512]{1,0:T(8,128)S(1)}, f32[64,512]{1,0:T(8,128)S(1)}, u32[]{:S(2)}, u32[]{:S(2)}) collective-permute-start(f32[64,512]{1,0:T(8,128)S(1)} %add.231), channel_id=1, source_target_pairs={{0,16},{4,20},{8,24},{12,28},{16,0},{20,4},{24,8},{28,12},{32,48},... | collective-permute-start | bytes 393224 | tf_op jit(solution)/shard_map/ppermute | solution.py:21
  229.7 10.7 %collective-permute-start.9 = (f32[64,512]{1,0:T(8,128)S(1)}, f32[64,512]{1,0:T(8,128)S(1)}, u32[]{:S(2)}, u32[]{:S(2)}) collective-permute-start(f32[64,512]{1,0:T(8,128)S(1)} %add.232), channel_id=1, source_target_pairs={{0,32},{4,36},{8,40},{12,44},{16,48},{20,52},{24,56},{28,60},{32,0... | collective-permute-start | bytes 393224 | tf_op jit(solution)/shard_map/ppermute | solution.py:21
  247.2 4.2 %copy-start.1 = (f32[512,2048]{1,0:T(8,128)}, f32[512,2048]{1,0:T(8,128)S(1)}, u32[]{:S(2)}) copy-start(f32[512,2048]{1,0:T(8,128)S(1)} %convolution_subtract_fusion.2) | copy-start | bytes 12582916
  251.4 1.4 collective-permute-start.10
  252.9 5.6 %collective-permute-start.11 = (f32[64,512]{1,0:T(8,128)S(1)}, f32[64,512]{1,0:T(8,128)S(1)}, u32[]{:S(2)}, u32[]{:S(2)}) collective-permute-start(f32[64,512]{1,0:T(8,128)S(1)} %add.239), channel_id=1, source_target_pairs={{0,8},{4,12},{8,0},{12,4},{16,24},{20,28},{24,16},{28,20},{32,40},... | collective-permute-start | bytes 393224 | tf_op jit(solution)/shard_map/ppermute | solution.py:21
  258.5 8.5 %collective-permute-start.12 = (f32[64,512]{1,0:T(8,128)S(1)}, f32[64,512]{1,0:T(8,128)S(1)}, u32[]{:S(2)}, u32[]{:S(2)}) collective-permute-start(f32[64,512]{1,0:T(8,128)S(1)} %add.240), channel_id=1, source_target_pairs={{0,16},{4,20},{8,24},{12,28},{16,0},{20,4},{24,8},{28,12},{32,48},... | collective-permute-start | bytes 393224 | tf_op jit(solution)/shard_map/ppermute | solution.py:21
  267.0 12.2 %collective-permute-start.13 = (f32[64,512]{1,0:T(8,128)S(1)}, f32[64,512]{1,0:T(8,128)S(1)}, u32[]{:S(2)}, u32[]{:S(2)}) collective-permute-start(f32[64,512]{1,0:T(8,128)S(1)} %add.241), channel_id=1, source_target_pairs={{0,32},{4,36},{8,40},{12,44},{16,48},{20,52},{24,56},{28,60},{32,0... | collective-permute-start | bytes 393224 | tf_op jit(solution)/shard_map/ppermute | solution.py:21
  279.3 5.9 %collective-permute-start.14 = (f32[64,512]{1,0:T(8,128)S(1)}, f32[64,512]{1,0:T(8,128)S(1)}, u32[]{:S(2)}, u32[]{:S(2)}) collective-permute-start(f32[64,512]{1,0:T(8,128)S(1)} %add.242), channel_id=1, source_target_pairs={{0,64},{4,68},{8,72},{12,76},{16,80},{20,84},{24,88},{28,92},{32,9... | collective-permute-start | bytes 393224 | tf_op jit(solution)/shard_map/ppermute | solution.py:21
  291.7 4.2 %copy-start = (f32[512,2048]{1,0:T(8,128)}, f32[512,2048]{1,0:T(8,128)S(1)}, u32[]{:S(2)}) copy-start(f32[512,2048]{1,0:T(8,128)S(1)} %convolution_subtract_fusion.1) | copy-start | bytes 12582916
  295.9 2.1 collective-permute-start.15
  298.0 6.0 %collective-permute-start.16 = (f32[64,512]{1,0:T(8,128)S(1)}, f32[64,512]{1,0:T(8,128)S(1)}, u32[]{:S(2)}, u32[]{:S(2)}) collective-permute-start(f32[64,512]{1,0:T(8,128)S(1)} %add.249), channel_id=1, source_target_pairs={{0,8},{4,12},{8,0},{12,4},{16,24},{20,28},{24,16},{28,20},{32,40},... | collective-permute-start | bytes 393224 | tf_op jit(solution)/shard_map/ppermute | solution.py:21
  304.0 8.8 %collective-permute-start.17 = (f32[64,512]{1,0:T(8,128)S(1)}, f32[64,512]{1,0:T(8,128)S(1)}, u32[]{:S(2)}, u32[]{:S(2)}) collective-permute-start(f32[64,512]{1,0:T(8,128)S(1)} %add.250), channel_id=1, source_target_pairs={{0,16},{4,20},{8,24},{12,28},{16,0},{20,4},{24,8},{28,12},{32,48},... | collective-permute-start | bytes 393224 | tf_op jit(solution)/shard_map/ppermute | solution.py:21
  312.9 11.7 %collective-permute-start.18 = (f32[64,512]{1,0:T(8,128)S(1)}, f32[64,512]{1,0:T(8,128)S(1)}, u32[]{:S(2)}, u32[]{:S(2)}) collective-permute-start(f32[64,512]{1,0:T(8,128)S(1)} %add.251), channel_id=1, source_target_pairs={{0,32},{4,36},{8,40},{12,44},{16,48},{20,52},{24,56},{28,60},{32,0... | collective-permute-start | bytes 393224 | tf_op jit(solution)/shard_map/ppermute | solution.py:21
  324.7 5.5 %collective-permute-start.19 = (f32[64,512]{1,0:T(8,128)S(1)}, f32[64,512]{1,0:T(8,128)S(1)}, u32[]{:S(2)}, u32[]{:S(2)}) collective-permute-start(f32[64,512]{1,0:T(8,128)S(1)} %add.252), channel_id=1, source_target_pairs={{0,64},{4,68},{8,72},{12,76},{16,80},{20,84},{24,88},{28,92},{32,9... | collective-permute-start | bytes 393224 | tf_op jit(solution)/shard_map/ppermute | solution.py:21
  330.2 7.5 %collective-permute-start.20 = (f32[64,512]{1,0:T(8,128)S(1)}, f32[64,512]{1,0:T(8,128)S(1)}, u32[]{:S(2)}, u32[]{:S(2)}) collective-permute-start(f32[64,512]{1,0:T(8,128)S(1)} %add.253), channel_id=1, source_target_pairs={{0,128},{4,132},{8,136},{12,140},{16,144},{20,148},{24,152},{28,15... | collective-permute-start | bytes 393224 | tf_op jit(solution)/shard_map/ppermute | solution.py:21
  (4 other events, 9.6 us)
Sparse Core Ops, SparseCore 0:
  24.4 92.7 all-gather.2
where the time goes:
time: 357 us; the launch traced here: 352 us
  other arithmetic  116 us (32%)
  matrix products  88.1 us (25%)
  waiting for transfers between devices  71.9 us (20%)
  local copies, waits for them, and re-layouts  26.5 us (7%)
  starting transfers between devices  23.6 us (7%)
  between operations  15 us (4%)
  blocking collectives  11.4 us (3%)
    another operation x24, other arithmetic, chol_apply(): lower_factor = jnp.linalg.cholesky(system)  52.5 us
    ppermute x21, waiting for transfers between devices, from_partner(): lax.ppermute(array, axis, [(i, i ^ 1 << stride) for i in range(lax.axis_s...  51.1 us
    another operation x16, other arithmetic, chol_apply(): lax.linalg.triangular_solve(lower_factor, middle, left_side=True, lower=T...  44.2 us
    dot_general x8, matrix products, expand(): lax.dot_general(update, basis, (((0,), (0,)), ((), ())), precision=HIGH)  41 us
    dot_general x8, matrix products, project(): lax.dot_general(basis, field, (((1,), (1,)), ((), ())), precision=HIGH)  32 us
    ppermute x21, starting transfers between devices, from_partner(): lax.ppermute(array, axis, [(i, i ^ 1 << stride) for i in range(lax.axis_s...  23.6 us
    all_gather x1, waiting for transfers between devices, local(): all_grams = lax.all_gather(grams[2:][None], 'leaf', axis=0, tiled=True)  20.8 us
    all_to_all x1, blocking collectives, from_everyone(): return lax.all_to_all(copies, axis, split_axis=0, concat_axis=0, tiled=True)  11.4 us
  transfers between devices with their start and end apart: 22, of which 15 were waited for; matrix products, arithmetic and copies ran while one was open for 37% of the time, Pallas kernels for 0%

commit v1 on v0

v1 whole, which is shorter than its diff:
```python
import functools
import math

import jax
import jax.numpy as jnp
from jax import lax
from jax.experimental import pallas as pl
from jax.experimental.pallas import tpu as pltpu
from jax.sharding import PartitionSpec as P


F32, BF16 = jnp.float32, jnp.bfloat16
HIGH = lax.Precision.HIGHEST
NT = (((1,), (1,)), ((), ()))
NN = (((1,), (0,)), ((), ()))
TN = (((0,), (0,)), ((), ()))

LEAF, R, ROWS, COLS, LEVELS = 1024, 64, 2048, 512, 7
UP = (LEVELS - 1) * R
BLK = 256
MIB = 1024 * 1024
VMEM = pl.BlockSpec(memory_space=pltpu.VMEM)
SMEM = pl.BlockSpec(memory_space=pltpu.SMEM)
HBM = pl.BlockSpec(memory_space=pltpu.HBM)


def params(mib, **more):
    return pltpu.CompilerParams(vmem_limit_bytes=mib * MIB, **more)


def cost(flops, moved):
    return pl.CostEstimate(flops=int(flops), bytes_accessed=int(moved), transcendentals=0)


def shape(*dims, dtype=F32):
    return jax.ShapeDtypeStruct(dims, dtype)


def stay(array):
    return pltpu.with_memory_space_constraint(array, pltpu.HBM)


def split(value):
    high = value.astype(BF16)
    return high, (value - high.astype(F32)).astype(BF16)


def dot(left, right, dims):
    return lax.dot_general(left, right, dims, preferred_element_type=F32)


def dot_high(left, right, dims):
    return lax.dot_general(left, right, dims, precision=HIGH, preferred_element_type=F32)


def twice(value, axis):
    return jnp.concatenate([value, value], axis=axis)


def gram_kernel(bases_ref, samples_ref, wide_ref, mine_ref, theirs_ref, first_ref, gram0_ref, cross0_ref, kept_ref,
                held_ref, tiles_ref, sems):
    load = pltpu.make_async_copy(bases_ref, held_ref, sems.at[0])
    load.start()
    keep = pltpu.make_async_copy(samples_ref, kept_ref, sems.at[1])
    keep.start()
    load.wait()
    nothing = jnp.zeros((R, LEAF), BF16)
    wide_ref[0:UP] = held_ref[1:].reshape(UP, ROWS)
    wide_ref[UP:UP + R, 0:LEAF] = held_ref[0, :, 0:LEAF]
    wide_ref[UP:UP + R, LEAF:] = nothing
    wide_ref[UP + R:, 0:LEAF] = nothing
    wide_ref[UP + R:, LEAF:] = held_ref[0, :, LEAF:]
    wide = wide_ref[...]
    gram = dot(wide, wide, NT)
    first_ref[...] = gram[:R, :UP]
    for part in range(8):
        tile = 0
        for level in range(6):
            top = level * R + 8 * part
            for lane in range(level // 2, 3):
                tiles_ref[part, tile] = gram[top:top + 8, lane * 128:lane * 128 + 128]
                tile += 1
    part, other = lax.axis_index("cols"), lax.axis_index("core") * 4
    mine_ref[...] = tiles_ref[part + other]
    theirs_ref[...] = tiles_ref[part + 4 - other]
    gram0_ref[...] = gram[UP:, UP:]
    cross0_ref[...] = gram[UP:, :UP]
    keep.wait()


def grams(bases, samples):
    return pl.pallas_call(
        gram_kernel,
        out_shape=(
            shape(512, ROWS, dtype=BF16), shape(12, 8, 128), shape(12, 8, 128), shape(R, UP), shape(128, 128),
            shape(128, UP),
            pltpu.VMEM((COLS, ROWS), BF16),
        ),
        in_specs=[HBM] * 2,
        out_specs=(VMEM,) * 7,
        scratch_shapes=[pltpu.VMEM((LEVELS, R, ROWS), BF16), pltpu.VMEM((8, 12, 8, 128), F32), pltpu.SemaphoreType.DMA((2,))],
        compiler_params=params(14),
        cost_estimate=cost(2e9, 4e6),
        name="gram",
    )(stay(bases), stay(samples))


def permute_block(samples_ref, order_ref, out_ref, begin):
    def block(j, carry):
        columns = pl.ds(pl.multiple_of(j * BLK, BLK), BLK)
        rows = lax.broadcasted_iota(jnp.int32, (ROWS, BLK), 0)
        source = pl.ds(pl.multiple_of(begin + j * BLK, BLK), BLK)
        local = jnp.bitwise_and(order_ref[:, source], ROWS - 1)
        chosen = (rows == local).astype(F32).astype(BF16)
        out_ref[:, columns] = dot(samples_ref[...], chosen, NN).astype(BF16)
        return carry

    lax.fori_loop(0, LEAF // BLK, block, 0)


def permute_first_kernel(samples_ref, order_ref, factor_ref, out_ref, kept_ref, sem):
    keep = pltpu.make_async_copy(factor_ref, kept_ref, sem)
    keep.start()
    permute_block(samples_ref, order_ref, out_ref, 0)
    keep.wait()


def permute_second_kernel(samples_ref, order_ref, out_ref):
    permute_block(samples_ref, order_ref, out_ref, LEAF)


def permute_first(samples, order, factor):
    return pl.pallas_call(
        permute_first_kernel,
        out_shape=(shape(COLS, LEAF, dtype=BF16), pltpu.VMEM((2, LEAF, LEAF), BF16)),
        in_specs=[VMEM, VMEM, HBM],
        out_specs=(VMEM,) * 2,
        scratch_shapes=[pltpu.SemaphoreType.DMA],
        compiler_params=params(14),
        cost_estimate=cost(COLS * ROWS * ROWS, 4e6),
        name="permute_first",
    )(samples, order, stay(factor))


def permute_second(samples, order):
    return pl.pallas_call(
        permute_second_kernel,
        out_shape=shape(COLS, LEAF, dtype=BF16),
        in_specs=[VMEM, VMEM],
        out_specs=VMEM,
        compiler_params=params(10),
        cost_estimate=cost(COLS * ROWS * ROWS, 4e6),
        name="permute_second",
    )(samples, order)


def leaf_kernel(permuted_ref, factor_ref, field_ref, *, half):
    def block(j, carry):
        columns = pl.ds(pl.multiple_of(j * 512, 512), 512)
        field_ref[:, columns] = dot(permuted_ref[...], factor_ref[half, :, columns], NN)
        return carry

    lax.fori_loop(0, 2, block, 0)


def leaf_product(permuted, factor, half):
    return pl.pallas_call(
        functools.partial(leaf_kernel, half=half),
        out_shape=shape(COLS, LEAF),
        in_specs=[VMEM] * 2,
        out_specs=VMEM,
        compiler_params=params(12),
        cost_estimate=cost(2 * COLS * LEAF * LEAF, 5e6),
    )(permuted, factor)


def project_kernel(first_ref, second_ref, wide_ref, q_ref):
    def rows_of(i, carry):
        rows = pl.ds(pl.multiple_of(i * 256, 256), 256)
        total = None
        for half, source in enumerate((first_ref, second_ref)):
            for part in split(source[rows, :]):
                term = dot(part, wide_ref[:, half * LEAF:(half + 1) * LEAF], NT)
                total = term if total is None else total + term
        q_ref[rows, :] = total
        return carry

    lax.fori_loop(0, COLS // 256, rows_of, 0)


def project(first, second, wide):
    return pl.pallas_call(
        project_kernel,
        out_shape=shape(COLS, 512),
        in_specs=[VMEM] * 3,
        out_specs=VMEM,
        compiler_params=params(14),
        cost_estimate=cost(4 * COLS * 512 * ROWS, 7e6),
        name="project",
    )(first, second, wide)


def coupling_forms(link):
    flipped = link.T
    plain = twice(flipped, 0).T
    return plain, twice(link, 0).T


def lanes(rows=R):
    return lax.broadcasted_iota(jnp.int32, (rows, 128), 1)


def system(link_dup, gram_tile, upper_half, rank_own, scale):
    lane = lanes()
    joint = jnp.where(jnp.bitwise_and(lane, R - 1) < rank_own, link_dup * scale, 0.0)
    placed = jnp.where((lane >= R) == upper_half, joint, 0.0)
    inner = dot_high(gram_tile, twice(placed, 0), NT)
    outer = dot_high(joint[:, :R], inner, NN)
    row = lax.broadcasted_iota(jnp.int32, (R, 128), 0)
    outer = outer + jnp.where(row == lane, 1.0, 0.0)
    return jnp.where(lane < R, outer, joint)


def eliminate(work_ref, count):
    row = lax.broadcasted_iota(jnp.int32, (count, R, 128), 1)
    tile_row = lax.broadcasted_iota(jnp.int32, (count, 8, 128), 1)

    def block(step, carry):
        top = pl.multiple_of(step * 8, 8)
        here = (row >= top) & (row < top + 8)
        value = work_ref[...]
        tile = work_ref[:, pl.ds(top, 8), :]
        heads = [jnp.broadcast_to(tile[:, :, j:j + 1], (count, 8, 128)) for j in range(8)]
        columns = [jnp.broadcast_to(value[:, :, j:j + 1], (count, R, 128)) for j in range(8)]
        for j in range(8):
            inverse = 1.0 / heads[j][:, j:j + 1, :]
            pivot = tile[:, j:j + 1, :] * inverse
            tile = jnp.where(tile_row == j, pivot, tile - heads[j] * pivot)
            for i in range(j + 1, 8):
                element = heads[i][:, j:j + 1, :] * inverse
                heads[i] = jnp.where(tile_row == j, element, heads[i] - heads[j] * element)
        for j in range(8):
            value = value - columns[j] * tile[:, j:j + 1, :]
        value = jnp.where(here, jnp.concatenate([tile] * 8, axis=1), value)
        work_ref[...] = pltpu.roll(value, 120, 2)
        return carry

    lax.fori_loop(0, 8, block, 0)


def solved(work_ref, item, rank_sibling, scale):
    row = lax.broadcasted_iota(jnp.int32, (R, 128), 0)
    keep = (row < rank_sibling) & (lanes() < R)
    return jnp.where(keep, work_ref[item] * scale, 0.0)


def pair(value):
    high, low = split(value)
    return jnp.concatenate([high, low], axis=1)


def apply_nt(value_pair, weight):
    high, low = split(weight)
    return dot(value_pair, twice(high, 1), NT) + dot(value_pair, twice(low, 1), NT)


def apply_nn(value_pair, weight):
    high, low = split(weight)
    return dot(value_pair, twice(high, 0), NN) + dot(value_pair, twice(low, 0), NN)


def packed(value_pair, weight):
    nothing = jnp.zeros_like(weight)
    left = jnp.concatenate([value_pair[0:128], value_pair[256:384]], axis=0)
    right = jnp.concatenate([value_pair[128:256], value_pair[384:512]], axis=0)
    return apply_nt(left, jnp.concatenate([weight, nothing], 0)) + apply_nt(right, jnp.concatenate([nothing, weight], 0))


def leaf_index():
    return (lax.axis_index("x") * 8 + lax.axis_index("z")) * 2 + lax.axis_index("core")


def scale_of(level):
    return 1.0 / math.sqrt(LEAF * 2**level)


def solve_early_kernel(ranks_ref, link_ref, gram0_ref, own1_ref, sib1_ref, from0_ref, weight_ref, onward_ref, work_ref):
    leaf = leaf_index()
    second = lax.axis_index("core")
    plain0, flipped0 = coupling_forms(link_ref[0, 0])
    plain1, flipped1 = coupling_forms(link_ref[1, 0])
    rank_f, rank_s = ranks_ref[0, 2 * leaf], ranks_ref[0, 2 * leaf + 1]
    rank_1, rank_1s = ranks_ref[1, 2 * leaf], ranks_ref[1, 2 * jnp.bitwise_xor(leaf, 1)]
    scale0, scale1 = scale_of(0), scale_of(1)
    work_ref[0] = system(flipped0, gram0_ref[0:R], False, rank_f, scale0)
    work_ref[1] = system(plain0, gram0_ref[R:], True, rank_s, scale0)
    work_ref[2] = system(jnp.where(second == 1, plain1, flipped1), own1_ref[:, :128], False, rank_1, scale1)
    eliminate(work_ref, 3)
    from0_ref[R:] = solved(work_ref, 0, rank_s, scale0)
    from0_ref[0:R] = pltpu.roll(solved(work_ref, 1, rank_f, scale0), R, 1)
    weight = solved(work_ref, 2, rank_1s, scale1)
    weight_ref[...] = weight
    onward_ref[...] = dot_high(weight, sib1_ref[...], TN)


def solve_early(ranks, coupling, gram0, own1, sib1):
    return pl.pallas_call(
        solve_early_kernel,
        out_shape=(shape(128, 128), shape(R, 128), shape(128, UP)),
        in_specs=[SMEM] + [VMEM] * 4,
        out_specs=(VMEM,) * 3,
        scratch_shapes=[pltpu.VMEM((3, R, 128), F32)],
        compiler_params=params(8),
        cost_estimate=cost(3e9, 4e6),
        name="solve_early",
    )(ranks, coupling, gram0, own1, sib1)


def early_kernel(q_ref, from0_ref, cross0_ref, weight_ref, onward_ref, u0_ref, u1_ref, x_ref):
    u0 = apply_nt(pair(q_ref[:, UP:]), from0_ref[...])
    u0_ref[...] = u0
    zero = pair(u0)
    cross0 = cross0_ref[...]
    head = pair(q_ref[:, :128] - apply_nn(zero, cross0[:, :128]))
    both = packed(head, weight_ref[...])
    u1_ref[0] = both[:128]
    u1_ref[1] = both[128:]
    onward = onward_ref[...]
    for group in range(3):
        at = slice(group * 128, group * 128 + 128)
        x_ref[:, at] = q_ref[:, at] - apply_nn(zero, cross0[:, at]) - apply_nn(head, onward[:, at])


def early(q, from0, cross0, weight, onward):
    return pl.pallas_call(
        early_kernel,
        out_shape=(shape(COLS, 128), shape(2, 128, 128), shape(COLS, UP)),
        in_specs=[VMEM] * 5,
        out_specs=(VMEM,) * 3,
        compiler_params=params(12),
        cost_estimate=cost(3e9, 4e6),
        name="early",
    )(q, from0, cross0, weight, onward)


OWN_TILE = {2: 0, 3: 3, 4: 5, 5: 7, 6: 8}
ONWARD = {2: ((1, 1), (2, 2)), 3: ((3, 1), (4, 2)), 4: ((6, 2),), 5: ((7, 2),), 6: ()}


def late_kernel(ranks_ref, link_ref, near_ref, far_ref, x_ref, keep_ref, send_ref, pk_ref, work_ref):
    leaf, col, core = leaf_index(), lax.axis_index("cols"), lax.axis_index("core")
    for other, source in ((0, near_ref), (1, far_ref)):
        for slot, offset in enumerate((0, 1, 3, 2)):
            part = jnp.bitwise_xor(core, other) * 4 + jnp.bitwise_xor(col, offset)
            rows = pl.ds(pl.multiple_of(part * 8, 8), 8)
            for tile in range(9):
                pk_ref[tile, rows, :] = source[slot, tile]
    systems = []
    for level in range(2, 7):
        child = jnp.right_shift(leaf, level - 1)
        plain, flipped = coupling_forms(link_ref[level, 0])
        rank = ranks_ref[level, jnp.left_shift(child, level)]
        which = jnp.where(jnp.bitwise_and(child, 1) == 1, plain, flipped)
        systems.append(system(which, pk_ref[OWN_TILE[level]], level % 2 == 0, rank, scale_of(level)))
    for item in range(5):
        work_ref[item] = systems[item]
    eliminate(work_ref, 5)
    weights, onwards = {}, {}
    for level in range(2, 7):
        child = jnp.right_shift(leaf, level - 1)
        rank = ranks_ref[level, jnp.left_shift(jnp.bitwise_xor(child, 1), level)]
        weight = solved(work_ref, level - 2, rank, scale_of(level))
        if level % 2 == 0:
            weight = pltpu.roll(weight, R, 1)
        weights[level] = weight
        onwards[level] = [(dot_high(weight, pk_ref[tile], TN), target) for tile, target in ONWARD[level]]
    groups = [x_ref[:, g * 128:g * 128 + 128] for g in range(3)]
    for level in range(2, 7):
        value = pair(groups[(level - 1) // 2])
        for onward, target in onwards[level]:
            groups[target] = groups[target] - apply_nn(value, onward)
        both = packed(value, weights[level])
        keep_ref[level - 2] = jnp.where(core == 0, both[:128], both[128:])
        send_ref[level - 2] = jnp.where(core == 0, both[128:], both[:128])


def late(ranks, coupling, near, far, x):
    return pl.pallas_call(
        late_kernel,
        out_shape=(shape(5, 128, 128), shape(5, 128, 128)),
        in_specs=[SMEM] + [VMEM] * 4,
        out_specs=(VMEM,) * 2,
        scratch_shapes=[pltpu.VMEM((9, R, 128), F32), pltpu.VMEM((5, R, 128), F32)],
        compiler_params=params(16),
        cost_estimate=cost(4e9, 4e6),
        name="late",
    )(ranks, coupling, near, far, x)


def turned(value):
    return pltpu.roll(value, 4, 0)


def two_kernel(keep_ref, recv_ref, two_ref):
    two_ref[...] = keep_ref[0] + recv_ref[0]


def level_two(keep, recv):
    return pl.pallas_call(
        two_kernel,
        out_shape=shape(128, 128),
        in_specs=[VMEM] * 2,
        out_specs=VMEM,
        compiler_params=params(4),
        cost_estimate=cost(1e6, 1e5),
        name="two",
    )(keep, recv)


def deal_kernel(keep_ref, recv_ref, out_ref):
    top = lax.broadcasted_iota(jnp.int32, (8, 128), 0) < 4
    for t in range(16):
        rows = slice(8 * t, 8 * t + 8)
        for group in range(2):
            first = keep_ref[2 * group + 1, rows] + recv_ref[2 * group + 1, rows]
            second = keep_ref[2 * group + 2, rows] + recv_ref[2 * group + 2, rows]
            to = slice(8 * group, 8 * group + 8)
            out_ref[2 * t, to] = jnp.where(top, first, turned(second))
            out_ref[2 * t + 1, to] = jnp.where(top, turned(first), second)


def deal(keep, recv):
    return pl.pallas_call(
        deal_kernel,
        out_shape=shape(32, 16, 128),
        in_specs=[VMEM] * 2,
        out_specs=VMEM,
        compiler_params=params(4),
        cost_estimate=cost(1e8, 1e6),
        name="deal",
    )(keep, recv)


def collect_kernel(got_ref, out_ref):
    top = lax.broadcasted_iota(jnp.int32, (8, 128), 0) < 4
    pieces = [got_ref[q] for q in range(32)]
    sums = []
    for _ in range(4):
        pieces = [pieces[2 * c] + pieces[2 * c + 1] for c in range(len(pieces) // 2)]
        sums.append(pieces)
    for e in range(32):
        parts = [sums[k][(e >> (k + 1)) ^ 1] for k in range(4)]
        out_ref[e, 0:8] = jnp.where(top, parts[0][0:8], parts[1][0:8])
        out_ref[e, 8:16] = jnp.where(top, parts[2][8:16], parts[3][8:16])


def collect(got):
    return pl.pallas_call(
        collect_kernel,
        out_shape=shape(32, 16, 128),
        in_specs=[VMEM],
        out_specs=VMEM,
        compiler_params=params(4),
        cost_estimate=cost(1e8, 1e6),
        name="collect",
    )(got)


def final_kernel(field0_ref, field1_ref, wide_ref, u0_ref, u1_ref, near2_ref, far2_ref, near_ref, far_ref,
                 out_ref, left_ref, all_ref):
    step = pl.program_id(0)
    half = step // (LEAF // BLK)

    @pl.when(step == 0)
    def _():
        core = lax.axis_index("core")
        top = lax.broadcasted_iota(jnp.int32, (8, 128), 0) < 4
        lane = lanes(8)

        def unpack(first, second, begin, group):
            columns = slice(group * 128, group * 128 + 128)
            upper = pl.ds(pl.multiple_of(begin, 8), 8)
            lower = pl.ds(pl.multiple_of(begin + 128, 8), 8)
            all_ref[upper, columns] = jnp.where(lane < R, first, pltpu.roll(second, R, 1))
            all_ref[lower, columns] = jnp.where(lane < R, pltpu.roll(first, R, 1), second)

        for two, rest, start in ((near2_ref, near_ref, core), (far2_ref, far_ref, 1 - core)):
            for t in range(16):
                rows = slice(8 * t, 8 * t + 8)
                begin = start * 256 + 8 * t
                unpack(u1_ref[start, rows], two[rows], begin, 0)
                for group in range(2):
                    one = rest[2 * t, 8 * group:8 * group + 8]
                    other = rest[2 * t + 1, 8 * group:8 * group + 8]
                    unpack(
                        jnp.where(top, one, turned(other)), jnp.where(top, turned(one), other), begin, group + 1
                    )
        high, low = split(all_ref[...])
        left_ref[:, 0:UP] = high
        left_ref[:, 512:512 + UP] = low
        high, low = split(u0_ref[...])
        left_ref[:, UP:512] = high
        left_ref[:, 512 + UP:] = low

    right = wide_ref[...]
    update = dot(left_ref[:, :512], right, NN) + dot(left_ref[:, 512:], right, NN)

    @pl.when(half == 0)
    def _():
        out_ref[...] = field0_ref[...] - update

    @pl.when(half == 1)
    def _():
        out_ref[...] = field1_ref[...] - update


def final(field0, field1, wide, *updates):
    steps = LEAF // BLK
    return pl.pallas_call(
        final_kernel,
        grid=(ROWS // BLK,),
        out_shape=shape(COLS, ROWS),
        in_specs=[
            pl.BlockSpec((COLS, BLK), lambda j: (0, jnp.minimum(j, steps - 1))),
            pl.BlockSpec((COLS, BLK), lambda j: (0, jnp.maximum(j - steps, 0))),
            pl.BlockSpec((512, BLK), lambda j: (0, j)),
        ] + [VMEM] * 6,
        out_specs=pl.BlockSpec((COLS, BLK), lambda j: (0, j)),
        scratch_shapes=[pltpu.VMEM((COLS, 1024), BF16), pltpu.VMEM((COLS, UP), F32)],
        compiler_params=params(16),
        cost_estimate=cost(2 * COLS * 1024 * ROWS, 12e6),
        name="final",
    )(stay(field0), stay(field1), stay(wide), *updates)


def swap(array, mask, axis):
    return lax.ppermute(array, axis, [(i, i ^ mask) for i in range(lax.axis_size(axis))])


def local(samples, order_perm, leaf_factor, bases, coupling, ranks):
    wide, mine, theirs, own1, gram0, cross0, samples = grams(bases, samples)
    order = order_perm.reshape(1, ROWS)
    got = swap(theirs, 1, "core")
    sib1 = swap(own1, 1, "core")
    permuted0, factor = permute_first(samples, order, leaf_factor)
    permuted1 = permute_second(samples, order)
    field0 = leaf_product(permuted0, factor, 0)
    field1 = leaf_product(permuted1, factor, 1)
    q = project(field0, field1, wide)
    from0, weight1, onward1 = solve_early(ranks, coupling, gram0, own1, sib1)
    u0, u1, x = early(q, from0, cross0, weight1, onward1)

    chip = (mine + got)[3:]
    got = swap(chip, 1, "z")
    low_lane = lax.broadcasted_iota(jnp.int32, (8, 128), 1) < R
    pack = [chip[0], got[1], got[2]]
    total = chip[3:] + got[3:]
    got = swap(total, 2, "z")
    pack += [jnp.where(low_lane, total[0], got[0]), got[1]]
    total = total[2:] + got[2:]
    got = swap(total, 4, "z")
    pack += [total[0], got[1]]
    total = total[2:] + got[2:]
    got = swap(total, 1, "x")
    pack += [jnp.where(low_lane, total[0], got[0]), total[1] + got[1]]
    pack = jnp.stack(pack)
    got = swap(pack, 1, "cols")
    pack = jnp.stack([pack, got])
    got = swap(pack, 3, "cols")
    near = jnp.concatenate([pack, got], axis=0)
    far = swap(near, 1, "core")
    u1 = swap(u1, 1, "core")
    keep, send = late(ranks, coupling, near, far, x)
    got = swap(send, 1, "core")
    two = level_two(keep, got)
    two = swap(two, 1, "z")
    dealt = deal(keep, got)
    got = lax.all_to_all(dealt, ("x", "z"), 0, 0, tiled=True)
    far_two = swap(two, 1, "core")
    total = collect(got)
    back = lax.all_to_all(total, ("x", "z"), 0, 0, tiled=True)
    far_back = swap(back, 1, "core")
    return final(field0, field1, wide, u0, u1, two, far_two, back, far_back)


def solution(mesh):
    fine = jax.sharding.Mesh(mesh.devices.reshape(4, 8, 2, 4), ("x", "z", "core", "cols"))
    leaf = ("x", "z", "core")
    in_specs = (
        P("cols", leaf),
        P(leaf),
        P(leaf, None, None),
        P(None, None, leaf),
        P(None, leaf, None, None),
        P(),
    )
    out_specs = P("cols", leaf)
    return jax.shard_map(local, mesh=fine, in_specs=in_specs, out_specs=out_specs, check_vma=False)
```

time: 357 us -> 115 us (0.32)
  the two profiles are of different devices: /device:TPU:16 before, /device:TPU:1 now
where the time goes in v1:
time: 115 us
  Pallas kernels  39.6 us (34%)
  blocking collectives  35.7 us (31%)
  starting transfers between devices  26.7 us (23%)
  waiting for transfers between devices  12.4 us (11%)
    ppermute x14, starting transfers between devices, swap(): lax.ppermute(array, axis, [(i, i ^ mask) for i in range(lax.axis_size(axi...  26.7 us
    all_to_all x1, blocking collectives, local(): got = lax.all_to_all(dealt, ('x', 'z'), 0, 0, tiled=True)  19.7 us
    all_to_all x1, blocking collectives, local(): back = lax.all_to_all(total, ('x', 'z'), 0, 0, tiled=True)  16.1 us
    ppermute x14, waiting for transfers between devices, swap(): lax.ppermute(array, axis, [(i, i ^ mask) for i in range(lax.axis_size(axi...  12.4 us
    pallas_call x1, Pallas kernels, late(): pl.pallas_call(late_kernel, out_shape=(shape(5, 128, 128), shape(5, 128,...  9.33 us
    pallas_call x1, Pallas kernels, final(): pl.pallas_call(final_kernel, grid=(ROWS // BLK,), out_shape=shape(COLS, R...  9.14 us
    pallas_call x1, Pallas kernels, solve_early(): pl.pallas_call(solve_early_kernel, out_shape=(shape(128, 128), shape(R, 1...  5.43 us
    pallas_call x1, Pallas kernels, permute_first(): pl.pallas_call(permute_first_kernel, out_shape=(shape(COLS, LEAF, dtype=B...  2.9 us
  transfers between devices with their start and end apart: 14, of which 7 were waited for; matrix products, arithmetic and copies ran while one was open for 0% of the time, Pallas kernels for 16%

profile of v1, /device:TPU:1, one launch (start us, length us, event | category | flops | bytes accessed | tf_op | source)
XLA Modules:
  0.0 114.6 jit_solution(14353941558490879230)
XLA Ops:
  0.0 2.9 %gram.1 = (bf16[512,2048]{1,0:T(8,128)(2,1)S(1)}, f32[12,8,128]{2,1,0:T(8,128)S(1)}, f32[12,8,128]{2,1,0:T(8,128)S(1)}, f32[64,384]{1,0:T(8,128)S(1)}, f32[128,1...) custom-call(bf16[7,64,2048]{2,1,0:T(8,128)(2,1)} %bases_ref.1, bf16[512,2048]{1,0:T(8,128)(2,1)} %samples_ref.1), custom_call_target="tpu_custom_call" | custom-call | flops 2000000000 | bytes 4000000 | tf_op jit(solution)/shard_map/gram/pallas_call | solution.py:92
  2.9 3.3 %collective-permute-start = (f32[64,384]{1,0:T(8,128)S(1)}, f32[64,384]{1,0:T(8,128)S(1)}, u32[]{:S(2)}, u32[]{:S(2)}) collective-permute-start(f32[64,384]{1,0:T(8,128)S(1)} %get-tuple-element.27.own1_ref), channel_id=1, source_target_pairs={{0,4},{4,0},{1,5},{5,1},{2,6},{6,2},{3,7},{7,3},{8,12},{12,8},{9,1... | collective-permute-start | bytes 294920 | tf_op jit(solution)/shard_map/ppermute | solution.py:537
  6.2 0.1 collective-permute-start.2
  6.3 2.9 %permute_second.1.permuted_ref = bf16[512,1024]{1,0:T(8,128)(2,1)S(1)} custom-call(bf16[512,2048]{1,0:T(8,128)(2,1)S(1)} %get-tuple-element.22.samples_ref, s32[1,2048]{1,0:T(1,128)S(1)} %bitcast.3), custom_call_target="tpu_custom_call" | custom-call | flops 2147483648 | bytes 4000000 | tf_op jit(solution)/shard_map/permute_second/pallas_call | solution.py:146
  9.2 2.9 %permute_first.1 = (bf16[512,1024]{1,0:T(8,128)(2,1)S(1)}, bf16[2,1024,1024]{2,1,0:T(8,128)(2,1)S(1)}) custom-call(bf16[512,2048]{1,0:T(8,128)(2,1)S(1)} %get-tuple-element.22.samples_ref, s32[1,2048]{1,0:T(1,128)S(1)} %bitcast.4, bf16[2,1024,1024]{2,1,0:T(8,128)(2,1)} %factor_ref.1), custom_call_target="tpu_custom_call" | custom-call | flops 2147483648 | bytes 4000000 | tf_op jit(solution)/shard_map/permute_first/pallas_call | solution.py:133
  12.1 1.4 %shard_map.64.first_ref.field0_ref = f32[512,1024]{1,0:T(8,128)S(1)} custom-call(bf16[512,1024]{1,0:T(8,128)(2,1)S(1)} %get-tuple-element.23.permuted_ref, bf16[2,1024,1024]{2,1,0:T(8,128)(2,1)S(1)} %get-tuple-element.24.factor_ref), custom_call_target="tpu_custom_call" | custom-call | flops 1073741824 | bytes 5000000 | tf_op jit(solution)/shard_map/pallas_call | solution.py:167
  13.5 1.4 %shard_map.65.second_ref.field1_ref = f32[512,1024]{1,0:T(8,128)S(1)} custom-call(bf16[512,1024]{1,0:T(8,128)(2,1)S(1)} %permute_second.1.permuted_ref, bf16[2,1024,1024]{2,1,0:T(8,128)(2,1)S(1)} %get-tuple-element.24.factor_ref), custom_call_target="tpu_custom_call" | custom-call | flops 1073741824 | bytes 5000000 | tf_op jit(solution)/shard_map/pallas_call | solution.py:167
  15.1 2.8 %collective-permute-done.3 = f32[9,8,128]{2,1,0:T(8,128)S(1)} collective-permute-done((f32[9,8,128]{2,1,0:T(8,128)S(1)}, f32[9,8,128]{2,1,0:T(8,128)S(1)}, u32[]{:S(2)}, u32[]{:S(2)}) %collective-permute-start.3) | collective-permute-done | bytes 36896 | tf_op jit(solution)/shard_map/ppermute | solution.py:537
  17.9 1.5 %collective-permute-start.4 = (f32[6,8,128]{2,1,0:T(8,128)S(1)}, f32[6,8,128]{2,1,0:T(8,128)S(1)}, u32[]{:S(2)}, u32[]{:S(2)}) collective-permute-start(f32[6,8,128]{2,1,0:T(8,128)S(1)} %slice_add_fusion), channel_id=1, source_target_pairs={{0,16},{8,24},{16,0},{24,8},{32,48},{40,56},{48,32},{56,40},{1,17}... | collective-permute-start | bytes 73736 | tf_op jit(solution)/shard_map/ppermute | solution.py:537
  19.4 2.1 %collective-permute-done.4 = f32[6,8,128]{2,1,0:T(8,128)S(1)} collective-permute-done((f32[6,8,128]{2,1,0:T(8,128)S(1)}, f32[6,8,128]{2,1,0:T(8,128)S(1)}, u32[]{:S(2)}, u32[]{:S(2)}) %collective-permute-start.4) | collective-permute-done | bytes 24608 | tf_op jit(solution)/shard_map/ppermute | solution.py:537
  21.5 5.2 %collective-permute-start.5 = (f32[4,8,128]{2,1,0:T(8,128)S(1)}, f32[4,8,128]{2,1,0:T(8,128)S(1)}, u32[]{:S(2)}, u32[]{:S(2)}) collective-permute-start(f32[4,8,128]{2,1,0:T(8,128)S(1)} %slice_add_fusion.1), channel_id=1, source_target_pairs={{0,32},{8,40},{16,48},{24,56},{32,0},{40,8},{48,16},{56,24},{1,33}... | collective-permute-start | bytes 49160 | tf_op jit(solution)/shard_map/ppermute | solution.py:537
  26.7 1.3 %collective-permute-done.5 = f32[4,8,128]{2,1,0:T(8,128)S(1)} collective-permute-done((f32[4,8,128]{2,1,0:T(8,128)S(1)}, f32[4,8,128]{2,1,0:T(8,128)S(1)}, u32[]{:S(2)}, u32[]{:S(2)}) %collective-permute-start.5) | collective-permute-done | bytes 16416 | tf_op jit(solution)/shard_map/ppermute | solution.py:537
  28.0 1.0 collective-permute-start.6
  29.0 1.7 %collective-permute-done.6 = f32[2,8,128]{2,1,0:T(8,128)S(1)} collective-permute-done((f32[2,8,128]{2,1,0:T(8,128)S(1)}, f32[2,8,128]{2,1,0:T(8,128)S(1)}, u32[]{:S(2)}, u32[]{:S(2)}) %collective-permute-start.6) | collective-permute-done | bytes 8224 | tf_op jit(solution)/shard_map/ppermute | solution.py:537
  30.8 1.2 %collective-permute-start.7 = (f32[9,8,128]{2,1,0:T(8,128)S(1)}, f32[9,8,128]{2,1,0:T(8,128)S(1)}, u32[]{:S(2)}, u32[]{:S(2)}) collective-permute-start(f32[9,8,128]{2,1,0:T(8,128)S(1)} %constant_dynamic-update-slice_fusion), channel_id=1, source_target_pairs={{0,1},{1,0},{2,3},{3,2},{4,5},{5,4},{6,7},{7,6},{8,9},{9,8},{10,11... | collective-permute-start | bytes 110600 | tf_op jit(solution)/shard_map/ppermute | solution.py:537
  32.0 2.6 %project.1.q_ref = f32[512,512]{1,0:T(8,128)S(1)} custom-call(f32[512,1024]{1,0:T(8,128)S(1)} %shard_map.64.first_ref.field0_ref, f32[512,1024]{1,0:T(8,128)S(1)} %shard_map.65.second_ref.field1_ref, bf16[512,2048]{1,0:T(8,128)(2,1)S(1)} %get-tuple-element.25.wide_ref), custom_call_target="tpu_custom_call" | custom-call | flops 2147483648 | bytes 7000000 | tf_op jit(solution)/shard_map/project/pallas_call | solution.py:192
  34.6 2.0 %collective-permute-start.8 = (f32[2,9,8,128]{3,2,1,0:T(8,128)S(1)}, f32[2,9,8,128]{3,2,1,0:T(8,128)S(1)}, u32[]{:S(2)}, u32[]{:S(2)}) collective-permute-start(f32[2,9,8,128]{3,2,1,0:T(8,128)S(1)} %pad_maximum_fusion.1), channel_id=1, source_target_pairs={{0,3},{1,2},{2,1},{3,0},{4,7},{5,6},{6,5},{7,4},{8,11},{9,10},{10,... | collective-permute-start | bytes 221192 | tf_op jit(solution)/shard_map/ppermute | solution.py:537
  36.6 5.4 %solve_early.1 = (f32[128,128]{1,0:T(8,128)S(1)}, f32[64,128]{1,0:T(8,128)S(1)}, f32[128,384]{1,0:T(8,128)S(1)}) custom-call(s32[7,128]{1,0:T(8,128)S(1)} %copy-done.5, f32[7,1,64,64]{3,2,1,0:T(8,128)S(1)} %copy-done.3, f32[128,128]{1,0:T(8,128)S(1)} %get-tuple-element.26.gram0_ref, f32[64,384]{1,0:T(8,128)S(1)} %get-tuple-element.27.own1_ref, ...), custom_call_target="tpu_custom_call" | custom-call | flops 3000000000 | bytes 4000000 | tf_op jit(solution)/shard_map/solve_early/pallas_call | solution.py:307
  42.1 5.9 %collective-permute-start.9 = (f32[4,9,8,128]{3,2,1,0:T(8,128)S(1)}, f32[4,9,8,128]{3,2,1,0:T(8,128)S(1)}, u32[]{:S(2)}, u32[]{:S(2)}) collective-permute-start(f32[4,9,8,128]{3,2,1,0:T(8,128)S(1)} %pad_maximum_fusion.near_ref), channel_id=1, source_target_pairs={{0,4},{4,0},{1,5},{5,1},{2,6},{6,2},{3,7},{7,3},{8,12},{12,8},{9,1... | collective-permute-start | bytes 442376 | tf_op jit(solution)/shard_map/ppermute | solution.py:537
  48.0 1.5 %early.1 = (f32[512,128]{1,0:T(8,128)S(1)}, f32[2,128,128]{2,1,0:T(8,128)S(1)}, f32[512,384]{1,0:T(8,128)S(1)}) custom-call(f32[512,512]{1,0:T(8,128)S(1)} %project.1.q_ref, f32[128,128]{1,0:T(8,128)S(1)} %get-tuple-element.28.from0_ref, f32[128,384]{1,0:T(8,128)S(1)} %get-tuple-element.29.cross0_ref, f32[64,128]{1,0:T(8,128)S(1)} %get-tuple-element.30.weight_ref, ...), custom_call_target="tpu_custom_call" | custom-call | flops 3000000000 | bytes 4000000 | tf_op jit(solution)/shard_map/early/pallas_call | solution.py:335
  49.5 9.3 %late.1 = (f32[5,128,128]{2,1,0:T(8,128)S(1)}, f32[5,128,128]{2,1,0:T(8,128)S(1)}) custom-call(s32[7,128]{1,0:T(8,128)S(1)} %copy-done.5, f32[7,1,64,64]{3,2,1,0:T(8,128)S(1)} %copy-done.3, f32[4,9,8,128]{3,2,1,0:T(8,128)S(1)} %pad_maximum_fusion.near_ref, f32[4,9,8,128]{3,2,1,0:T(8,128)S(1)} %collective-permute-done.9.far_ref, ...), custom_call_target="tpu_custom_call" | custom-call | flops 4000000000 | bytes 4000000 | tf_op jit(solution)/shard_map/late/pallas_call | solution.py:388
  58.8 0.1 collective-permute-start.10
  58.9 1.6 %collective-permute-done.10.recv_ref = f32[5,128,128]{2,1,0:T(8,128)S(1)} collective-permute-done((f32[5,128,128]{2,1,0:T(8,128)S(1)}, f32[5,128,128]{2,1,0:T(8,128)S(1)}, u32[]{:S(2)}, u32[]{:S(2)}) %collective-permute-start.10) | collective-permute-done | bytes 327712 | tf_op jit(solution)/shard_map/ppermute | solution.py:537
  60.6 19.7 %all_to_all.10.got_ref = f32[32,16,128]{2,1,0:T(8,128)S(1)} all-to-all(f32[32,16,128]{2,1,0:T(8,128)S(1)} %deal.1), channel_id=1, replica_groups=mesh['x'=4,'z'=8,'core'=2,'cols'=4] {'x','z'}, dimensions={0} | all-to-all | bytes 524288 | tf_op jit(solution)/shard_map/all_to_all | solution.py:578
  80.3 16.1 %all_to_all.11.near_ref = f32[32,16,128]{2,1,0:T(8,128)S(1)} all-to-all(f32[32,16,128]{2,1,0:T(8,128)S(1)} %collect.1), channel_id=1, replica_groups=mesh['x'=4,'z'=8,'core'=2,'cols'=4] {'x','z'}, dimensions={0} | all-to-all | bytes 524288 | tf_op jit(solution)/shard_map/all_to_all | solution.py:581
  96.4 3.6 %collective-permute-start.13 = (f32[32,16,128]{2,1,0:T(8,128)S(1)}, f32[32,16,128]{2,1,0:T(8,128)S(1)}, u32[]{:S(2)}, u32[]{:S(2)}) collective-permute-start(f32[32,16,128]{2,1,0:T(8,128)S(1)} %all_to_all.11.near_ref), channel_id=1, source_target_pairs={{0,4},{4,0},{1,5},{5,1},{2,6},{6,2},{3,7},{7,3},{8,12},{12,8},{9,1... | collective-permute-start | bytes 786440 | tf_op jit(solution)/shard_map/ppermute | solution.py:537
  100.0 1.5 %collective-permute-start.11 = (f32[128,128]{1,0:T(8,128)S(1)}, f32[128,128]{1,0:T(8,128)S(1)}, u32[]{:S(2)}, u32[]{:S(2)}) collective-permute-start(f32[128,128]{1,0:T(8,128)S(1)} %two.1), channel_id=1, source_target_pairs={{0,8},{8,0},{16,24},{24,16},{32,40},{40,32},{48,56},{56,48},{1,9},... | collective-permute-start | bytes 196616 | tf_op jit(solution)/shard_map/ppermute | solution.py:537
  101.5 0.3 collective-permute-start.1
  101.8 1.9 %collective-permute-done.11.near2_ref = f32[128,128]{1,0:T(8,128)S(1)} collective-permute-done((f32[128,128]{1,0:T(8,128)S(1)}, f32[128,128]{1,0:T(8,128)S(1)}, u32[]{:S(2)}, u32[]{:S(2)}) %collective-permute-start.11) | collective-permute-done | bytes 65568 | tf_op jit(solution)/shard_map/ppermute | solution.py:537
  103.7 0.9 collective-permute-start.12
  104.6 0.9 collective-permute-done.12.far2_ref
  105.5 9.1 %final.1 = f32[512,2048]{1,0:T(8,128)} custom-call(f32[512,1024]{1,0:T(8,128)} %copy-done, f32[512,1024]{1,0:T(8,128)} %copy-done.1, bf16[512,2048]{1,0:T(8,128)(2,1)} %copy-done.2, f32[512,128]{1,0:T(8,128)S(1)} %get-tuple-element.32.u0_ref, f32[2,128,128]{2,1,0:T(8,128)S(1)} %collective-permute-done.1.u1_ref, ...), custom_call_target="tpu_custom_call" | custom-call | flops 2147483648 | bytes 12000000 | tf_op jit(solution)/shard_map/final/pallas_call | solution.py:519
  (39 shorter events, 0.3 us)
Async XLA Ops:
  0.0 6.3 %copy-start.4 = (s32[2048]{0:T(1024)S(1)}, s32[2048]{0:T(1024)}, u32[]{:S(2)}) copy-start(s32[2048]{0:T(1024)} %param.7) | copy-start | bytes 24580
  2.9 29.1 %copy-start.2 = (bf16[512,2048]{1,0:T(8,128)(2,1)}, bf16[512,2048]{1,0:T(8,128)(2,1)S(1)}, u32[]{:S(2)}) copy-start(bf16[512,2048]{1,0:T(8,128)(2,1)S(1)} %get-tuple-element.25.wide_ref) | copy-start | bytes 6291460
  2.9 33.7 %collective-permute-start = (f32[64,384]{1,0:T(8,128)S(1)}, f32[64,384]{1,0:T(8,128)S(1)}, u32[]{:S(2)}, u32[]{:S(2)}) collective-permute-start(f32[64,384]{1,0:T(8,128)S(1)} %get-tuple-element.27.own1_ref), channel_id=1, source_target_pairs={{0,4},{4,0},{1,5},{5,1},{2,6},{6,2},{3,7},{7,3},{8,12},{12,8},{9,1... | collective-permute-start | bytes 294920 | tf_op jit(solution)/shard_map/ppermute | solution.py:537
  6.2 8.8 %collective-permute-start.2 = (f32[12,8,128]{2,1,0:T(8,128)S(1)}, f32[12,8,128]{2,1,0:T(8,128)S(1)}, u32[]{:S(2)}, u32[]{:S(2)}) collective-permute-start(f32[12,8,128]{2,1,0:T(8,128)S(1)} %get-tuple-element.35), channel_id=1, source_target_pairs={{0,4},{4,0},{1,5},{5,1},{2,6},{6,2},{3,7},{7,3},{8,12},{12,8},{9,1... | collective-permute-start | bytes 147464 | tf_op jit(solution)/shard_map/ppermute | solution.py:537
  13.5 18.5 %copy-start = (f32[512,1024]{1,0:T(8,128)}, f32[512,1024]{1,0:T(8,128)S(1)}, u32[]{:S(2)}) copy-start(f32[512,1024]{1,0:T(8,128)S(1)} %shard_map.64.first_ref.field0_ref) | copy-start | bytes 6291460
  14.9 19.7 %copy-start.1 = (f32[512,1024]{1,0:T(8,128)}, f32[512,1024]{1,0:T(8,128)S(1)}, u32[]{:S(2)}) copy-start(f32[512,1024]{1,0:T(8,128)S(1)} %shard_map.65.second_ref.field1_ref) | copy-start | bytes 6291460
  15.0 2.9 %collective-permute-start.3 = (f32[9,8,128]{2,1,0:T(8,128)S(1)}, f32[9,8,128]{2,1,0:T(8,128)S(1)}, u32[]{:S(2)}, u32[]{:S(2)}) collective-permute-start(f32[9,8,128]{2,1,0:T(8,128)S(1)} %slice.77), channel_id=1, source_target_pairs={{0,8},{8,0},{16,24},{24,16},{32,40},{40,32},{48,56},{56,48},{1,9},... | collective-permute-start | bytes 110600 | tf_op jit(solution)/shard_map/ppermute | solution.py:537
  17.9 3.6 %collective-permute-start.4 = (f32[6,8,128]{2,1,0:T(8,128)S(1)}, f32[6,8,128]{2,1,0:T(8,128)S(1)}, u32[]{:S(2)}, u32[]{:S(2)}) collective-permute-start(f32[6,8,128]{2,1,0:T(8,128)S(1)} %slice_add_fusion), channel_id=1, source_target_pairs={{0,16},{8,24},{16,0},{24,8},{32,48},{40,56},{48,32},{56,40},{1,17}... | collective-permute-start | bytes 73736 | tf_op jit(solution)/shard_map/ppermute | solution.py:537
  21.5 6.5 %collective-permute-start.5 = (f32[4,8,128]{2,1,0:T(8,128)S(1)}, f32[4,8,128]{2,1,0:T(8,128)S(1)}, u32[]{:S(2)}, u32[]{:S(2)}) collective-permute-start(f32[4,8,128]{2,1,0:T(8,128)S(1)} %slice_add_fusion.1), channel_id=1, source_target_pairs={{0,32},{8,40},{16,48},{24,56},{32,0},{40,8},{48,16},{56,24},{1,33}... | collective-permute-start | bytes 49160 | tf_op jit(solution)/shard_map/ppermute | solution.py:537
  28.0 2.8 %collective-permute-start.6 = (f32[2,8,128]{2,1,0:T(8,128)S(1)}, f32[2,8,128]{2,1,0:T(8,128)S(1)}, u32[]{:S(2)}, u32[]{:S(2)}) collective-permute-start(f32[2,8,128]{2,1,0:T(8,128)S(1)} %slice_add_fusion.2), channel_id=1, source_target_pairs={{0,64},{64,0},{128,192},{192,128},{1,65},{65,1},{129,193},{193,129... | collective-permute-start | bytes 24584 | tf_op jit(solution)/shard_map/ppermute | solution.py:537
  30.8 3.8 %collective-permute-start.7 = (f32[9,8,128]{2,1,0:T(8,128)S(1)}, f32[9,8,128]{2,1,0:T(8,128)S(1)}, u32[]{:S(2)}, u32[]{:S(2)}) collective-permute-start(f32[9,8,128]{2,1,0:T(8,128)S(1)} %constant_dynamic-update-slice_fusion), channel_id=1, source_target_pairs={{0,1},{1,0},{2,3},{3,2},{4,5},{5,4},{6,7},{7,6},{8,9},{9,8},{10,11... | collective-permute-start | bytes 110600 | tf_op jit(solution)/shard_map/ppermute | solution.py:537
  32.0 4.6 %copy-start.3 = (f32[7,1,64,64]{3,2,1,0:T(8,128)S(1)}, f32[7,1,64,64]{3,2,1,0:T(8,128)}, u32[]{:S(2)}) copy-start(f32[7,1,64,64]{3,2,1,0:T(8,128)} %link_ref.3) | copy-start | bytes 344068
  32.0 4.6 %copy-start.5 = (s32[7,128]{1,0:T(8,128)S(1)}, s32[7,128]{1,0:T(8,128)}, u32[]{:S(2)}) copy-start(s32[7,128]{1,0:T(8,128)} %ranks_ref.3) | copy-start | bytes 10756
  34.6 7.4 %collective-permute-start.8 = (f32[2,9,8,128]{3,2,1,0:T(8,128)S(1)}, f32[2,9,8,128]{3,2,1,0:T(8,128)S(1)}, u32[]{:S(2)}, u32[]{:S(2)}) collective-permute-start(f32[2,9,8,128]{3,2,1,0:T(8,128)S(1)} %pad_maximum_fusion.1), channel_id=1, source_target_pairs={{0,3},{1,2},{2,1},{3,0},{4,7},{5,6},{6,5},{7,4},{8,11},{9,10},{10,... | collective-permute-start | bytes 221192 | tf_op jit(solution)/shard_map/ppermute | solution.py:537
  42.1 7.4 %collective-permute-start.9 = (f32[4,9,8,128]{3,2,1,0:T(8,128)S(1)}, f32[4,9,8,128]{3,2,1,0:T(8,128)S(1)}, u32[]{:S(2)}, u32[]{:S(2)}) collective-permute-start(f32[4,9,8,128]{3,2,1,0:T(8,128)S(1)} %pad_maximum_fusion.near_ref), channel_id=1, source_target_pairs={{0,4},{4,0},{1,5},{5,1},{2,6},{6,2},{3,7},{7,3},{8,12},{12,8},{9,1... | collective-permute-start | bytes 442376 | tf_op jit(solution)/shard_map/ppermute | solution.py:537
  58.8 1.7 %collective-permute-start.10 = (f32[5,128,128]{2,1,0:T(8,128)S(1)}, f32[5,128,128]{2,1,0:T(8,128)S(1)}, u32[]{:S(2)}, u32[]{:S(2)}) collective-permute-start(f32[5,128,128]{2,1,0:T(8,128)S(1)} %get-tuple-element.38), channel_id=1, source_target_pairs={{0,4},{4,0},{1,5},{5,1},{2,6},{6,2},{3,7},{7,3},{8,12},{12,8},{9,1... | collective-permute-start | bytes 983048 | tf_op jit(solution)/shard_map/ppermute | solution.py:537
  96.4 9.1 %collective-permute-start.13 = (f32[32,16,128]{2,1,0:T(8,128)S(1)}, f32[32,16,128]{2,1,0:T(8,128)S(1)}, u32[]{:S(2)}, u32[]{:S(2)}) collective-permute-start(f32[32,16,128]{2,1,0:T(8,128)S(1)} %all_to_all.11.near_ref), channel_id=1, source_target_pairs={{0,4},{4,0},{1,5},{5,1},{2,6},{6,2},{3,7},{7,3},{8,12},{12,8},{9,1... | collective-permute-start | bytes 786440 | tf_op jit(solution)/shard_map/ppermute | solution.py:537
  100.0 3.7 %collective-permute-start.11 = (f32[128,128]{1,0:T(8,128)S(1)}, f32[128,128]{1,0:T(8,128)S(1)}, u32[]{:S(2)}, u32[]{:S(2)}) collective-permute-start(f32[128,128]{1,0:T(8,128)S(1)} %two.1), channel_id=1, source_target_pairs={{0,8},{8,0},{16,24},{24,16},{32,40},{40,32},{48,56},{56,48},{1,9},... | collective-permute-start | bytes 196616 | tf_op jit(solution)/shard_map/ppermute | solution.py:537
  101.5 3.1 %collective-permute-start.1 = (f32[2,128,128]{2,1,0:T(8,128)S(1)}, f32[2,128,128]{2,1,0:T(8,128)S(1)}, u32[]{:S(2)}, u32[]{:S(2)}) collective-permute-start(f32[2,128,128]{2,1,0:T(8,128)S(1)} %get-tuple-element.33), channel_id=1, source_target_pairs={{0,4},{4,0},{1,5},{5,1},{2,6},{6,2},{3,7},{7,3},{8,12},{12,8},{9,1... | collective-permute-start | bytes 393224 | tf_op jit(solution)/shard_map/ppermute | solution.py:537
  103.7 1.8 %collective-permute-start.12 = (f32[128,128]{1,0:T(8,128)S(1)}, f32[128,128]{1,0:T(8,128)S(1)}, u32[]{:S(2)}, u32[]{:S(2)}) collective-permute-start(f32[128,128]{1,0:T(8,128)S(1)} %collective-permute-done.11.near2_ref), channel_id=1, source_target_pairs={{0,4},{4,0},{1,5},{5,1},{2,6},{6,2},{3,7},{7,3},{8,12},{12,8},{9,1... | collective-permute-start | bytes 196616 | tf_op jit(solution)/shard_map/ppermute | solution.py:537

commit v2 on v1

--- a/solution.py
+++ b/solution.py
@@ -210,9 +210,12 @@
     return lax.broadcasted_iota(jnp.int32, (rows, 128), 1)
 
 
-def system(link_dup, gram_tile, upper_half, rank_own, scale):
+def jointly(link_dup, rank_own, scale):
+    return jnp.where(jnp.bitwise_and(lanes(), R - 1) < rank_own, link_dup * scale, 0.0)
+
+
+def system(joint, gram_tile, upper_half):
     lane = lanes()
-    joint = jnp.where(jnp.bitwise_and(lane, R - 1) < rank_own, link_dup * scale, 0.0)
     placed = jnp.where((lane >= R) == upper_half, joint, 0.0)
     inner = dot_high(gram_tile, twice(placed, 0), NT)
     outer = dot_high(joint[:, :R], inner, NN)
@@ -292,9 +295,10 @@
     rank_f, rank_s = ranks_ref[0, 2 * leaf], ranks_ref[0, 2 * leaf + 1]
     rank_1, rank_1s = ranks_ref[1, 2 * leaf], ranks_ref[1, 2 * jnp.bitwise_xor(leaf, 1)]
     scale0, scale1 = scale_of(0), scale_of(1)
-    work_ref[0] = system(flipped0, gram0_ref[0:R], False, rank_f, scale0)
-    work_ref[1] = system(plain0, gram0_ref[R:], True, rank_s, scale0)
-    work_ref[2] = system(jnp.where(second == 1, plain1, flipped1), own1_ref[:, :128], False, rank_1, scale1)
+    work_ref[0] = system(jointly(flipped0, rank_f, scale0), gram0_ref[0:R], False)
+    work_ref[1] = system(jointly(plain0, rank_s, scale0), gram0_ref[R:], True)
+    joint1 = jointly(jnp.where(second == 1, plain1, flipped1), rank_1, scale1)
+    work_ref[2] = system(joint1, own1_ref[:, :128], False)
     eliminate(work_ref, 3)
     from0_ref[R:] = solved(work_ref, 0, rank_s, scale0)
     from0_ref[0:R] = pltpu.roll(solved(work_ref, 1, rank_f, scale0), R, 1)
@@ -316,7 +320,15 @@
     )(ranks, coupling, gram0, own1, sib1)
 
 
-def early_kernel(q_ref, from0_ref, cross0_ref, weight_ref, onward_ref, u0_ref, u1_ref, x_ref):
+def early_kernel(ranks_ref, link_ref, q_ref, from0_ref, cross0_ref, weight_ref, onward_ref,
+                 u0_ref, u1_ref, x_ref, joint_ref):
+    leaf = leaf_index()
+    for level in range(2, 7):
+        child = jnp.right_shift(leaf, level - 1)
+        plain, flipped = coupling_forms(link_ref[level, 0])
+        rank = ranks_ref[level, jnp.left_shift(child, level)]
+        which = jnp.where(jnp.bitwise_and(child, 1) == 1, plain, flipped)
+        joint_ref[level - 2] = jointly(which, rank, scale_of(level))
     u0 = apply_nt(pair(q_ref[:, UP:]), from0_ref[...])
     u0_ref[...] = u0
     zero = pair(u0)
@@ -331,37 +343,33 @@
         x_ref[:, at] = q_ref[:, at] - apply_nn(zero, cross0[:, at]) - apply_nn(head, onward[:, at])
 
 
-def early(q, from0, cross0, weight, onward):
+def early(ranks, coupling, q, from0, cross0, weight, onward):
     return pl.pallas_call(
         early_kernel,
-        out_shape=(shape(COLS, 128), shape(2, 128, 128), shape(COLS, UP)),
-        in_specs=[VMEM] * 5,
-        out_specs=(VMEM,) * 3,
+        out_shape=(shape(COLS, 128), shape(2, 128, 128), shape(COLS, UP), shape(5, R, 128)),
+        in_specs=[SMEM] + [VMEM] * 6,
+        out_specs=(VMEM,) * 4,
         compiler_params=params(12),
         cost_estimate=cost(3e9, 4e6),
         name="early",
-    )(q, from0, cross0, weight, onward)
+    )(ranks, coupling, q, from0, cross0, weight, onward)
 
 
 OWN_TILE = {2: 0, 3: 3, 4: 5, 5: 7, 6: 8}
 ONWARD = {2: ((1, 1), (2, 2)), 3: ((3, 1), (4, 2)), 4: ((6, 2),), 5: ((7, 2),), 6: ()}
 
 
-def late_kernel(ranks_ref, link_ref, near_ref, far_ref, x_ref, keep_ref, send_ref, pk_ref, work_ref):
+def late_kernel(ranks_ref, joint_ref, near_ref, far_ref, x_ref, keep_ref, send_ref, pk_ref, work_ref):
     leaf, col, core = leaf_index(), lax.axis_index("cols"), lax.axis_index("core")
     for other, source in ((0, near_ref), (1, far_ref)):
-        for slot, offset in enumerate((0, 1, 3, 2)):
+        for slot, offset in enumerate((0, 1, 2, 3)):
             part = jnp.bitwise_xor(core, other) * 4 + jnp.bitwise_xor(col, offset)
             rows = pl.ds(pl.multiple_of(part * 8, 8), 8)
             for tile in range(9):
                 pk_ref[tile, rows, :] = source[slot, tile]
     systems = []
     for level in range(2, 7):
-        child = jnp.right_shift(leaf, level - 1)
-        plain, flipped = coupling_forms(link_ref[level, 0])
-        rank = ranks_ref[level, jnp.left_shift(child, level)]
-        which = jnp.where(jnp.bitwise_and(child, 1) == 1, plain, flipped)
-        systems.append(system(which, pk_ref[OWN_TILE[level]], level % 2 == 0, rank, scale_of(level)))
+        systems.append(system(joint_ref[level - 2], pk_ref[OWN_TILE[level]], level % 2 == 0))
     for item in range(5):
         work_ref[item] = systems[item]
     eliminate(work_ref, 5)
@@ -384,7 +392,7 @@
         send_ref[level - 2] = jnp.where(core == 0, both[128:], both[:128])
 
 
-def late(ranks, coupling, near, far, x):
+def late(ranks, joint, near, far, x):
     return pl.pallas_call(
         late_kernel,
         out_shape=(shape(5, 128, 128), shape(5, 128, 128)),
@@ -394,7 +402,7 @@
         compiler_params=params(16),
         cost_estimate=cost(4e9, 4e6),
         name="late",
-    )(ranks, coupling, near, far, x)
+    )(ranks, joint, near, far, x)
 
 
 def turned(value):
@@ -467,12 +475,26 @@
 
 
 def final_kernel(field0_ref, field1_ref, wide_ref, u0_ref, u1_ref, near2_ref, far2_ref, near_ref, far_ref,
-                 out_ref, left_ref, all_ref):
+                 out_ref, left_ref, all_ref, wide_vmem, field_vmem, sems):
     step = pl.program_id(0)
     half = step // (LEAF // BLK)
+    loads = [
+        pltpu.make_async_copy(
+            wide_ref.at[:, j * BLK:j * BLK + BLK], wide_vmem.at[:, j * BLK:j * BLK + BLK], sems.at[j]
+        )
+        for j in range(8)
+    ]
+    loads += [
+        pltpu.make_async_copy(
+            field1_ref.at[:, j * BLK:j * BLK + BLK], field_vmem.at[:, j * BLK:j * BLK + BLK], sems.at[8 + j]
+        )
+        for j in range(4)
+    ]
 
     @pl.when(step == 0)
     def _():
+        for load in loads:
+            load.start()
         core = lax.axis_index("core")
         top = lax.broadcasted_iota(jnp.int32, (8, 128), 0) < 4
         lane = lanes(8)
@@ -502,35 +524,42 @@
         left_ref[:, UP:512] = high
         left_ref[:, 512 + UP:] = low
 
-    right = wide_ref[...]
+    for j in range(8):
+        @pl.when(step == j)
+        def _():
+            loads[j].wait()
+            if j >= 4:
+                loads[j + 4].wait()
+
+    right = wide_vmem[:, pl.ds(pl.multiple_of(step * BLK, BLK), BLK)]
     update = dot(left_ref[:, :512], right, NN) + dot(left_ref[:, 512:], right, NN)
 
     @pl.when(half == 0)
     def _():
-        out_ref[...] = field0_ref[...] - update
+        out_ref[...] = field0_ref[:, pl.ds(pl.multiple_of(step * BLK, BLK), BLK)] - update
 
     @pl.when(half == 1)
     def _():
-        out_ref[...] = field1_ref[...] - update
+        out_ref[...] = field_vmem[:, pl.ds(pl.multiple_of((step - 4) * BLK, BLK), BLK)] - update
 
 
 def final(field0, field1, wide, *updates):
-    steps = LEAF // BLK
     return pl.pallas_call(
         final_kernel,
         grid=(ROWS // BLK,),
         out_shape=shape(COLS, ROWS),
         in_specs=[
-            pl.BlockSpec((COLS, BLK), lambda j: (0, jnp.minimum(j, steps - 1))),
-            pl.BlockSpec((COLS, BLK), lambda j: (0, jnp.maximum(j - steps, 0))),
-            pl.BlockSpec((512, BLK), lambda j: (0, j)),
+            VMEM, HBM, HBM,
         ] + [VMEM] * 6,
         out_specs=pl.BlockSpec((COLS, BLK), lambda j: (0, j)),
-        scratch_shapes=[pltpu.VMEM((COLS, 1024), BF16), pltpu.VMEM((COLS, UP), F32)],
-        compiler_params=params(16),
+        scratch_shapes=[
+            pltpu.VMEM((COLS, 1024), BF16), pltpu.VMEM((COLS, UP), F32), pltpu.VMEM((512, ROWS), BF16),
+            pltpu.VMEM((COLS, LEAF), F32), pltpu.SemaphoreType.DMA((12,)),
+        ],
+        compiler_params=params(20),
         cost_estimate=cost(2 * COLS * 1024 * ROWS, 12e6),
         name="final",
-    )(stay(field0), stay(field1), stay(wide), *updates)
+    )(field0, stay(field1), stay(wide), *updates)
 
 
 def swap(array, mask, axis):
@@ -548,7 +577,7 @@
     field1 = leaf_product(permuted1, factor, 1)
     q = project(field0, field1, wide)
     from0, weight1, onward1 = solve_early(ranks, coupling, gram0, own1, sib1)
-    u0, u1, x = early(q, from0, cross0, weight1, onward1)
+    u0, u1, x, joint = early(ranks, coupling, q, from0, cross0, weight1, onward1)
 
     chip = (mine + got)[3:]
     got = swap(chip, 1, "z")
@@ -558,7 +587,7 @@
     got = swap(total, 2, "z")
     pack += [jnp.where(low_lane, total[0], got[0]), got[1]]
     total = total[2:] + got[2:]
-    got = swap(total, 4, "z")
+    got = swap(total, 7, "z")
     pack += [total[0], got[1]]
     total = total[2:] + got[2:]
     got = swap(total, 1, "x")
@@ -566,11 +595,11 @@
     pack = jnp.stack(pack)
     got = swap(pack, 1, "cols")
     pack = jnp.stack([pack, got])
-    got = swap(pack, 3, "cols")
+    got = swap(pack, 2, "cols")
     near = jnp.concatenate([pack, got], axis=0)
     far = swap(near, 1, "core")
     u1 = swap(u1, 1, "core")
-    keep, send = late(ranks, coupling, near, far, x)
+    keep, send = late(ranks, joint, near, far, x)
     got = swap(send, 1, "core")
     two = level_two(keep, got)
     two = swap(two, 1, "z")

time: 115 us -> 112 us (0.974)
  Pallas kernels: 39.6 us -> 37.9 us
    pallas_call x1, Pallas kernels: 9.14 us -> 7.03 us  [final(): pl.pallas_call(final_kernel, grid=(ROWS // BLK,), out_shape=shape(COLS, R...]
  transfers between devices with their start and end apart: 14 -> 14, of which waited for: 7 -> 7; matrix products, arithmetic and copies ran while one was open for 0% -> 0% of each run, Pallas kernels for 16% -> 17%
where the time goes in v2:
time: 112 us
  Pallas kernels  37.9 us (34%)
  blocking collectives  35.6 us (32%)
  starting transfers between devices  25.9 us (23%)
  waiting for transfers between devices  12.1 us (11%)
    ppermute x14, starting transfers between devices, swap(): lax.ppermute(array, axis, [(i, i ^ mask) for i in range(lax.axis_size(axi...  25.9 us
    all_to_all x1, blocking collectives, local(): got = lax.all_to_all(dealt, ('x', 'z'), 0, 0, tiled=True)  19.6 us
    all_to_all x1, blocking collectives, local(): back = lax.all_to_all(total, ('x', 'z'), 0, 0, tiled=True)  16.1 us
    ppermute x14, waiting for transfers between devices, swap(): lax.ppermute(array, axis, [(i, i ^ mask) for i in range(lax.axis_size(axi...  12.1 us
    pallas_call x1, Pallas kernels, late(): pl.pallas_call(late_kernel, out_shape=(shape(5, 128, 128), shape(5, 128,...  9.2 us
    pallas_call x1, Pallas kernels, final(): pl.pallas_call(final_kernel, grid=(ROWS // BLK,), out_shape=shape(COLS, R...  7.03 us
    pallas_call x1, Pallas kernels, solve_early(): pl.pallas_call(solve_early_kernel, out_shape=(shape(128, 128), shape(R, 1...  5.43 us
    pallas_call x1, Pallas kernels, permute_first(): pl.pallas_call(permute_first_kernel, out_shape=(shape(COLS, LEAF, dtype=B...  2.9 us
  transfers between devices with their start and end apart: 14, of which 7 were waited for; matrix products, arithmetic and copies ran while one was open for 0% of the time, Pallas kernels for 17%

profile of v2, /device:TPU:1, one launch (start us, length us, event | category | flops | bytes accessed | tf_op | source)
XLA Modules:
  0.0 111.9 jit_solution(4508188907618030958)
XLA Ops:
  0.0 2.9 %gram.1 = (bf16[512,2048]{1,0:T(8,128)(2,1)S(1)}, f32[12,8,128]{2,1,0:T(8,128)S(1)}, f32[12,8,128]{2,1,0:T(8,128)S(1)}, f32[64,384]{1,0:T(8,128)S(1)}, f32[128,1...) custom-call(bf16[7,64,2048]{2,1,0:T(8,128)(2,1)} %bases_ref.1, bf16[512,2048]{1,0:T(8,128)(2,1)} %samples_ref.1), custom_call_target="tpu_custom_call" | custom-call | flops 2000000000 | bytes 4000000 | tf_op jit(solution)/shard_map/gram/pallas_call | solution.py:92
  2.9 3.3 %collective-permute-start = (f32[64,384]{1,0:T(8,128)S(1)}, f32[64,384]{1,0:T(8,128)S(1)}, u32[]{:S(2)}, u32[]{:S(2)}) collective-permute-start(f32[64,384]{1,0:T(8,128)S(1)} %get-tuple-element.28.own1_ref), channel_id=1, source_target_pairs={{0,4},{4,0},{1,5},{5,1},{2,6},{6,2},{3,7},{7,3},{8,12},{12,8},{9,1... | collective-permute-start | bytes 294920 | tf_op jit(solution)/shard_map/ppermute | solution.py:566
  6.2 0.1 collective-permute-start.2
  6.3 2.9 %permute_second.1.permuted_ref = bf16[512,1024]{1,0:T(8,128)(2,1)S(1)} custom-call(bf16[512,2048]{1,0:T(8,128)(2,1)S(1)} %get-tuple-element.23.samples_ref, s32[1,2048]{1,0:T(1,128)S(1)} %bitcast.3), custom_call_target="tpu_custom_call" | custom-call | flops 2147483648 | bytes 4000000 | tf_op jit(solution)/shard_map/permute_second/pallas_call | solution.py:146
  9.2 2.9 %permute_first.1 = (bf16[512,1024]{1,0:T(8,128)(2,1)S(1)}, bf16[2,1024,1024]{2,1,0:T(8,128)(2,1)S(1)}) custom-call(bf16[512,2048]{1,0:T(8,128)(2,1)S(1)} %get-tuple-element.23.samples_ref, s32[1,2048]{1,0:T(1,128)S(1)} %bitcast.4, bf16[2,1024,1024]{2,1,0:T(8,128)(2,1)} %factor_ref.1), custom_call_target="tpu_custom_call" | custom-call | flops 2147483648 | bytes 4000000 | tf_op jit(solution)/shard_map/permute_first/pallas_call | solution.py:133
  12.1 1.4 %shard_map.64.first_ref.field0_ref = f32[512,1024]{1,0:T(8,128)S(1)} custom-call(bf16[512,1024]{1,0:T(8,128)(2,1)S(1)} %get-tuple-element.24.permuted_ref, bf16[2,1024,1024]{2,1,0:T(8,128)(2,1)S(1)} %get-tuple-element.25.factor_ref), custom_call_target="tpu_custom_call" | custom-call | flops 1073741824 | bytes 5000000 | tf_op jit(solution)/shard_map/pallas_call | solution.py:167
  13.5 1.4 %shard_map.65.second_ref.field1_ref = f32[512,1024]{1,0:T(8,128)S(1)} custom-call(bf16[512,1024]{1,0:T(8,128)(2,1)S(1)} %permute_second.1.permuted_ref, bf16[2,1024,1024]{2,1,0:T(8,128)(2,1)S(1)} %get-tuple-element.25.factor_ref), custom_call_target="tpu_custom_call" | custom-call | flops 1073741824 | bytes 5000000 | tf_op jit(solution)/shard_map/pallas_call | solution.py:167
  15.1 2.8 %collective-permute-done.3 = f32[9,8,128]{2,1,0:T(8,128)S(1)} collective-permute-done((f32[9,8,128]{2,1,0:T(8,128)S(1)}, f32[9,8,128]{2,1,0:T(8,128)S(1)}, u32[]{:S(2)}, u32[]{:S(2)}) %collective-permute-start.3) | collective-permute-done | bytes 36896 | tf_op jit(solution)/shard_map/ppermute | solution.py:566
  17.9 1.5 %collective-permute-start.4 = (f32[6,8,128]{2,1,0:T(8,128)S(1)}, f32[6,8,128]{2,1,0:T(8,128)S(1)}, u32[]{:S(2)}, u32[]{:S(2)}) collective-permute-start(f32[6,8,128]{2,1,0:T(8,128)S(1)} %slice_add_fusion), channel_id=1, source_target_pairs={{0,16},{8,24},{16,0},{24,8},{32,48},{40,56},{48,32},{56,40},{1,17}... | collective-permute-start | bytes 73736 | tf_op jit(solution)/shard_map/ppermute | solution.py:566
  19.3 2.1 %collective-permute-done.4 = f32[6,8,128]{2,1,0:T(8,128)S(1)} collective-permute-done((f32[6,8,128]{2,1,0:T(8,128)S(1)}, f32[6,8,128]{2,1,0:T(8,128)S(1)}, u32[]{:S(2)}, u32[]{:S(2)}) %collective-permute-start.4) | collective-permute-done | bytes 24608 | tf_op jit(solution)/shard_map/ppermute | solution.py:566
  21.5 3.9 %collective-permute-start.5 = (f32[4,8,128]{2,1,0:T(8,128)S(1)}, f32[4,8,128]{2,1,0:T(8,128)S(1)}, u32[]{:S(2)}, u32[]{:S(2)}) collective-permute-start(f32[4,8,128]{2,1,0:T(8,128)S(1)} %slice_add_fusion.1), channel_id=1, source_target_pairs={{0,56},{8,48},{16,40},{24,32},{32,24},{40,16},{48,8},{56,0},{1,57}... | collective-permute-start | bytes 49160 | tf_op jit(solution)/shard_map/ppermute | solution.py:566
  25.3 1.1 collective-permute-done.5
  26.5 1.2 %collective-permute-start.6 = (f32[2,8,128]{2,1,0:T(8,128)S(1)}, f32[2,8,128]{2,1,0:T(8,128)S(1)}, u32[]{:S(2)}, u32[]{:S(2)}) collective-permute-start(f32[2,8,128]{2,1,0:T(8,128)S(1)} %slice_add_fusion.2), channel_id=1, source_target_pairs={{0,64},{64,0},{128,192},{192,128},{1,65},{65,1},{129,193},{193,129... | collective-permute-start | bytes 24584 | tf_op jit(solution)/shard_map/ppermute | solution.py:566
  27.7 1.6 %collective-permute-done.6 = f32[2,8,128]{2,1,0:T(8,128)S(1)} collective-permute-done((f32[2,8,128]{2,1,0:T(8,128)S(1)}, f32[2,8,128]{2,1,0:T(8,128)S(1)}, u32[]{:S(2)}, u32[]{:S(2)}) %collective-permute-start.6) | collective-permute-done | bytes 8224 | tf_op jit(solution)/shard_map/ppermute | solution.py:566
  29.3 1.4 %collective-permute-start.7 = (f32[9,8,128]{2,1,0:T(8,128)S(1)}, f32[9,8,128]{2,1,0:T(8,128)S(1)}, u32[]{:S(2)}, u32[]{:S(2)}) collective-permute-start(f32[9,8,128]{2,1,0:T(8,128)S(1)} %constant_dynamic-update-slice_fusion), channel_id=1, source_target_pairs={{0,1},{1,0},{2,3},{3,2},{4,5},{5,4},{6,7},{7,6},{8,9},{9,8},{10,11... | collective-permute-start | bytes 110600 | tf_op jit(solution)/shard_map/ppermute | solution.py:566
  30.7 2.6 %project.1.q_ref = f32[512,512]{1,0:T(8,128)S(1)} custom-call(f32[512,1024]{1,0:T(8,128)S(1)} %shard_map.64.first_ref.field0_ref, f32[512,1024]{1,0:T(8,128)S(1)} %shard_map.65.second_ref.field1_ref, bf16[512,2048]{1,0:T(8,128)(2,1)S(1)} %get-tuple-element.26.wide_ref), custom_call_target="tpu_custom_call" | custom-call | flops 2147483648 | bytes 7000000 | tf_op jit(solution)/shard_map/project/pallas_call | solution.py:192
  33.3 2.7 %collective-permute-start.8 = (f32[2,9,8,128]{3,2,1,0:T(8,128)S(1)}, f32[2,9,8,128]{3,2,1,0:T(8,128)S(1)}, u32[]{:S(2)}, u32[]{:S(2)}) collective-permute-start(f32[2,9,8,128]{3,2,1,0:T(8,128)S(1)} %pad_maximum_fusion.1), channel_id=1, source_target_pairs={{0,2},{1,3},{2,0},{3,1},{4,6},{5,7},{6,4},{7,5},{8,10},{9,11},{10,... | collective-permute-start | bytes 221192 | tf_op jit(solution)/shard_map/ppermute | solution.py:566
  36.0 5.4 %solve_early.1 = (f32[128,128]{1,0:T(8,128)S(1)}, f32[64,128]{1,0:T(8,128)S(1)}, f32[128,384]{1,0:T(8,128)S(1)}) custom-call(s32[7,128]{1,0:T(8,128)S(1)} %copy-done.4, f32[7,1,64,64]{3,2,1,0:T(8,128)S(1)} %copy-done.2, f32[128,128]{1,0:T(8,128)S(1)} %get-tuple-element.27.gram0_ref, f32[64,384]{1,0:T(8,128)S(1)} %get-tuple-element.28.own1_ref, ...), custom_call_target="tpu_custom_call" | custom-call | flops 3000000000 | bytes 4000000 | tf_op jit(solution)/shard_map/solve_early/pallas_call | solution.py:311
  41.5 5.4 %collective-permute-start.9 = (f32[4,9,8,128]{3,2,1,0:T(8,128)S(1)}, f32[4,9,8,128]{3,2,1,0:T(8,128)S(1)}, u32[]{:S(2)}, u32[]{:S(2)}) collective-permute-start(f32[4,9,8,128]{3,2,1,0:T(8,128)S(1)} %pad_maximum_fusion.near_ref), channel_id=1, source_target_pairs={{0,4},{4,0},{1,5},{5,1},{2,6},{6,2},{3,7},{7,3},{8,12},{12,8},{9,1... | collective-permute-start | bytes 442376 | tf_op jit(solution)/shard_map/ppermute | solution.py:566
  46.8 2.1 %early.1 = (f32[512,128]{1,0:T(8,128)S(1)}, f32[2,128,128]{2,1,0:T(8,128)S(1)}, f32[512,384]{1,0:T(8,128)S(1)}, f32[5,64,128]{2,1,0:T(8,128)S(1)}) custom-call(s32[7,128]{1,0:T(8,128)S(1)} %copy-done.4, f32[7,1,64,64]{3,2,1,0:T(8,128)S(1)} %copy-done.2, f32[512,512]{1,0:T(8,128)S(1)} %project.1.q_ref, f32[128,128]{1,0:T(8,128)S(1)} %get-tuple-element.29.from0_ref, ...), custom_call_target="tpu_custom_call" | custom-call | flops 3000000000 | bytes 4000000 | tf_op jit(solution)/shard_map/early/pallas_call | solution.py:347
  49.0 9.2 %late.1 = (f32[5,128,128]{2,1,0:T(8,128)S(1)}, f32[5,128,128]{2,1,0:T(8,128)S(1)}) custom-call(s32[7,128]{1,0:T(8,128)S(1)} %copy-done.4, f32[5,64,128]{2,1,0:T(8,128)S(1)} %get-tuple-element.35.joint_ref, f32[4,9,8,128]{3,2,1,0:T(8,128)S(1)} %pad_maximum_fusion.near_ref, f32[4,9,8,128]{3,2,1,0:T(8,128)S(1)} %collective-permute-done.9.far_ref, ...), custom_call_target="tpu_custom_call" | custom-call | flops 4000000000 | bytes 4000000 | tf_op jit(solution)/shard_map/late/pallas_call | solution.py:396
  58.2 0.1 collective-permute-start.10
  58.3 1.6 %collective-permute-done.10.recv_ref = f32[5,128,128]{2,1,0:T(8,128)S(1)} collective-permute-done((f32[5,128,128]{2,1,0:T(8,128)S(1)}, f32[5,128,128]{2,1,0:T(8,128)S(1)}, u32[]{:S(2)}, u32[]{:S(2)}) %collective-permute-start.10) | collective-permute-done | bytes 327712 | tf_op jit(solution)/shard_map/ppermute | solution.py:566
  59.9 19.6 %all_to_all.10.got_ref = f32[32,16,128]{2,1,0:T(8,128)S(1)} all-to-all(f32[32,16,128]{2,1,0:T(8,128)S(1)} %deal.1), channel_id=1, replica_groups=mesh['x'=4,'z'=8,'core'=2,'cols'=4] {'x','z'}, dimensions={0} | all-to-all | bytes 524288 | tf_op jit(solution)/shard_map/all_to_all | solution.py:607
  79.5 16.1 %all_to_all.11.near_ref = f32[32,16,128]{2,1,0:T(8,128)S(1)} all-to-all(f32[32,16,128]{2,1,0:T(8,128)S(1)} %collect.1), channel_id=1, replica_groups=mesh['x'=4,'z'=8,'core'=2,'cols'=4] {'x','z'}, dimensions={0} | all-to-all | bytes 524288 | tf_op jit(solution)/shard_map/all_to_all | solution.py:610
  95.6 3.6 %collective-permute-start.13 = (f32[32,16,128]{2,1,0:T(8,128)S(1)}, f32[32,16,128]{2,1,0:T(8,128)S(1)}, u32[]{:S(2)}, u32[]{:S(2)}) collective-permute-start(f32[32,16,128]{2,1,0:T(8,128)S(1)} %all_to_all.11.near_ref), channel_id=1, source_target_pairs={{0,4},{4,0},{1,5},{5,1},{2,6},{6,2},{3,7},{7,3},{8,12},{12,8},{9,1... | collective-permute-start | bytes 786440 | tf_op jit(solution)/shard_map/ppermute | solution.py:566
  99.2 1.5 %collective-permute-start.11 = (f32[128,128]{1,0:T(8,128)S(1)}, f32[128,128]{1,0:T(8,128)S(1)}, u32[]{:S(2)}, u32[]{:S(2)}) collective-permute-start(f32[128,128]{1,0:T(8,128)S(1)} %two.1), channel_id=1, source_target_pairs={{0,8},{8,0},{16,24},{24,16},{32,40},{40,32},{48,56},{56,48},{1,9},... | collective-permute-start | bytes 196616 | tf_op jit(solution)/shard_map/ppermute | solution.py:566
  100.7 0.3 collective-permute-start.1
  101.0 1.9 %collective-permute-done.11.near2_ref = f32[128,128]{1,0:T(8,128)S(1)} collective-permute-done((f32[128,128]{1,0:T(8,128)S(1)}, f32[128,128]{1,0:T(8,128)S(1)}, u32[]{:S(2)}, u32[]{:S(2)}) %collective-permute-start.11) | collective-permute-done | bytes 65568 | tf_op jit(solution)/shard_map/ppermute | solution.py:566
  103.0 0.9 collective-permute-start.12
  103.8 0.9 collective-permute-done.12.far2_ref
  104.7 7.0 %final.1 = f32[512,2048]{1,0:T(8,128)} custom-call(f32[512,1024]{1,0:T(8,128)S(1)} %shard_map.64.first_ref.field0_ref, f32[512,1024]{1,0:T(8,128)} %copy-done, bf16[512,2048]{1,0:T(8,128)(2,1)} %copy-done.1, f32[512,128]{1,0:T(8,128)S(1)} %get-tuple-element.33.u0_ref, f32[2,128,128]{2,1,0:T(8,128)S(1)} %collective-permute-done.1.u1_ref, ...), custom_call_target="tpu_custom_call" | custom-call | flops 2147483648 | bytes 12000000 | tf_op jit(solution)/shard_map/final/pallas_call | solution.py:547
  (37 shorter events, 0.3 us)
Async XLA Ops:
  0.0 6.3 %copy-start.3 = (s32[2048]{0:T(1024)S(1)}, s32[2048]{0:T(1024)}, u32[]{:S(2)}) copy-start(s32[2048]{0:T(1024)} %param.7) | copy-start | bytes 24580
  2.9 27.8 %copy-start.1 = (bf16[512,2048]{1,0:T(8,128)(2,1)}, bf16[512,2048]{1,0:T(8,128)(2,1)S(1)}, u32[]{:S(2)}) copy-start(bf16[512,2048]{1,0:T(8,128)(2,1)S(1)} %get-tuple-element.26.wide_ref) | copy-start | bytes 6291460
  2.9 33.1 %collective-permute-start = (f32[64,384]{1,0:T(8,128)S(1)}, f32[64,384]{1,0:T(8,128)S(1)}, u32[]{:S(2)}, u32[]{:S(2)}) collective-permute-start(f32[64,384]{1,0:T(8,128)S(1)} %get-tuple-element.28.own1_ref), channel_id=1, source_target_pairs={{0,4},{4,0},{1,5},{5,1},{2,6},{6,2},{3,7},{7,3},{8,12},{12,8},{9,1... | collective-permute-start | bytes 294920 | tf_op jit(solution)/shard_map/ppermute | solution.py:566
  6.2 8.8 %collective-permute-start.2 = (f32[12,8,128]{2,1,0:T(8,128)S(1)}, f32[12,8,128]{2,1,0:T(8,128)S(1)}, u32[]{:S(2)}, u32[]{:S(2)}) collective-permute-start(f32[12,8,128]{2,1,0:T(8,128)S(1)} %get-tuple-element.37), channel_id=1, source_target_pairs={{0,4},{4,0},{1,5},{5,1},{2,6},{6,2},{3,7},{7,3},{8,12},{12,8},{9,1... | collective-permute-start | bytes 147464 | tf_op jit(solution)/shard_map/ppermute | solution.py:566
  14.9 18.3 %copy-start = (f32[512,1024]{1,0:T(8,128)}, f32[512,1024]{1,0:T(8,128)S(1)}, u32[]{:S(2)}) copy-start(f32[512,1024]{1,0:T(8,128)S(1)} %shard_map.65.second_ref.field1_ref) | copy-start | bytes 6291460
  15.0 2.9 %collective-permute-start.3 = (f32[9,8,128]{2,1,0:T(8,128)S(1)}, f32[9,8,128]{2,1,0:T(8,128)S(1)}, u32[]{:S(2)}, u32[]{:S(2)}) collective-permute-start(f32[9,8,128]{2,1,0:T(8,128)S(1)} %slice.77), channel_id=1, source_target_pairs={{0,8},{8,0},{16,24},{24,16},{32,40},{40,32},{48,56},{56,48},{1,9},... | collective-permute-start | bytes 110600 | tf_op jit(solution)/shard_map/ppermute | solution.py:566
  17.9 3.6 %collective-permute-start.4 = (f32[6,8,128]{2,1,0:T(8,128)S(1)}, f32[6,8,128]{2,1,0:T(8,128)S(1)}, u32[]{:S(2)}, u32[]{:S(2)}) collective-permute-start(f32[6,8,128]{2,1,0:T(8,128)S(1)} %slice_add_fusion), channel_id=1, source_target_pairs={{0,16},{8,24},{16,0},{24,8},{32,48},{40,56},{48,32},{56,40},{1,17}... | collective-permute-start | bytes 73736 | tf_op jit(solution)/shard_map/ppermute | solution.py:566
  21.5 5.0 %collective-permute-start.5 = (f32[4,8,128]{2,1,0:T(8,128)S(1)}, f32[4,8,128]{2,1,0:T(8,128)S(1)}, u32[]{:S(2)}, u32[]{:S(2)}) collective-permute-start(f32[4,8,128]{2,1,0:T(8,128)S(1)} %slice_add_fusion.1), channel_id=1, source_target_pairs={{0,56},{8,48},{16,40},{24,32},{32,24},{40,16},{48,8},{56,0},{1,57}... | collective-permute-start | bytes 49160 | tf_op jit(solution)/shard_map/ppermute | solution.py:566
  26.5 2.8 %collective-permute-start.6 = (f32[2,8,128]{2,1,0:T(8,128)S(1)}, f32[2,8,128]{2,1,0:T(8,128)S(1)}, u32[]{:S(2)}, u32[]{:S(2)}) collective-permute-start(f32[2,8,128]{2,1,0:T(8,128)S(1)} %slice_add_fusion.2), channel_id=1, source_target_pairs={{0,64},{64,0},{128,192},{192,128},{1,65},{65,1},{129,193},{193,129... | collective-permute-start | bytes 24584 | tf_op jit(solution)/shard_map/ppermute | solution.py:566
  29.3 4.0 %collective-permute-start.7 = (f32[9,8,128]{2,1,0:T(8,128)S(1)}, f32[9,8,128]{2,1,0:T(8,128)S(1)}, u32[]{:S(2)}, u32[]{:S(2)}) collective-permute-start(f32[9,8,128]{2,1,0:T(8,128)S(1)} %constant_dynamic-update-slice_fusion), channel_id=1, source_target_pairs={{0,1},{1,0},{2,3},{3,2},{4,5},{5,4},{6,7},{7,6},{8,9},{9,8},{10,11... | collective-permute-start | bytes 110600 | tf_op jit(solution)/shard_map/ppermute | solution.py:566
  30.7 5.3 %copy-start.2 = (f32[7,1,64,64]{3,2,1,0:T(8,128)S(1)}, f32[7,1,64,64]{3,2,1,0:T(8,128)}, u32[]{:S(2)}) copy-start(f32[7,1,64,64]{3,2,1,0:T(8,128)} %link_ref.3) | copy-start | bytes 344068
  30.7 5.3 %copy-start.4 = (s32[7,128]{1,0:T(8,128)S(1)}, s32[7,128]{1,0:T(8,128)}, u32[]{:S(2)}) copy-start(s32[7,128]{1,0:T(8,128)} %ranks_ref.5) | copy-start | bytes 10756
  33.3 8.2 %collective-permute-start.8 = (f32[2,9,8,128]{3,2,1,0:T(8,128)S(1)}, f32[2,9,8,128]{3,2,1,0:T(8,128)S(1)}, u32[]{:S(2)}, u32[]{:S(2)}) collective-permute-start(f32[2,9,8,128]{3,2,1,0:T(8,128)S(1)} %pad_maximum_fusion.1), channel_id=1, source_target_pairs={{0,2},{1,3},{2,0},{3,1},{4,6},{5,7},{6,4},{7,5},{8,10},{9,11},{10,... | collective-permute-start | bytes 221192 | tf_op jit(solution)/shard_map/ppermute | solution.py:566
  41.5 7.5 %collective-permute-start.9 = (f32[4,9,8,128]{3,2,1,0:T(8,128)S(1)}, f32[4,9,8,128]{3,2,1,0:T(8,128)S(1)}, u32[]{:S(2)}, u32[]{:S(2)}) collective-permute-start(f32[4,9,8,128]{3,2,1,0:T(8,128)S(1)} %pad_maximum_fusion.near_ref), channel_id=1, source_target_pairs={{0,4},{4,0},{1,5},{5,1},{2,6},{6,2},{3,7},{7,3},{8,12},{12,8},{9,1... | collective-permute-start | bytes 442376 | tf_op jit(solution)/shard_map/ppermute | solution.py:566
  58.2 1.7 %collective-permute-start.10 = (f32[5,128,128]{2,1,0:T(8,128)S(1)}, f32[5,128,128]{2,1,0:T(8,128)S(1)}, u32[]{:S(2)}, u32[]{:S(2)}) collective-permute-start(f32[5,128,128]{2,1,0:T(8,128)S(1)} %get-tuple-element.40), channel_id=1, source_target_pairs={{0,4},{4,0},{1,5},{5,1},{2,6},{6,2},{3,7},{7,3},{8,12},{12,8},{9,1... | collective-permute-start | bytes 983048 | tf_op jit(solution)/shard_map/ppermute | solution.py:566
  95.6 9.1 %collective-permute-start.13 = (f32[32,16,128]{2,1,0:T(8,128)S(1)}, f32[32,16,128]{2,1,0:T(8,128)S(1)}, u32[]{:S(2)}, u32[]{:S(2)}) collective-permute-start(f32[32,16,128]{2,1,0:T(8,128)S(1)} %all_to_all.11.near_ref), channel_id=1, source_target_pairs={{0,4},{4,0},{1,5},{5,1},{2,6},{6,2},{3,7},{7,3},{8,12},{12,8},{9,1... | collective-permute-start | bytes 786440 | tf_op jit(solution)/shard_map/ppermute | solution.py:566
  99.2 3.7 %collective-permute-start.11 = (f32[128,128]{1,0:T(8,128)S(1)}, f32[128,128]{1,0:T(8,128)S(1)}, u32[]{:S(2)}, u32[]{:S(2)}) collective-permute-start(f32[128,128]{1,0:T(8,128)S(1)} %two.1), channel_id=1, source_target_pairs={{0,8},{8,0},{16,24},{24,16},{32,40},{40,32},{48,56},{56,48},{1,9},... | collective-permute-start | bytes 196616 | tf_op jit(solution)/shard_map/ppermute | solution.py:566
  100.7 3.1 %collective-permute-start.1 = (f32[2,128,128]{2,1,0:T(8,128)S(1)}, f32[2,128,128]{2,1,0:T(8,128)S(1)}, u32[]{:S(2)}, u32[]{:S(2)}) collective-permute-start(f32[2,128,128]{2,1,0:T(8,128)S(1)} %get-tuple-element.34), channel_id=1, source_target_pairs={{0,4},{4,0},{1,5},{5,1},{2,6},{6,2},{3,7},{7,3},{8,12},{12,8},{9,1... | collective-permute-start | bytes 393224 | tf_op jit(solution)/shard_map/ppermute | solution.py:566
  103.0 1.8 %collective-permute-start.12 = (f32[128,128]{1,0:T(8,128)S(1)}, f32[128,128]{1,0:T(8,128)S(1)}, u32[]{:S(2)}, u32[]{:S(2)}) collective-permute-start(f32[128,128]{1,0:T(8,128)S(1)} %collective-permute-done.11.near2_ref), channel_id=1, source_target_pairs={{0,4},{4,0},{1,5},{5,1},{2,6},{6,2},{3,7},{7,3},{8,12},{12,8},{9,1... | collective-permute-start | bytes 196616 | tf_op jit(solution)/shard_map/ppermute | solution.py:566

commit v3 on v2

--- a/solution.py
+++ b/solution.py
@@ -73,16 +73,16 @@
     wide = wide_ref[...]
     gram = dot(wide, wide, NT)
     first_ref[...] = gram[:R, :UP]
-    for part in range(8):
-        tile = 0
-        for level in range(6):
-            top = level * R + 8 * part
-            for lane in range(level // 2, 3):
-                tiles_ref[part, tile] = gram[top:top + 8, lane * 128:lane * 128 + 128]
-                tile += 1
-    part, other = lax.axis_index("cols"), lax.axis_index("core") * 4
-    mine_ref[...] = tiles_ref[part + other]
-    theirs_ref[...] = tiles_ref[part + 4 - other]
+    tile = 0
+    for level in range(6):
+        for lane in range(level // 2, 3):
+            for half in range(2):
+                top = level * R + 32 * half
+                tiles_ref[half, tile] = gram[top:top + 32, lane * 128:lane * 128 + 128]
+            tile += 1
+    core = lax.axis_index("core")
+    mine_ref[...] = tiles_ref[core]
+    theirs_ref[...] = tiles_ref[1 - core]
     gram0_ref[...] = gram[UP:, UP:]
     cross0_ref[...] = gram[UP:, :UP]
     keep.wait()
@@ -92,13 +92,13 @@
     return pl.pallas_call(
         gram_kernel,
         out_shape=(
-            shape(512, ROWS, dtype=BF16), shape(12, 8, 128), shape(12, 8, 128), shape(R, UP), shape(128, 128),
+            shape(512, ROWS, dtype=BF16), shape(12, 32, 128), shape(12, 32, 128), shape(R, UP), shape(128, 128),
             shape(128, UP),
             pltpu.VMEM((COLS, ROWS), BF16),
         ),
         in_specs=[HBM] * 2,
         out_specs=(VMEM,) * 7,
-        scratch_shapes=[pltpu.VMEM((LEVELS, R, ROWS), BF16), pltpu.VMEM((8, 12, 8, 128), F32), pltpu.SemaphoreType.DMA((2,))],
+        scratch_shapes=[pltpu.VMEM((LEVELS, R, ROWS), BF16), pltpu.VMEM((2, 12, 32, 128), F32), pltpu.SemaphoreType.DMA((2,))],
         compiler_params=params(14),
         cost_estimate=cost(2e9, 4e6),
         name="gram",
@@ -360,13 +360,11 @@
 
 
 def late_kernel(ranks_ref, joint_ref, near_ref, far_ref, x_ref, keep_ref, send_ref, pk_ref, work_ref):
-    leaf, col, core = leaf_index(), lax.axis_index("cols"), lax.axis_index("core")
+    leaf, core = leaf_index(), lax.axis_index("core")
     for other, source in ((0, near_ref), (1, far_ref)):
-        for slot, offset in enumerate((0, 1, 2, 3)):
-            part = jnp.bitwise_xor(core, other) * 4 + jnp.bitwise_xor(col, offset)
-            rows = pl.ds(pl.multiple_of(part * 8, 8), 8)
-            for tile in range(9):
-                pk_ref[tile, rows, :] = source[slot, tile]
+        rows = pl.ds(pl.multiple_of(jnp.bitwise_xor(core, other) * 32, 32), 32)
+        for tile in range(9):
+            pk_ref[tile, rows, :] = source[tile]
     systems = []
     for level in range(2, 7):
         systems.append(system(joint_ref[level - 2], pk_ref[OWN_TILE[level]], level % 2 == 0))
@@ -581,7 +579,7 @@
 
     chip = (mine + got)[3:]
     got = swap(chip, 1, "z")
-    low_lane = lax.broadcasted_iota(jnp.int32, (8, 128), 1) < R
+    low_lane = lax.broadcasted_iota(jnp.int32, (32, 128), 1) < R
     pack = [chip[0], got[1], got[2]]
     total = chip[3:] + got[3:]
     got = swap(total, 2, "z")
@@ -592,11 +590,7 @@
     total = total[2:] + got[2:]
     got = swap(total, 1, "x")
     pack += [jnp.where(low_lane, total[0], got[0]), total[1] + got[1]]
-    pack = jnp.stack(pack)
-    got = swap(pack, 1, "cols")
-    pack = jnp.stack([pack, got])
-    got = swap(pack, 2, "cols")
-    near = jnp.concatenate([pack, got], axis=0)
+    near = jnp.stack(pack)
     far = swap(near, 1, "core")
     u1 = swap(u1, 1, "core")
     keep, send = late(ranks, joint, near, far, x)

time: 112 us -> 112 us (level)
  the two profiles are of different devices: /device:TPU:1 before, /device:TPU:16 now
where the time goes in v3:
time: 112 us; the launch traced here: 111 us
  blocking collectives  38.3 us (34%)
  Pallas kernels  37.9 us (34%)
  waiting for transfers between devices  18.6 us (17%)
  starting transfers between devices  15.3 us (14%)
    all_to_all x1, blocking collectives, local(): got = lax.all_to_all(dealt, ('x', 'z'), 0, 0, tiled=True)  21.7 us
    ppermute x12, waiting for transfers between devices, swap(): lax.ppermute(array, axis, [(i, i ^ mask) for i in range(lax.axis_size(axi...  18.6 us
    all_to_all x1, blocking collectives, local(): back = lax.all_to_all(total, ('x', 'z'), 0, 0, tiled=True)  16.6 us
    ppermute x12, starting transfers between devices, swap(): lax.ppermute(array, axis, [(i, i ^ mask) for i in range(lax.axis_size(axi...  15.3 us
    pallas_call x1, Pallas kernels, late(): pl.pallas_call(late_kernel, out_shape=(shape(5, 128, 128), shape(5, 128,...  9.2 us
    pallas_call x1, Pallas kernels, final(): pl.pallas_call(final_kernel, grid=(ROWS // BLK,), out_shape=shape(COLS, R...  7.03 us
    pallas_call x1, Pallas kernels, solve_early(): pl.pallas_call(solve_early_kernel, out_shape=(shape(128, 128), shape(R, 1...  5.43 us
    pallas_call x1, Pallas kernels, permute_first(): pl.pallas_call(permute_first_kernel, out_shape=(shape(COLS, LEAF, dtype=B...  2.9 us
  transfers between devices with their start and end apart: 12, of which 7 were waited for; matrix products, arithmetic and copies ran while one was open for 0% of the time, Pallas kernels for 17%

profile of v3, /device:TPU:16, one launch (start us, length us, event | category | flops | bytes accessed | tf_op | source)
XLA Modules:
  0.0 110.6 jit_solution(13286216578214288487)
XLA Ops:
  0.0 2.9 %gram.1 = (bf16[512,2048]{1,0:T(8,128)(2,1)S(1)}, f32[12,32,128]{2,1,0:T(8,128)S(1)}, f32[12,32,128]{2,1,0:T(8,128)S(1)}, f32[64,384]{1,0:T(8,128)S(1)}, f32[128...) custom-call(bf16[7,64,2048]{2,1,0:T(8,128)(2,1)} %bases_ref.1, bf16[512,2048]{1,0:T(8,128)(2,1)} %samples_ref.1), custom_call_target="tpu_custom_call" | custom-call | flops 2000000000 | bytes 4000000 | tf_op jit(solution)/shard_map/gram/pallas_call | solution.py:92
  2.9 0.1 collective-permute-start.2
  3.0 0.5 collective-permute-start
  3.5 2.9 %permute_second.1.permuted_ref = bf16[512,1024]{1,0:T(8,128)(2,1)S(1)} custom-call(bf16[512,2048]{1,0:T(8,128)(2,1)S(1)} %get-tuple-element.23.samples_ref, s32[1,2048]{1,0:T(1,128)S(1)} %bitcast.1), custom_call_target="tpu_custom_call" | custom-call | flops 2147483648 | bytes 4000000 | tf_op jit(solution)/shard_map/permute_second/pallas_call | solution.py:146
  6.4 2.9 %permute_first.1 = (bf16[512,1024]{1,0:T(8,128)(2,1)S(1)}, bf16[2,1024,1024]{2,1,0:T(8,128)(2,1)S(1)}) custom-call(bf16[512,2048]{1,0:T(8,128)(2,1)S(1)} %get-tuple-element.23.samples_ref, s32[1,2048]{1,0:T(1,128)S(1)} %bitcast.2, bf16[2,1024,1024]{2,1,0:T(8,128)(2,1)} %factor_ref.1), custom_call_target="tpu_custom_call" | custom-call | flops 2147483648 | bytes 4000000 | tf_op jit(solution)/shard_map/permute_first/pallas_call | solution.py:133
  9.3 1.4 %shard_map.64.first_ref.field0_ref = f32[512,1024]{1,0:T(8,128)S(1)} custom-call(bf16[512,1024]{1,0:T(8,128)(2,1)S(1)} %get-tuple-element.24.permuted_ref, bf16[2,1024,1024]{2,1,0:T(8,128)(2,1)S(1)} %get-tuple-element.25.factor_ref), custom_call_target="tpu_custom_call" | custom-call | flops 1073741824 | bytes 5000000 | tf_op jit(solution)/shard_map/pallas_call | solution.py:167
  10.7 1.4 %shard_map.65.second_ref.field1_ref = f32[512,1024]{1,0:T(8,128)S(1)} custom-call(bf16[512,1024]{1,0:T(8,128)(2,1)S(1)} %permute_second.1.permuted_ref, bf16[2,1024,1024]{2,1,0:T(8,128)(2,1)S(1)} %get-tuple-element.25.factor_ref), custom_call_target="tpu_custom_call" | custom-call | flops 1073741824 | bytes 5000000 | tf_op jit(solution)/shard_map/pallas_call | solution.py:167
  12.2 0.0 copy-start.2
  12.2 0.0 copy-start.4
  12.2 2.6 %project.1.q_ref = f32[512,512]{1,0:T(8,128)S(1)} custom-call(f32[512,1024]{1,0:T(8,128)S(1)} %shard_map.64.first_ref.field0_ref, f32[512,1024]{1,0:T(8,128)S(1)} %shard_map.65.second_ref.field1_ref, bf16[512,2048]{1,0:T(8,128)(2,1)S(1)} %get-tuple-element.26.wide_ref), custom_call_target="tpu_custom_call" | custom-call | flops 2147483648 | bytes 7000000 | tf_op jit(solution)/shard_map/project/pallas_call | solution.py:192
  14.8 5.4 %solve_early.1 = (f32[128,128]{1,0:T(8,128)S(1)}, f32[64,128]{1,0:T(8,128)S(1)}, f32[128,384]{1,0:T(8,128)S(1)}) custom-call(s32[7,128]{1,0:T(8,128)S(1)} %copy-done.4, f32[7,1,64,64]{3,2,1,0:T(8,128)S(1)} %copy-done.2, f32[128,128]{1,0:T(8,128)S(1)} %get-tuple-element.27.gram0_ref, f32[64,384]{1,0:T(8,128)S(1)} %get-tuple-element.28.own1_ref, ...), custom_call_target="tpu_custom_call" | custom-call | flops 3000000000 | bytes 4000000 | tf_op jit(solution)/shard_map/solve_early/pallas_call | solution.py:311
  20.3 2.0 %collective-permute-start.3 = (f32[9,32,128]{2,1,0:T(8,128)S(1)}, f32[9,32,128]{2,1,0:T(8,128)S(1)}, u32[]{:S(2)}, u32[]{:S(2)}) collective-permute-start(f32[9,32,128]{2,1,0:T(8,128)S(1)} %slice.77), channel_id=1, source_target_pairs={{0,8},{8,0},{16,24},{24,16},{32,40},{40,32},{48,56},{56,48},{1,9},... | collective-permute-start | bytes 442376 | tf_op jit(solution)/shard_map/ppermute | solution.py:564
  22.3 4.1 %collective-permute-done.3 = f32[9,32,128]{2,1,0:T(8,128)S(1)} collective-permute-done((f32[9,32,128]{2,1,0:T(8,128)S(1)}, f32[9,32,128]{2,1,0:T(8,128)S(1)}, u32[]{:S(2)}, u32[]{:S(2)}) %collective-permute-start.3) | collective-permute-done | bytes 147488 | tf_op jit(solution)/shard_map/ppermute | solution.py:564
  26.5 3.4 %collective-permute-start.4 = (f32[6,32,128]{2,1,0:T(8,128)S(1)}, f32[6,32,128]{2,1,0:T(8,128)S(1)}, u32[]{:S(2)}, u32[]{:S(2)}) collective-permute-start(f32[6,32,128]{2,1,0:T(8,128)S(1)} %slice_add_fusion), channel_id=1, source_target_pairs={{0,16},{8,24},{16,0},{24,8},{32,48},{40,56},{48,32},{56,40},{1,17}... | collective-permute-start | bytes 294920 | tf_op jit(solution)/shard_map/ppermute | solution.py:564
  29.8 4.5 %collective-permute-done.4 = f32[6,32,128]{2,1,0:T(8,128)S(1)} collective-permute-done((f32[6,32,128]{2,1,0:T(8,128)S(1)}, f32[6,32,128]{2,1,0:T(8,128)S(1)}, u32[]{:S(2)}, u32[]{:S(2)}) %collective-permute-start.4) | collective-permute-done | bytes 98336 | tf_op jit(solution)/shard_map/ppermute | solution.py:564
  34.3 5.0 %collective-permute-start.5 = (f32[4,32,128]{2,1,0:T(8,128)S(1)}, f32[4,32,128]{2,1,0:T(8,128)S(1)}, u32[]{:S(2)}, u32[]{:S(2)}) collective-permute-start(f32[4,32,128]{2,1,0:T(8,128)S(1)} %slice_add_fusion.1), channel_id=1, source_target_pairs={{0,56},{8,48},{16,40},{24,32},{32,24},{40,16},{48,8},{56,0},{1,57}... | collective-permute-start | bytes 196616 | tf_op jit(solution)/shard_map/ppermute | solution.py:564
  39.3 2.5 %collective-permute-done.5 = f32[4,32,128]{2,1,0:T(8,128)S(1)} collective-permute-done((f32[4,32,128]{2,1,0:T(8,128)S(1)}, f32[4,32,128]{2,1,0:T(8,128)S(1)}, u32[]{:S(2)}, u32[]{:S(2)}) %collective-permute-start.5) | collective-permute-done | bytes 65568 | tf_op jit(solution)/shard_map/ppermute | solution.py:564
  41.8 1.5 %collective-permute-start.6 = (f32[2,32,128]{2,1,0:T(8,128)S(1)}, f32[2,32,128]{2,1,0:T(8,128)S(1)}, u32[]{:S(2)}, u32[]{:S(2)}) collective-permute-start(f32[2,32,128]{2,1,0:T(8,128)S(1)} %slice_add_fusion.2), channel_id=1, source_target_pairs={{0,64},{64,0},{128,192},{192,128},{1,65},{65,1},{129,193},{193,129... | collective-permute-start | bytes 98312 | tf_op jit(solution)/shard_map/ppermute | solution.py:564
  43.3 2.4 %collective-permute-done.6 = f32[2,32,128]{2,1,0:T(8,128)S(1)} collective-permute-done((f32[2,32,128]{2,1,0:T(8,128)S(1)}, f32[2,32,128]{2,1,0:T(8,128)S(1)}, u32[]{:S(2)}, u32[]{:S(2)}) %collective-permute-start.6) | collective-permute-done | bytes 32800 | tf_op jit(solution)/shard_map/ppermute | solution.py:564
  45.7 0.3 collective-permute-start.7
  46.0 2.1 %early.1 = (f32[512,128]{1,0:T(8,128)S(1)}, f32[2,128,128]{2,1,0:T(8,128)S(1)}, f32[512,384]{1,0:T(8,128)S(1)}, f32[5,64,128]{2,1,0:T(8,128)S(1)}) custom-call(s32[7,128]{1,0:T(8,128)S(1)} %copy-done.4, f32[7,1,64,64]{3,2,1,0:T(8,128)S(1)} %copy-done.2, f32[512,512]{1,0:T(8,128)S(1)} %project.1.q_ref, f32[128,128]{1,0:T(8,128)S(1)} %get-tuple-element.29.from0_ref, ...), custom_call_target="tpu_custom_call" | custom-call | flops 3000000000 | bytes 4000000 | tf_op jit(solution)/shard_map/early/pallas_call | solution.py:347
  48.1 0.0 collective-permute-done.7.far_ref
  48.1 9.2 %late.1 = (f32[5,128,128]{2,1,0:T(8,128)S(1)}, f32[5,128,128]{2,1,0:T(8,128)S(1)}) custom-call(s32[7,128]{1,0:T(8,128)S(1)} %copy-done.4, f32[5,64,128]{2,1,0:T(8,128)S(1)} %get-tuple-element.35.joint_ref, f32[9,32,128]{2,1,0:T(8,128)S(1)} %constant_dynamic-update-slice_fusion.near_ref, f32[9,32,128]{2,1,0:T(8,128)S(1)} %collective-permute-done.7.far_ref, ...), custom_call_target="tpu_custom_call" | custom-call | flops 4000000000 | bytes 4000000 | tf_op jit(solution)/shard_map/late/pallas_call | solution.py:394
  57.4 0.6 collective-permute-start.8
  57.9 1.3 %collective-permute-done.8.recv_ref = f32[5,128,128]{2,1,0:T(8,128)S(1)} collective-permute-done((f32[5,128,128]{2,1,0:T(8,128)S(1)}, f32[5,128,128]{2,1,0:T(8,128)S(1)}, u32[]{:S(2)}, u32[]{:S(2)}) %collective-permute-start.8) | collective-permute-done | bytes 327712 | tf_op jit(solution)/shard_map/ppermute | solution.py:564
  59.2 21.7 %all_to_all.10.got_ref = f32[32,16,128]{2,1,0:T(8,128)S(1)} all-to-all(f32[32,16,128]{2,1,0:T(8,128)S(1)} %deal.1), channel_id=1, replica_groups=mesh['x'=4,'z'=8,'core'=2,'cols'=4] {'x','z'}, dimensions={0} | all-to-all | bytes 524288 | tf_op jit(solution)/shard_map/all_to_all | solution.py:601
  80.9 16.6 %all_to_all.11.near_ref = f32[32,16,128]{2,1,0:T(8,128)S(1)} all-to-all(f32[32,16,128]{2,1,0:T(8,128)S(1)} %collect.1), channel_id=1, replica_groups=mesh['x'=4,'z'=8,'core'=2,'cols'=4] {'x','z'}, dimensions={0} | all-to-all | bytes 524288 | tf_op jit(solution)/shard_map/all_to_all | solution.py:604
  97.6 1.8 %collective-permute-start.9 = (f32[128,128]{1,0:T(8,128)S(1)}, f32[128,128]{1,0:T(8,128)S(1)}, u32[]{:S(2)}, u32[]{:S(2)}) collective-permute-start(f32[128,128]{1,0:T(8,128)S(1)} %two.1), channel_id=1, source_target_pairs={{0,8},{8,0},{16,24},{24,16},{32,40},{40,32},{48,56},{56,48},{1,9},... | collective-permute-start | bytes 196616 | tf_op jit(solution)/shard_map/ppermute | solution.py:564
  99.4 0.2 collective-permute-start.1
  99.6 2.6 %collective-permute-done.9.near2_ref = f32[128,128]{1,0:T(8,128)S(1)} collective-permute-done((f32[128,128]{1,0:T(8,128)S(1)}, f32[128,128]{1,0:T(8,128)S(1)}, u32[]{:S(2)}, u32[]{:S(2)}) %collective-permute-start.9) | collective-permute-done | bytes 65568 | tf_op jit(solution)/shard_map/ppermute | solution.py:564
  102.2 1.2 %collective-permute-done.10.far2_ref = f32[128,128]{1,0:T(8,128)S(1)} collective-permute-done((f32[128,128]{1,0:T(8,128)S(1)}, f32[128,128]{1,0:T(8,128)S(1)}, u32[]{:S(2)}, u32[]{:S(2)}) %collective-permute-start.10) | collective-permute-done | bytes 65568 | tf_op jit(solution)/shard_map/ppermute | solution.py:564
  103.4 7.0 %final.1 = f32[512,2048]{1,0:T(8,128)} custom-call(f32[512,1024]{1,0:T(8,128)S(1)} %shard_map.64.first_ref.field0_ref, f32[512,1024]{1,0:T(8,128)} %copy-done, bf16[512,2048]{1,0:T(8,128)(2,1)} %copy-done.1, f32[512,128]{1,0:T(8,128)S(1)} %get-tuple-element.33.u0_ref, f32[2,128,128]{2,1,0:T(8,128)S(1)} %collective-permute-done.1.u1_ref, ...), custom_call_target="tpu_custom_call" | custom-call | flops 2147483648 | bytes 12000000 | tf_op jit(solution)/shard_map/final/pallas_call | solution.py:545
  (31 shorter events, 0.2 us)
Async XLA Ops:
  0.0 3.5 %copy-start.3 = (s32[2048]{0:T(1024)S(1)}, s32[2048]{0:T(1024)}, u32[]{:S(2)}) copy-start(s32[2048]{0:T(1024)} %param.7) | copy-start | bytes 24580
  2.9 9.3 %copy-start.1 = (bf16[512,2048]{1,0:T(8,128)(2,1)}, bf16[512,2048]{1,0:T(8,128)(2,1)S(1)}, u32[]{:S(2)}) copy-start(bf16[512,2048]{1,0:T(8,128)(2,1)S(1)} %get-tuple-element.26.wide_ref) | copy-start | bytes 6291460
  2.9 17.4 %collective-permute-start.2 = (f32[12,32,128]{2,1,0:T(8,128)S(1)}, f32[12,32,128]{2,1,0:T(8,128)S(1)}, u32[]{:S(2)}, u32[]{:S(2)}) collective-permute-start(f32[12,32,128]{2,1,0:T(8,128)S(1)} %get-tuple-element.37), channel_id=1, source_target_pairs={{0,4},{4,0},{1,5},{5,1},{2,6},{6,2},{3,7},{7,3},{8,12},{12,8},{9,1... | collective-permute-start | bytes 589832 | tf_op jit(solution)/shard_map/ppermute | solution.py:564
  3.0 11.8 %collective-permute-start = (f32[64,384]{1,0:T(8,128)S(1)}, f32[64,384]{1,0:T(8,128)S(1)}, u32[]{:S(2)}, u32[]{:S(2)}) collective-permute-start(f32[64,384]{1,0:T(8,128)S(1)} %get-tuple-element.28.own1_ref), channel_id=1, source_target_pairs={{0,4},{4,0},{1,5},{5,1},{2,6},{6,2},{3,7},{7,3},{8,12},{12,8},{9,1... | collective-permute-start | bytes 294920 | tf_op jit(solution)/shard_map/ppermute | solution.py:564
  12.1 2.6 %copy-start = (f32[512,1024]{1,0:T(8,128)}, f32[512,1024]{1,0:T(8,128)S(1)}, u32[]{:S(2)}) copy-start(f32[512,1024]{1,0:T(8,128)S(1)} %shard_map.65.second_ref.field1_ref) | copy-start | bytes 6291460
  12.2 2.6 %copy-start.2 = (f32[7,1,64,64]{3,2,1,0:T(8,128)S(1)}, f32[7,1,64,64]{3,2,1,0:T(8,128)}, u32[]{:S(2)}) copy-start(f32[7,1,64,64]{3,2,1,0:T(8,128)} %link_ref.3) | copy-start | bytes 344068
  12.2 2.6 %copy-start.4 = (s32[7,128]{1,0:T(8,128)S(1)}, s32[7,128]{1,0:T(8,128)}, u32[]{:S(2)}) copy-start(s32[7,128]{1,0:T(8,128)} %ranks_ref.5) | copy-start | bytes 10756
  20.3 6.1 %collective-permute-start.3 = (f32[9,32,128]{2,1,0:T(8,128)S(1)}, f32[9,32,128]{2,1,0:T(8,128)S(1)}, u32[]{:S(2)}, u32[]{:S(2)}) collective-permute-start(f32[9,32,128]{2,1,0:T(8,128)S(1)} %slice.77), channel_id=1, source_target_pairs={{0,8},{8,0},{16,24},{24,16},{32,40},{40,32},{48,56},{56,48},{1,9},... | collective-permute-start | bytes 442376 | tf_op jit(solution)/shard_map/ppermute | solution.py:564
  26.5 7.8 %collective-permute-start.4 = (f32[6,32,128]{2,1,0:T(8,128)S(1)}, f32[6,32,128]{2,1,0:T(8,128)S(1)}, u32[]{:S(2)}, u32[]{:S(2)}) collective-permute-start(f32[6,32,128]{2,1,0:T(8,128)S(1)} %slice_add_fusion), channel_id=1, source_target_pairs={{0,16},{8,24},{16,0},{24,8},{32,48},{40,56},{48,32},{56,40},{1,17}... | collective-permute-start | bytes 294920 | tf_op jit(solution)/shard_map/ppermute | solution.py:564
  34.3 7.5 %collective-permute-start.5 = (f32[4,32,128]{2,1,0:T(8,128)S(1)}, f32[4,32,128]{2,1,0:T(8,128)S(1)}, u32[]{:S(2)}, u32[]{:S(2)}) collective-permute-start(f32[4,32,128]{2,1,0:T(8,128)S(1)} %slice_add_fusion.1), channel_id=1, source_target_pairs={{0,56},{8,48},{16,40},{24,32},{32,24},{40,16},{48,8},{56,0},{1,57}... | collective-permute-start | bytes 196616 | tf_op jit(solution)/shard_map/ppermute | solution.py:564
  41.8 3.9 %collective-permute-start.6 = (f32[2,32,128]{2,1,0:T(8,128)S(1)}, f32[2,32,128]{2,1,0:T(8,128)S(1)}, u32[]{:S(2)}, u32[]{:S(2)}) collective-permute-start(f32[2,32,128]{2,1,0:T(8,128)S(1)} %slice_add_fusion.2), channel_id=1, source_target_pairs={{0,64},{64,0},{128,192},{192,128},{1,65},{65,1},{129,193},{193,129... | collective-permute-start | bytes 98312 | tf_op jit(solution)/shard_map/ppermute | solution.py:564
  45.7 2.4 %collective-permute-start.7 = (f32[9,32,128]{2,1,0:T(8,128)S(1)}, f32[9,32,128]{2,1,0:T(8,128)S(1)}, u32[]{:S(2)}, u32[]{:S(2)}) collective-permute-start(f32[9,32,128]{2,1,0:T(8,128)S(1)} %constant_dynamic-update-slice_fusion.near_ref), channel_id=1, source_target_pairs={{0,4},{4,0},{1,5},{5,1},{2,6},{6,2},{3,7},{7,3},{8,12},{12,8},{9,1... | collective-permute-start | bytes 442376 | tf_op jit(solution)/shard_map/ppermute | solution.py:564
  57.4 1.8 %collective-permute-start.8 = (f32[5,128,128]{2,1,0:T(8,128)S(1)}, f32[5,128,128]{2,1,0:T(8,128)S(1)}, u32[]{:S(2)}, u32[]{:S(2)}) collective-permute-start(f32[5,128,128]{2,1,0:T(8,128)S(1)} %get-tuple-element.40), channel_id=1, source_target_pairs={{0,4},{4,0},{1,5},{5,1},{2,6},{6,2},{3,7},{7,3},{8,12},{12,8},{9,1... | collective-permute-start | bytes 983048 | tf_op jit(solution)/shard_map/ppermute | solution.py:564
  97.6 5.9 %collective-permute-start.11 = (f32[32,16,128]{2,1,0:T(8,128)S(1)}, f32[32,16,128]{2,1,0:T(8,128)S(1)}, u32[]{:S(2)}, u32[]{:S(2)}) collective-permute-start(f32[32,16,128]{2,1,0:T(8,128)S(1)} %all_to_all.11.near_ref), channel_id=1, source_target_pairs={{0,4},{4,0},{1,5},{5,1},{2,6},{6,2},{3,7},{7,3},{8,12},{12,8},{9,1... | collective-permute-start | bytes 786440 | tf_op jit(solution)/shard_map/ppermute | solution.py:564
  97.6 4.6 %collective-permute-start.9 = (f32[128,128]{1,0:T(8,128)S(1)}, f32[128,128]{1,0:T(8,128)S(1)}, u32[]{:S(2)}, u32[]{:S(2)}) collective-permute-start(f32[128,128]{1,0:T(8,128)S(1)} %two.1), channel_id=1, source_target_pairs={{0,8},{8,0},{16,24},{24,16},{32,40},{40,32},{48,56},{56,48},{1,9},... | collective-permute-start | bytes 196616 | tf_op jit(solution)/shard_map/ppermute | solution.py:564
  99.4 2.8 %collective-permute-start.1 = (f32[2,128,128]{2,1,0:T(8,128)S(1)}, f32[2,128,128]{2,1,0:T(8,128)S(1)}, u32[]{:S(2)}, u32[]{:S(2)}) collective-permute-start(f32[2,128,128]{2,1,0:T(8,128)S(1)} %get-tuple-element.34), channel_id=1, source_target_pairs={{0,4},{4,0},{1,5},{5,1},{2,6},{6,2},{3,7},{7,3},{8,12},{12,8},{9,1... | collective-permute-start | bytes 393224 | tf_op jit(solution)/shard_map/ppermute | solution.py:564
  102.2 1.3 %collective-permute-start.10 = (f32[128,128]{1,0:T(8,128)S(1)}, f32[128,128]{1,0:T(8,128)S(1)}, u32[]{:S(2)}, u32[]{:S(2)}) collective-permute-start(f32[128,128]{1,0:T(8,128)S(1)} %collective-permute-done.9.near2_ref), channel_id=1, source_target_pairs={{0,4},{4,0},{1,5},{5,1},{2,6},{6,2},{3,7},{7,3},{8,12},{12,8},{9,1... | collective-permute-start | bytes 196616 | tf_op jit(solution)/shard_map/ppermute | solution.py:564

commit v4 on v3

--- a/solution.py
+++ b/solution.py
@@ -227,14 +227,12 @@
 def eliminate(work_ref, count):
     row = lax.broadcasted_iota(jnp.int32, (count, R, 128), 1)
     tile_row = lax.broadcasted_iota(jnp.int32, (count, 8, 128), 1)
-
-    def block(step, carry):
-        top = pl.multiple_of(step * 8, 8)
+    value = work_ref[...]
+    for top in range(0, R, 8):
         here = (row >= top) & (row < top + 8)
-        value = work_ref[...]
-        tile = work_ref[:, pl.ds(top, 8), :]
-        heads = [jnp.broadcast_to(tile[:, :, j:j + 1], (count, 8, 128)) for j in range(8)]
-        columns = [jnp.broadcast_to(value[:, :, j:j + 1], (count, R, 128)) for j in range(8)]
+        tile = value[:, top:top + 8, :]
+        heads = [jnp.broadcast_to(tile[:, :, j:j + 1], (count, 8, 128)) for j in range(top, top + 8)]
+        columns = [jnp.broadcast_to(value[:, :, j:j + 1], (count, R, 128)) for j in range(top, top + 8)]
         for j in range(8):
             inverse = 1.0 / heads[j][:, j:j + 1, :]
             pivot = tile[:, j:j + 1, :] * inverse
@@ -245,10 +243,7 @@
         for j in range(8):
             value = value - columns[j] * tile[:, j:j + 1, :]
         value = jnp.where(here, jnp.concatenate([tile] * 8, axis=1), value)
-        work_ref[...] = pltpu.roll(value, 120, 2)
-        return carry
-
-    lax.fori_loop(0, 8, block, 0)
+    work_ref[...] = pltpu.roll(value, R, 2)
 
 
 def solved(work_ref, item, rank_sibling, scale):

time: 112 us -> 108 us (0.964)
  Pallas kernels: 37.9 us -> 34.2 us
    pallas_call x1, Pallas kernels: 9.2 us -> 6.88 us  [late(): pl.pallas_call(late_kernel, out_shape=(shape(5, 128, 128), shape(5, 128,...]
    pallas_call x1, Pallas kernels: 5.43 us -> 4.05 us  [solve_early(): pl.pallas_call(solve_early_kernel, out_shape=(shape(128, 128), shape(R, 1...]
  transfers between devices with their start and end apart: 12 -> 12, of which waited for: 7 -> 7; matrix products, arithmetic and copies ran while one was open for 0% -> 0% of each run, Pallas kernels for 17% -> 16%
where the time goes in v4:
time: 108 us; the launch traced here: 107 us
  blocking collectives  38.3 us (35%)
  Pallas kernels  34.2 us (32%)
  waiting for transfers between devices  18.6 us (17%)
  starting transfers between devices  15.3 us (14%)
    all_to_all x1, blocking collectives, local(): got = lax.all_to_all(dealt, ('x', 'z'), 0, 0, tiled=True)  21.7 us
    ppermute x12, waiting for transfers between devices, swap(): lax.ppermute(array, axis, [(i, i ^ mask) for i in range(lax.axis_size(axi...  18.6 us
    all_to_all x1, blocking collectives, local(): back = lax.all_to_all(total, ('x', 'z'), 0, 0, tiled=True)  16.6 us
    ppermute x12, starting transfers between devices, swap(): lax.ppermute(array, axis, [(i, i ^ mask) for i in range(lax.axis_size(axi...  15.3 us
    pallas_call x1, Pallas kernels, final(): pl.pallas_call(final_kernel, grid=(ROWS // BLK,), out_shape=shape(COLS, R...  7.03 us
    pallas_call x1, Pallas kernels, late(): pl.pallas_call(late_kernel, out_shape=(shape(5, 128, 128), shape(5, 128,...  6.88 us
    pallas_call x1, Pallas kernels, solve_early(): pl.pallas_call(solve_early_kernel, out_shape=(shape(128, 128), shape(R, 1...  4.05 us
    pallas_call x1, Pallas kernels, permute_first(): pl.pallas_call(permute_first_kernel, out_shape=(shape(COLS, LEAF, dtype=B...  2.9 us
  transfers between devices with their start and end apart: 12, of which 7 were waited for; matrix products, arithmetic and copies ran while one was open for 0% of the time, Pallas kernels for 16%

profile of v4, /device:TPU:16, one launch (start us, length us, event | category | flops | bytes accessed | tf_op | source)
XLA Modules:
  0.0 106.9 jit_solution(405775425169731901)
XLA Ops:
  0.0 2.9 %gram.1 = (bf16[512,2048]{1,0:T(8,128)(2,1)S(1)}, f32[12,32,128]{2,1,0:T(8,128)S(1)}, f32[12,32,128]{2,1,0:T(8,128)S(1)}, f32[64,384]{1,0:T(8,128)S(1)}, f32[128...) custom-call(bf16[7,64,2048]{2,1,0:T(8,128)(2,1)} %bases_ref.1, bf16[512,2048]{1,0:T(8,128)(2,1)} %samples_ref.1), custom_call_target="tpu_custom_call" | custom-call | flops 2000000000 | bytes 4000000 | tf_op jit(solution)/shard_map/gram/pallas_call | solution.py:92
  2.9 0.1 collective-permute-start.2
  3.0 0.5 collective-permute-start
  3.5 2.9 %permute_second.1.permuted_ref = bf16[512,1024]{1,0:T(8,128)(2,1)S(1)} custom-call(bf16[512,2048]{1,0:T(8,128)(2,1)S(1)} %get-tuple-element.23.samples_ref, s32[1,2048]{1,0:T(1,128)S(1)} %bitcast.1), custom_call_target="tpu_custom_call" | custom-call | flops 2147483648 | bytes 4000000 | tf_op jit(solution)/shard_map/permute_second/pallas_call | solution.py:146
  6.4 2.9 %permute_first.1 = (bf16[512,1024]{1,0:T(8,128)(2,1)S(1)}, bf16[2,1024,1024]{2,1,0:T(8,128)(2,1)S(1)}) custom-call(bf16[512,2048]{1,0:T(8,128)(2,1)S(1)} %get-tuple-element.23.samples_ref, s32[1,2048]{1,0:T(1,128)S(1)} %bitcast.2, bf16[2,1024,1024]{2,1,0:T(8,128)(2,1)} %factor_ref.1), custom_call_target="tpu_custom_call" | custom-call | flops 2147483648 | bytes 4000000 | tf_op jit(solution)/shard_map/permute_first/pallas_call | solution.py:133
  9.3 1.4 %shard_map.64.first_ref.field0_ref = f32[512,1024]{1,0:T(8,128)S(1)} custom-call(bf16[512,1024]{1,0:T(8,128)(2,1)S(1)} %get-tuple-element.24.permuted_ref, bf16[2,1024,1024]{2,1,0:T(8,128)(2,1)S(1)} %get-tuple-element.25.factor_ref), custom_call_target="tpu_custom_call" | custom-call | flops 1073741824 | bytes 5000000 | tf_op jit(solution)/shard_map/pallas_call | solution.py:167
  10.7 1.4 %shard_map.65.second_ref.field1_ref = f32[512,1024]{1,0:T(8,128)S(1)} custom-call(bf16[512,1024]{1,0:T(8,128)(2,1)S(1)} %permute_second.1.permuted_ref, bf16[2,1024,1024]{2,1,0:T(8,128)(2,1)S(1)} %get-tuple-element.25.factor_ref), custom_call_target="tpu_custom_call" | custom-call | flops 1073741824 | bytes 5000000 | tf_op jit(solution)/shard_map/pallas_call | solution.py:167
  12.2 0.0 copy-start.2
  12.2 0.0 copy-start.4
  12.2 2.6 %project.1.q_ref = f32[512,512]{1,0:T(8,128)S(1)} custom-call(f32[512,1024]{1,0:T(8,128)S(1)} %shard_map.64.first_ref.field0_ref, f32[512,1024]{1,0:T(8,128)S(1)} %shard_map.65.second_ref.field1_ref, bf16[512,2048]{1,0:T(8,128)(2,1)S(1)} %get-tuple-element.26.wide_ref), custom_call_target="tpu_custom_call" | custom-call | flops 2147483648 | bytes 7000000 | tf_op jit(solution)/shard_map/project/pallas_call | solution.py:192
  14.8 4.1 %solve_early.1 = (f32[128,128]{1,0:T(8,128)S(1)}, f32[64,128]{1,0:T(8,128)S(1)}, f32[128,384]{1,0:T(8,128)S(1)}) custom-call(s32[7,128]{1,0:T(8,128)S(1)} %copy-done.4, f32[7,1,64,64]{3,2,1,0:T(8,128)S(1)} %copy-done.2, f32[128,128]{1,0:T(8,128)S(1)} %get-tuple-element.27.gram0_ref, f32[64,384]{1,0:T(8,128)S(1)} %get-tuple-element.28.own1_ref, ...), custom_call_target="tpu_custom_call" | custom-call | flops 3000000000 | bytes 4000000 | tf_op jit(solution)/shard_map/solve_early/pallas_call | solution.py:306
  18.9 0.0 collective-permute-done.2
  18.9 2.0 %collective-permute-start.3 = (f32[9,32,128]{2,1,0:T(8,128)S(1)}, f32[9,32,128]{2,1,0:T(8,128)S(1)}, u32[]{:S(2)}, u32[]{:S(2)}) collective-permute-start(f32[9,32,128]{2,1,0:T(8,128)S(1)} %slice.77), channel_id=1, source_target_pairs={{0,8},{8,0},{16,24},{24,16},{32,40},{40,32},{48,56},{56,48},{1,9},... | collective-permute-start | bytes 442376 | tf_op jit(solution)/shard_map/ppermute | solution.py:559
  21.0 4.1 %collective-permute-done.3 = f32[9,32,128]{2,1,0:T(8,128)S(1)} collective-permute-done((f32[9,32,128]{2,1,0:T(8,128)S(1)}, f32[9,32,128]{2,1,0:T(8,128)S(1)}, u32[]{:S(2)}, u32[]{:S(2)}) %collective-permute-start.3) | collective-permute-done | bytes 147488 | tf_op jit(solution)/shard_map/ppermute | solution.py:559
  25.1 3.4 %collective-permute-start.4 = (f32[6,32,128]{2,1,0:T(8,128)S(1)}, f32[6,32,128]{2,1,0:T(8,128)S(1)}, u32[]{:S(2)}, u32[]{:S(2)}) collective-permute-start(f32[6,32,128]{2,1,0:T(8,128)S(1)} %slice_add_fusion), channel_id=1, source_target_pairs={{0,16},{8,24},{16,0},{24,8},{32,48},{40,56},{48,32},{56,40},{1,17}... | collective-permute-start | bytes 294920 | tf_op jit(solution)/shard_map/ppermute | solution.py:559
  28.4 4.5 %collective-permute-done.4 = f32[6,32,128]{2,1,0:T(8,128)S(1)} collective-permute-done((f32[6,32,128]{2,1,0:T(8,128)S(1)}, f32[6,32,128]{2,1,0:T(8,128)S(1)}, u32[]{:S(2)}, u32[]{:S(2)}) %collective-permute-start.4) | collective-permute-done | bytes 98336 | tf_op jit(solution)/shard_map/ppermute | solution.py:559
  32.9 4.9 %collective-permute-start.5 = (f32[4,32,128]{2,1,0:T(8,128)S(1)}, f32[4,32,128]{2,1,0:T(8,128)S(1)}, u32[]{:S(2)}, u32[]{:S(2)}) collective-permute-start(f32[4,32,128]{2,1,0:T(8,128)S(1)} %slice_add_fusion.1), channel_id=1, source_target_pairs={{0,56},{8,48},{16,40},{24,32},{32,24},{40,16},{48,8},{56,0},{1,57}... | collective-permute-start | bytes 196616 | tf_op jit(solution)/shard_map/ppermute | solution.py:559
  37.9 2.5 %collective-permute-done.5 = f32[4,32,128]{2,1,0:T(8,128)S(1)} collective-permute-done((f32[4,32,128]{2,1,0:T(8,128)S(1)}, f32[4,32,128]{2,1,0:T(8,128)S(1)}, u32[]{:S(2)}, u32[]{:S(2)}) %collective-permute-start.5) | collective-permute-done | bytes 65568 | tf_op jit(solution)/shard_map/ppermute | solution.py:559
  40.4 1.5 %collective-permute-start.6 = (f32[2,32,128]{2,1,0:T(8,128)S(1)}, f32[2,32,128]{2,1,0:T(8,128)S(1)}, u32[]{:S(2)}, u32[]{:S(2)}) collective-permute-start(f32[2,32,128]{2,1,0:T(8,128)S(1)} %slice_add_fusion.2), channel_id=1, source_target_pairs={{0,64},{64,0},{128,192},{192,128},{1,65},{65,1},{129,193},{193,129... | collective-permute-start | bytes 98312 | tf_op jit(solution)/shard_map/ppermute | solution.py:559
  41.9 2.4 %collective-permute-done.6 = f32[2,32,128]{2,1,0:T(8,128)S(1)} collective-permute-done((f32[2,32,128]{2,1,0:T(8,128)S(1)}, f32[2,32,128]{2,1,0:T(8,128)S(1)}, u32[]{:S(2)}, u32[]{:S(2)}) %collective-permute-start.6) | collective-permute-done | bytes 32800 | tf_op jit(solution)/shard_map/ppermute | solution.py:559
  44.3 0.3 collective-permute-start.7
  44.6 2.1 %early.1 = (f32[512,128]{1,0:T(8,128)S(1)}, f32[2,128,128]{2,1,0:T(8,128)S(1)}, f32[512,384]{1,0:T(8,128)S(1)}, f32[5,64,128]{2,1,0:T(8,128)S(1)}) custom-call(s32[7,128]{1,0:T(8,128)S(1)} %copy-done.4, f32[7,1,64,64]{3,2,1,0:T(8,128)S(1)} %copy-done.2, f32[512,512]{1,0:T(8,128)S(1)} %project.1.q_ref, f32[128,128]{1,0:T(8,128)S(1)} %get-tuple-element.29.from0_ref, ...), custom_call_target="tpu_custom_call" | custom-call | flops 3000000000 | bytes 4000000 | tf_op jit(solution)/shard_map/early/pallas_call | solution.py:342
  46.8 6.9 %late.1 = (f32[5,128,128]{2,1,0:T(8,128)S(1)}, f32[5,128,128]{2,1,0:T(8,128)S(1)}) custom-call(s32[7,128]{1,0:T(8,128)S(1)} %copy-done.4, f32[5,64,128]{2,1,0:T(8,128)S(1)} %get-tuple-element.35.joint_ref, f32[9,32,128]{2,1,0:T(8,128)S(1)} %constant_dynamic-update-slice_fusion.near_ref, f32[9,32,128]{2,1,0:T(8,128)S(1)} %collective-permute-done.7.far_ref, ...), custom_call_target="tpu_custom_call" | custom-call | flops 4000000000 | bytes 4000000 | tf_op jit(solution)/shard_map/late/pallas_call | solution.py:389
  53.7 0.6 collective-permute-start.8
  54.2 1.3 %collective-permute-done.8.recv_ref = f32[5,128,128]{2,1,0:T(8,128)S(1)} collective-permute-done((f32[5,128,128]{2,1,0:T(8,128)S(1)}, f32[5,128,128]{2,1,0:T(8,128)S(1)}, u32[]{:S(2)}, u32[]{:S(2)}) %collective-permute-start.8) | collective-permute-done | bytes 327712 | tf_op jit(solution)/shard_map/ppermute | solution.py:559
  55.5 21.7 %all_to_all.10.got_ref = f32[32,16,128]{2,1,0:T(8,128)S(1)} all-to-all(f32[32,16,128]{2,1,0:T(8,128)S(1)} %deal.1), channel_id=1, replica_groups=mesh['x'=4,'z'=8,'core'=2,'cols'=4] {'x','z'}, dimensions={0} | all-to-all | bytes 524288 | tf_op jit(solution)/shard_map/all_to_all | solution.py:596
  77.3 16.6 %all_to_all.11.near_ref = f32[32,16,128]{2,1,0:T(8,128)S(1)} all-to-all(f32[32,16,128]{2,1,0:T(8,128)S(1)} %collect.1), channel_id=1, replica_groups=mesh['x'=4,'z'=8,'core'=2,'cols'=4] {'x','z'}, dimensions={0} | all-to-all | bytes 524288 | tf_op jit(solution)/shard_map/all_to_all | solution.py:599
  93.9 1.8 %collective-permute-start.9 = (f32[128,128]{1,0:T(8,128)S(1)}, f32[128,128]{1,0:T(8,128)S(1)}, u32[]{:S(2)}, u32[]{:S(2)}) collective-permute-start(f32[128,128]{1,0:T(8,128)S(1)} %two.1), channel_id=1, source_target_pairs={{0,8},{8,0},{16,24},{24,16},{32,40},{40,32},{48,56},{56,48},{1,9},... | collective-permute-start | bytes 196616 | tf_op jit(solution)/shard_map/ppermute | solution.py:559
  95.7 0.2 collective-permute-start.1
  95.9 2.6 %collective-permute-done.9.near2_ref = f32[128,128]{1,0:T(8,128)S(1)} collective-permute-done((f32[128,128]{1,0:T(8,128)S(1)}, f32[128,128]{1,0:T(8,128)S(1)}, u32[]{:S(2)}, u32[]{:S(2)}) %collective-permute-start.9) | collective-permute-done | bytes 65568 | tf_op jit(solution)/shard_map/ppermute | solution.py:559
  98.5 1.2 %collective-permute-done.10.far2_ref = f32[128,128]{1,0:T(8,128)S(1)} collective-permute-done((f32[128,128]{1,0:T(8,128)S(1)}, f32[128,128]{1,0:T(8,128)S(1)}, u32[]{:S(2)}, u32[]{:S(2)}) %collective-permute-start.10) | collective-permute-done | bytes 65568 | tf_op jit(solution)/shard_map/ppermute | solution.py:559
  99.8 7.0 %final.1 = f32[512,2048]{1,0:T(8,128)} custom-call(f32[512,1024]{1,0:T(8,128)S(1)} %shard_map.64.first_ref.field0_ref, f32[512,1024]{1,0:T(8,128)} %copy-done, bf16[512,2048]{1,0:T(8,128)(2,1)} %copy-done.1, f32[512,128]{1,0:T(8,128)S(1)} %get-tuple-element.33.u0_ref, f32[2,128,128]{2,1,0:T(8,128)S(1)} %collective-permute-done.1.u1_ref, ...), custom_call_target="tpu_custom_call" | custom-call | flops 2147483648 | bytes 12000000 | tf_op jit(solution)/shard_map/final/pallas_call | solution.py:540
  (31 shorter events, 0.2 us)
Async XLA Ops:
  0.0 3.5 %copy-start.3 = (s32[2048]{0:T(1024)S(1)}, s32[2048]{0:T(1024)}, u32[]{:S(2)}) copy-start(s32[2048]{0:T(1024)} %param.7) | copy-start | bytes 24580
  2.9 9.3 %copy-start.1 = (bf16[512,2048]{1,0:T(8,128)(2,1)}, bf16[512,2048]{1,0:T(8,128)(2,1)S(1)}, u32[]{:S(2)}) copy-start(bf16[512,2048]{1,0:T(8,128)(2,1)S(1)} %get-tuple-element.26.wide_ref) | copy-start | bytes 6291460
  2.9 16.0 %collective-permute-start.2 = (f32[12,32,128]{2,1,0:T(8,128)S(1)}, f32[12,32,128]{2,1,0:T(8,128)S(1)}, u32[]{:S(2)}, u32[]{:S(2)}) collective-permute-start(f32[12,32,128]{2,1,0:T(8,128)S(1)} %get-tuple-element.37), channel_id=1, source_target_pairs={{0,4},{4,0},{1,5},{5,1},{2,6},{6,2},{3,7},{7,3},{8,12},{12,8},{9,1... | collective-permute-start | bytes 589832 | tf_op jit(solution)/shard_map/ppermute | solution.py:559
  3.0 11.8 %collective-permute-start = (f32[64,384]{1,0:T(8,128)S(1)}, f32[64,384]{1,0:T(8,128)S(1)}, u32[]{:S(2)}, u32[]{:S(2)}) collective-permute-start(f32[64,384]{1,0:T(8,128)S(1)} %get-tuple-element.28.own1_ref), channel_id=1, source_target_pairs={{0,4},{4,0},{1,5},{5,1},{2,6},{6,2},{3,7},{7,3},{8,12},{12,8},{9,1... | collective-permute-start | bytes 294920 | tf_op jit(solution)/shard_map/ppermute | solution.py:559
  12.1 2.6 %copy-start = (f32[512,1024]{1,0:T(8,128)}, f32[512,1024]{1,0:T(8,128)S(1)}, u32[]{:S(2)}) copy-start(f32[512,1024]{1,0:T(8,128)S(1)} %shard_map.65.second_ref.field1_ref) | copy-start | bytes 6291460
  12.2 2.6 %copy-start.2 = (f32[7,1,64,64]{3,2,1,0:T(8,128)S(1)}, f32[7,1,64,64]{3,2,1,0:T(8,128)}, u32[]{:S(2)}) copy-start(f32[7,1,64,64]{3,2,1,0:T(8,128)} %link_ref.3) | copy-start | bytes 344068
  12.2 2.6 %copy-start.4 = (s32[7,128]{1,0:T(8,128)S(1)}, s32[7,128]{1,0:T(8,128)}, u32[]{:S(2)}) copy-start(s32[7,128]{1,0:T(8,128)} %ranks_ref.5) | copy-start | bytes 10756
  18.9 6.1 %collective-permute-start.3 = (f32[9,32,128]{2,1,0:T(8,128)S(1)}, f32[9,32,128]{2,1,0:T(8,128)S(1)}, u32[]{:S(2)}, u32[]{:S(2)}) collective-permute-start(f32[9,32,128]{2,1,0:T(8,128)S(1)} %slice.77), channel_id=1, source_target_pairs={{0,8},{8,0},{16,24},{24,16},{32,40},{40,32},{48,56},{56,48},{1,9},... | collective-permute-start | bytes 442376 | tf_op jit(solution)/shard_map/ppermute | solution.py:559
  25.1 7.8 %collective-permute-start.4 = (f32[6,32,128]{2,1,0:T(8,128)S(1)}, f32[6,32,128]{2,1,0:T(8,128)S(1)}, u32[]{:S(2)}, u32[]{:S(2)}) collective-permute-start(f32[6,32,128]{2,1,0:T(8,128)S(1)} %slice_add_fusion), channel_id=1, source_target_pairs={{0,16},{8,24},{16,0},{24,8},{32,48},{40,56},{48,32},{56,40},{1,17}... | collective-permute-start | bytes 294920 | tf_op jit(solution)/shard_map/ppermute | solution.py:559
  32.9 7.5 %collective-permute-start.5 = (f32[4,32,128]{2,1,0:T(8,128)S(1)}, f32[4,32,128]{2,1,0:T(8,128)S(1)}, u32[]{:S(2)}, u32[]{:S(2)}) collective-permute-start(f32[4,32,128]{2,1,0:T(8,128)S(1)} %slice_add_fusion.1), channel_id=1, source_target_pairs={{0,56},{8,48},{16,40},{24,32},{32,24},{40,16},{48,8},{56,0},{1,57}... | collective-permute-start | bytes 196616 | tf_op jit(solution)/shard_map/ppermute | solution.py:559
  40.4 3.9 %collective-permute-start.6 = (f32[2,32,128]{2,1,0:T(8,128)S(1)}, f32[2,32,128]{2,1,0:T(8,128)S(1)}, u32[]{:S(2)}, u32[]{:S(2)}) collective-permute-start(f32[2,32,128]{2,1,0:T(8,128)S(1)} %slice_add_fusion.2), channel_id=1, source_target_pairs={{0,64},{64,0},{128,192},{192,128},{1,65},{65,1},{129,193},{193,129... | collective-permute-start | bytes 98312 | tf_op jit(solution)/shard_map/ppermute | solution.py:559
  44.3 2.4 %collective-permute-start.7 = (f32[9,32,128]{2,1,0:T(8,128)S(1)}, f32[9,32,128]{2,1,0:T(8,128)S(1)}, u32[]{:S(2)}, u32[]{:S(2)}) collective-permute-start(f32[9,32,128]{2,1,0:T(8,128)S(1)} %constant_dynamic-update-slice_fusion.near_ref), channel_id=1, source_target_pairs={{0,4},{4,0},{1,5},{5,1},{2,6},{6,2},{3,7},{7,3},{8,12},{12,8},{9,1... | collective-permute-start | bytes 442376 | tf_op jit(solution)/shard_map/ppermute | solution.py:559
  53.7 1.8 %collective-permute-start.8 = (f32[5,128,128]{2,1,0:T(8,128)S(1)}, f32[5,128,128]{2,1,0:T(8,128)S(1)}, u32[]{:S(2)}, u32[]{:S(2)}) collective-permute-start(f32[5,128,128]{2,1,0:T(8,128)S(1)} %get-tuple-element.40), channel_id=1, source_target_pairs={{0,4},{4,0},{1,5},{5,1},{2,6},{6,2},{3,7},{7,3},{8,12},{12,8},{9,1... | collective-permute-start | bytes 983048 | tf_op jit(solution)/shard_map/ppermute | solution.py:559
  93.9 5.9 %collective-permute-start.11 = (f32[32,16,128]{2,1,0:T(8,128)S(1)}, f32[32,16,128]{2,1,0:T(8,128)S(1)}, u32[]{:S(2)}, u32[]{:S(2)}) collective-permute-start(f32[32,16,128]{2,1,0:T(8,128)S(1)} %all_to_all.11.near_ref), channel_id=1, source_target_pairs={{0,4},{4,0},{1,5},{5,1},{2,6},{6,2},{3,7},{7,3},{8,12},{12,8},{9,1... | collective-permute-start | bytes 786440 | tf_op jit(solution)/shard_map/ppermute | solution.py:559
  93.9 4.6 %collective-permute-start.9 = (f32[128,128]{1,0:T(8,128)S(1)}, f32[128,128]{1,0:T(8,128)S(1)}, u32[]{:S(2)}, u32[]{:S(2)}) collective-permute-start(f32[128,128]{1,0:T(8,128)S(1)} %two.1), channel_id=1, source_target_pairs={{0,8},{8,0},{16,24},{24,16},{32,40},{40,32},{48,56},{56,48},{1,9},... | collective-permute-start | bytes 196616 | tf_op jit(solution)/shard_map/ppermute | solution.py:559
  95.7 2.8 %collective-permute-start.1 = (f32[2,128,128]{2,1,0:T(8,128)S(1)}, f32[2,128,128]{2,1,0:T(8,128)S(1)}, u32[]{:S(2)}, u32[]{:S(2)}) collective-permute-start(f32[2,128,128]{2,1,0:T(8,128)S(1)} %get-tuple-element.34), channel_id=1, source_target_pairs={{0,4},{4,0},{1,5},{5,1},{2,6},{6,2},{3,7},{7,3},{8,12},{12,8},{9,1... | collective-permute-start | bytes 393224 | tf_op jit(solution)/shard_map/ppermute | solution.py:559
  98.5 1.3 %collective-permute-start.10 = (f32[128,128]{1,0:T(8,128)S(1)}, f32[128,128]{1,0:T(8,128)S(1)}, u32[]{:S(2)}, u32[]{:S(2)}) collective-permute-start(f32[128,128]{1,0:T(8,128)S(1)} %collective-permute-done.9.near2_ref), channel_id=1, source_target_pairs={{0,4},{4,0},{1,5},{5,1},{2,6},{6,2},{3,7},{7,3},{8,12},{12,8},{9,1... | collective-permute-start | bytes 196616 | tf_op jit(solution)/shard_map/ppermute | solution.py:559

commit v5 on v4

--- a/solution.py
+++ b/solution.py
@@ -18,6 +18,7 @@
 LEAF, R, ROWS, COLS, LEVELS = 1024, 64, 2048, 512, 7
 UP = (LEVELS - 1) * R
 BLK = 256
+WIDE = 512
 MIB = 1024 * 1024
 VMEM = pl.BlockSpec(memory_space=pltpu.VMEM)
 SMEM = pl.BlockSpec(memory_space=pltpu.SMEM)
@@ -470,18 +471,18 @@
 def final_kernel(field0_ref, field1_ref, wide_ref, u0_ref, u1_ref, near2_ref, far2_ref, near_ref, far_ref,
                  out_ref, left_ref, all_ref, wide_vmem, field_vmem, sems):
     step = pl.program_id(0)
-    half = step // (LEAF // BLK)
+    half = step // (LEAF // WIDE)
     loads = [
         pltpu.make_async_copy(
-            wide_ref.at[:, j * BLK:j * BLK + BLK], wide_vmem.at[:, j * BLK:j * BLK + BLK], sems.at[j]
+            wide_ref.at[:, j * WIDE:j * WIDE + WIDE], wide_vmem.at[:, j * WIDE:j * WIDE + WIDE], sems.at[j]
         )
-        for j in range(8)
+        for j in range(4)
     ]
     loads += [
         pltpu.make_async_copy(
-            field1_ref.at[:, j * BLK:j * BLK + BLK], field_vmem.at[:, j * BLK:j * BLK + BLK], sems.at[8 + j]
+            field1_ref.at[:, j * WIDE:j * WIDE + WIDE], field_vmem.at[:, j * WIDE:j * WIDE + WIDE], sems.at[4 + j]
         )
-        for j in range(4)
+        for j in range(2)
     ]
 
     @pl.when(step == 0)
@@ -517,37 +518,37 @@
         left_ref[:, UP:512] = high
         left_ref[:, 512 + UP:] = low
 
-    for j in range(8):
+    for j in range(4):
         @pl.when(step == j)
         def _():
             loads[j].wait()
-            if j >= 4:
-                loads[j + 4].wait()
-
-    right = wide_vmem[:, pl.ds(pl.multiple_of(step * BLK, BLK), BLK)]
+            if j >= 2:
+                loads[j + 2].wait()
+
+    right = wide_vmem[:, pl.ds(pl.multiple_of(step * WIDE, WIDE), WIDE)]
     update = dot(left_ref[:, :512], right, NN) + dot(left_ref[:, 512:], right, NN)
 
     @pl.when(half == 0)
     def _():
-        out_ref[...] = field0_ref[:, pl.ds(pl.multiple_of(step * BLK, BLK), BLK)] - update
+        out_ref[...] = field0_ref[:, pl.ds(pl.multiple_of(step * WIDE, WIDE), WIDE)] - update
 
     @pl.when(half == 1)
     def _():
-        out_ref[...] = field_vmem[:, pl.ds(pl.multiple_of((step - 4) * BLK, BLK), BLK)] - update
+        out_ref[...] = field_vmem[:, pl.ds(pl.multiple_of((step - 2) * WIDE, WIDE), WIDE)] - update
 
 
 def final(field0, field1, wide, *updates):
     return pl.pallas_call(
         final_kernel,
-        grid=(ROWS // BLK,),
+        grid=(ROWS // WIDE,),
         out_shape=shape(COLS, ROWS),
         in_specs=[
             VMEM, HBM, HBM,
         ] + [VMEM] * 6,
-        out_specs=pl.BlockSpec((COLS, BLK), lambda j: (0, j)),
+        out_specs=pl.BlockSpec((COLS, WIDE), lambda j: (0, j)),
         scratch_shapes=[
             pltpu.VMEM((COLS, 1024), BF16), pltpu.VMEM((COLS, UP), F32), pltpu.VMEM((512, ROWS), BF16),
-            pltpu.VMEM((COLS, LEAF), F32), pltpu.SemaphoreType.DMA((12,)),
+            pltpu.VMEM((COLS, LEAF), F32), pltpu.SemaphoreType.DMA((6,)),
         ],
         compiler_params=params(20),
         cost_estimate=cost(2 * COLS * 1024 * ROWS, 12e6),

time: 108 us -> 107 us (level)
  Pallas kernels: 34.2 us -> 33 us
    pallas_call x1, Pallas kernels: 7.03 us -> 5.78 us  [final(): pl.pallas_call(final_kernel, grid=(ROWS // WIDE,), out_shape=shape(COLS,...]
where the time goes in v5:
time: 107 us; the launch traced here: 106 us
  blocking collectives  38.3 us (36%)
  Pallas kernels  33 us (31%)
  waiting for transfers between devices  18.6 us (17%)
  starting transfers between devices  15.3 us (14%)
    all_to_all x1, blocking collectives, local(): got = lax.all_to_all(dealt, ('x', 'z'), 0, 0, tiled=True)  21.7 us
    ppermute x12, waiting for transfers between devices, swap(): lax.ppermute(array, axis, [(i, i ^ mask) for i in range(lax.axis_size(axi...  18.6 us
    all_to_all x1, blocking collectives, local(): back = lax.all_to_all(total, ('x', 'z'), 0, 0, tiled=True)  16.6 us
    ppermute x12, starting transfers between devices, swap(): lax.ppermute(array, axis, [(i, i ^ mask) for i in range(lax.axis_size(axi...  15.3 us
    pallas_call x1, Pallas kernels, late(): pl.pallas_call(late_kernel, out_shape=(shape(5, 128, 128), shape(5, 128,...  6.88 us
    pallas_call x1, Pallas kernels, final(): pl.pallas_call(final_kernel, grid=(ROWS // WIDE,), out_shape=shape(COLS,...  5.78 us
    pallas_call x1, Pallas kernels, solve_early(): pl.pallas_call(solve_early_kernel, out_shape=(shape(128, 128), shape(R, 1...  4.05 us
    pallas_call x1, Pallas kernels, permute_first(): pl.pallas_call(permute_first_kernel, out_shape=(shape(COLS, LEAF, dtype=B...  2.9 us
  transfers between devices with their start and end apart: 12, of which 7 were waited for; matrix products, arithmetic and copies ran while one was open for 0% of the time, Pallas kernels for 16%

profile of v5, /device:TPU:16, one launch (start us, length us, event | category | flops | bytes accessed | tf_op | source)
XLA Modules:
  0.0 105.7 jit_solution(1576075931936121229)
XLA Ops:
  0.0 2.9 %gram.1 = (bf16[512,2048]{1,0:T(8,128)(2,1)S(1)}, f32[12,32,128]{2,1,0:T(8,128)S(1)}, f32[12,32,128]{2,1,0:T(8,128)S(1)}, f32[64,384]{1,0:T(8,128)S(1)}, f32[128...) custom-call(bf16[7,64,2048]{2,1,0:T(8,128)(2,1)} %bases_ref.1, bf16[512,2048]{1,0:T(8,128)(2,1)} %samples_ref.1), custom_call_target="tpu_custom_call" | custom-call | flops 2000000000 | bytes 4000000 | tf_op jit(solution)/shard_map/gram/pallas_call | solution.py:93
  2.9 0.1 collective-permute-start.2
  3.0 0.5 collective-permute-start
  3.5 2.9 %permute_second.1.permuted_ref = bf16[512,1024]{1,0:T(8,128)(2,1)S(1)} custom-call(bf16[512,2048]{1,0:T(8,128)(2,1)S(1)} %get-tuple-element.23.samples_ref, s32[1,2048]{1,0:T(1,128)S(1)} %bitcast.1), custom_call_target="tpu_custom_call" | custom-call | flops 2147483648 | bytes 4000000 | tf_op jit(solution)/shard_map/permute_second/pallas_call | solution.py:147
  6.4 2.9 %permute_first.1 = (bf16[512,1024]{1,0:T(8,128)(2,1)S(1)}, bf16[2,1024,1024]{2,1,0:T(8,128)(2,1)S(1)}) custom-call(bf16[512,2048]{1,0:T(8,128)(2,1)S(1)} %get-tuple-element.23.samples_ref, s32[1,2048]{1,0:T(1,128)S(1)} %bitcast.2, bf16[2,1024,1024]{2,1,0:T(8,128)(2,1)} %factor_ref.1), custom_call_target="tpu_custom_call" | custom-call | flops 2147483648 | bytes 4000000 | tf_op jit(solution)/shard_map/permute_first/pallas_call | solution.py:134
  9.3 1.4 %shard_map.64.first_ref.field0_ref = f32[512,1024]{1,0:T(8,128)S(1)} custom-call(bf16[512,1024]{1,0:T(8,128)(2,1)S(1)} %get-tuple-element.24.permuted_ref, bf16[2,1024,1024]{2,1,0:T(8,128)(2,1)S(1)} %get-tuple-element.25.factor_ref), custom_call_target="tpu_custom_call" | custom-call | flops 1073741824 | bytes 5000000 | tf_op jit(solution)/shard_map/pallas_call | solution.py:168
  10.7 1.4 %shard_map.65.second_ref.field1_ref = f32[512,1024]{1,0:T(8,128)S(1)} custom-call(bf16[512,1024]{1,0:T(8,128)(2,1)S(1)} %permute_second.1.permuted_ref, bf16[2,1024,1024]{2,1,0:T(8,128)(2,1)S(1)} %get-tuple-element.25.factor_ref), custom_call_target="tpu_custom_call" | custom-call | flops 1073741824 | bytes 5000000 | tf_op jit(solution)/shard_map/pallas_call | solution.py:168
  12.2 0.0 copy-start.2
  12.2 0.0 copy-start.4
  12.2 2.6 %project.1.q_ref = f32[512,512]{1,0:T(8,128)S(1)} custom-call(f32[512,1024]{1,0:T(8,128)S(1)} %shard_map.64.first_ref.field0_ref, f32[512,1024]{1,0:T(8,128)S(1)} %shard_map.65.second_ref.field1_ref, bf16[512,2048]{1,0:T(8,128)(2,1)S(1)} %get-tuple-element.26.wide_ref), custom_call_target="tpu_custom_call" | custom-call | flops 2147483648 | bytes 7000000 | tf_op jit(solution)/shard_map/project/pallas_call | solution.py:193
  14.8 4.1 %solve_early.1 = (f32[128,128]{1,0:T(8,128)S(1)}, f32[64,128]{1,0:T(8,128)S(1)}, f32[128,384]{1,0:T(8,128)S(1)}) custom-call(s32[7,128]{1,0:T(8,128)S(1)} %copy-done.4, f32[7,1,64,64]{3,2,1,0:T(8,128)S(1)} %copy-done.2, f32[128,128]{1,0:T(8,128)S(1)} %get-tuple-element.27.gram0_ref, f32[64,384]{1,0:T(8,128)S(1)} %get-tuple-element.28.own1_ref, ...), custom_call_target="tpu_custom_call" | custom-call | flops 3000000000 | bytes 4000000 | tf_op jit(solution)/shard_map/solve_early/pallas_call | solution.py:307
  18.9 0.0 collective-permute-done.2
  18.9 2.0 %collective-permute-start.3 = (f32[9,32,128]{2,1,0:T(8,128)S(1)}, f32[9,32,128]{2,1,0:T(8,128)S(1)}, u32[]{:S(2)}, u32[]{:S(2)}) collective-permute-start(f32[9,32,128]{2,1,0:T(8,128)S(1)} %slice.77), channel_id=1, source_target_pairs={{0,8},{8,0},{16,24},{24,16},{32,40},{40,32},{48,56},{56,48},{1,9},... | collective-permute-start | bytes 442376 | tf_op jit(solution)/shard_map/ppermute | solution.py:560
  21.0 4.1 %collective-permute-done.3 = f32[9,32,128]{2,1,0:T(8,128)S(1)} collective-permute-done((f32[9,32,128]{2,1,0:T(8,128)S(1)}, f32[9,32,128]{2,1,0:T(8,128)S(1)}, u32[]{:S(2)}, u32[]{:S(2)}) %collective-permute-start.3) | collective-permute-done | bytes 147488 | tf_op jit(solution)/shard_map/ppermute | solution.py:560
  25.1 3.4 %collective-permute-start.4 = (f32[6,32,128]{2,1,0:T(8,128)S(1)}, f32[6,32,128]{2,1,0:T(8,128)S(1)}, u32[]{:S(2)}, u32[]{:S(2)}) collective-permute-start(f32[6,32,128]{2,1,0:T(8,128)S(1)} %slice_add_fusion), channel_id=1, source_target_pairs={{0,16},{8,24},{16,0},{24,8},{32,48},{40,56},{48,32},{56,40},{1,17}... | collective-permute-start | bytes 294920 | tf_op jit(solution)/shard_map/ppermute | solution.py:560
  28.4 4.5 %collective-permute-done.4 = f32[6,32,128]{2,1,0:T(8,128)S(1)} collective-permute-done((f32[6,32,128]{2,1,0:T(8,128)S(1)}, f32[6,32,128]{2,1,0:T(8,128)S(1)}, u32[]{:S(2)}, u32[]{:S(2)}) %collective-permute-start.4) | collective-permute-done | bytes 98336 | tf_op jit(solution)/shard_map/ppermute | solution.py:560
  32.9 4.9 %collective-permute-start.5 = (f32[4,32,128]{2,1,0:T(8,128)S(1)}, f32[4,32,128]{2,1,0:T(8,128)S(1)}, u32[]{:S(2)}, u32[]{:S(2)}) collective-permute-start(f32[4,32,128]{2,1,0:T(8,128)S(1)} %slice_add_fusion.1), channel_id=1, source_target_pairs={{0,56},{8,48},{16,40},{24,32},{32,24},{40,16},{48,8},{56,0},{1,57}... | collective-permute-start | bytes 196616 | tf_op jit(solution)/shard_map/ppermute | solution.py:560
  37.9 2.5 %collective-permute-done.5 = f32[4,32,128]{2,1,0:T(8,128)S(1)} collective-permute-done((f32[4,32,128]{2,1,0:T(8,128)S(1)}, f32[4,32,128]{2,1,0:T(8,128)S(1)}, u32[]{:S(2)}, u32[]{:S(2)}) %collective-permute-start.5) | collective-permute-done | bytes 65568 | tf_op jit(solution)/shard_map/ppermute | solution.py:560
  40.4 1.5 %collective-permute-start.6 = (f32[2,32,128]{2,1,0:T(8,128)S(1)}, f32[2,32,128]{2,1,0:T(8,128)S(1)}, u32[]{:S(2)}, u32[]{:S(2)}) collective-permute-start(f32[2,32,128]{2,1,0:T(8,128)S(1)} %slice_add_fusion.2), channel_id=1, source_target_pairs={{0,64},{64,0},{128,192},{192,128},{1,65},{65,1},{129,193},{193,129... | collective-permute-start | bytes 98312 | tf_op jit(solution)/shard_map/ppermute | solution.py:560
  41.9 2.4 %collective-permute-done.6 = f32[2,32,128]{2,1,0:T(8,128)S(1)} collective-permute-done((f32[2,32,128]{2,1,0:T(8,128)S(1)}, f32[2,32,128]{2,1,0:T(8,128)S(1)}, u32[]{:S(2)}, u32[]{:S(2)}) %collective-permute-start.6) | collective-permute-done | bytes 32800 | tf_op jit(solution)/shard_map/ppermute | solution.py:560
  44.3 0.3 collective-permute-start.7
  44.6 2.1 %early.1 = (f32[512,128]{1,0:T(8,128)S(1)}, f32[2,128,128]{2,1,0:T(8,128)S(1)}, f32[512,384]{1,0:T(8,128)S(1)}, f32[5,64,128]{2,1,0:T(8,128)S(1)}) custom-call(s32[7,128]{1,0:T(8,128)S(1)} %copy-done.4, f32[7,1,64,64]{3,2,1,0:T(8,128)S(1)} %copy-done.2, f32[512,512]{1,0:T(8,128)S(1)} %project.1.q_ref, f32[128,128]{1,0:T(8,128)S(1)} %get-tuple-element.29.from0_ref, ...), custom_call_target="tpu_custom_call" | custom-call | flops 3000000000 | bytes 4000000 | tf_op jit(solution)/shard_map/early/pallas_call | solution.py:343
  46.8 6.9 %late.1 = (f32[5,128,128]{2,1,0:T(8,128)S(1)}, f32[5,128,128]{2,1,0:T(8,128)S(1)}) custom-call(s32[7,128]{1,0:T(8,128)S(1)} %copy-done.4, f32[5,64,128]{2,1,0:T(8,128)S(1)} %get-tuple-element.35.joint_ref, f32[9,32,128]{2,1,0:T(8,128)S(1)} %constant_dynamic-update-slice_fusion.near_ref, f32[9,32,128]{2,1,0:T(8,128)S(1)} %collective-permute-done.7.far_ref, ...), custom_call_target="tpu_custom_call" | custom-call | flops 4000000000 | bytes 4000000 | tf_op jit(solution)/shard_map/late/pallas_call | solution.py:390
  53.7 0.6 collective-permute-start.8
  54.2 1.3 %collective-permute-done.8.recv_ref = f32[5,128,128]{2,1,0:T(8,128)S(1)} collective-permute-done((f32[5,128,128]{2,1,0:T(8,128)S(1)}, f32[5,128,128]{2,1,0:T(8,128)S(1)}, u32[]{:S(2)}, u32[]{:S(2)}) %collective-permute-start.8) | collective-permute-done | bytes 327712 | tf_op jit(solution)/shard_map/ppermute | solution.py:560
  55.5 21.7 %all_to_all.10.got_ref = f32[32,16,128]{2,1,0:T(8,128)S(1)} all-to-all(f32[32,16,128]{2,1,0:T(8,128)S(1)} %deal.1), channel_id=1, replica_groups=mesh['x'=4,'z'=8,'core'=2,'cols'=4] {'x','z'}, dimensions={0} | all-to-all | bytes 524288 | tf_op jit(solution)/shard_map/all_to_all | solution.py:597
  77.3 16.6 %all_to_all.11.near_ref = f32[32,16,128]{2,1,0:T(8,128)S(1)} all-to-all(f32[32,16,128]{2,1,0:T(8,128)S(1)} %collect.1), channel_id=1, replica_groups=mesh['x'=4,'z'=8,'core'=2,'cols'=4] {'x','z'}, dimensions={0} | all-to-all | bytes 524288 | tf_op jit(solution)/shard_map/all_to_all | solution.py:600
  93.9 1.8 %collective-permute-start.9 = (f32[128,128]{1,0:T(8,128)S(1)}, f32[128,128]{1,0:T(8,128)S(1)}, u32[]{:S(2)}, u32[]{:S(2)}) collective-permute-start(f32[128,128]{1,0:T(8,128)S(1)} %two.1), channel_id=1, source_target_pairs={{0,8},{8,0},{16,24},{24,16},{32,40},{40,32},{48,56},{56,48},{1,9},... | collective-permute-start | bytes 196616 | tf_op jit(solution)/shard_map/ppermute | solution.py:560
  95.7 0.2 collective-permute-start.1
  95.9 2.6 %collective-permute-done.9.near2_ref = f32[128,128]{1,0:T(8,128)S(1)} collective-permute-done((f32[128,128]{1,0:T(8,128)S(1)}, f32[128,128]{1,0:T(8,128)S(1)}, u32[]{:S(2)}, u32[]{:S(2)}) %collective-permute-start.9) | collective-permute-done | bytes 65568 | tf_op jit(solution)/shard_map/ppermute | solution.py:560
  98.5 1.2 %collective-permute-done.10.far2_ref = f32[128,128]{1,0:T(8,128)S(1)} collective-permute-done((f32[128,128]{1,0:T(8,128)S(1)}, f32[128,128]{1,0:T(8,128)S(1)}, u32[]{:S(2)}, u32[]{:S(2)}) %collective-permute-start.10) | collective-permute-done | bytes 65568 | tf_op jit(solution)/shard_map/ppermute | solution.py:560
  99.8 5.8 %final.1 = f32[512,2048]{1,0:T(8,128)} custom-call(f32[512,1024]{1,0:T(8,128)S(1)} %shard_map.64.first_ref.field0_ref, f32[512,1024]{1,0:T(8,128)} %copy-done, bf16[512,2048]{1,0:T(8,128)(2,1)} %copy-done.1, f32[512,128]{1,0:T(8,128)S(1)} %get-tuple-element.33.u0_ref, f32[2,128,128]{2,1,0:T(8,128)S(1)} %collective-permute-done.1.u1_ref, ...), custom_call_target="tpu_custom_call" | custom-call | flops 2147483648 | bytes 12000000 | tf_op jit(solution)/shard_map/final/pallas_call | solution.py:541
  (31 shorter events, 0.2 us)
Async XLA Ops:
  0.0 3.5 %copy-start.3 = (s32[2048]{0:T(1024)S(1)}, s32[2048]{0:T(1024)}, u32[]{:S(2)}) copy-start(s32[2048]{0:T(1024)} %param.7) | copy-start | bytes 24580
  2.9 9.3 %copy-start.1 = (bf16[512,2048]{1,0:T(8,128)(2,1)}, bf16[512,2048]{1,0:T(8,128)(2,1)S(1)}, u32[]{:S(2)}) copy-start(bf16[512,2048]{1,0:T(8,128)(2,1)S(1)} %get-tuple-element.26.wide_ref) | copy-start | bytes 6291460
  2.9 16.0 %collective-permute-start.2 = (f32[12,32,128]{2,1,0:T(8,128)S(1)}, f32[12,32,128]{2,1,0:T(8,128)S(1)}, u32[]{:S(2)}, u32[]{:S(2)}) collective-permute-start(f32[12,32,128]{2,1,0:T(8,128)S(1)} %get-tuple-element.37), channel_id=1, source_target_pairs={{0,4},{4,0},{1,5},{5,1},{2,6},{6,2},{3,7},{7,3},{8,12},{12,8},{9,1... | collective-permute-start | bytes 589832 | tf_op jit(solution)/shard_map/ppermute | solution.py:560
  3.0 11.8 %collective-permute-start = (f32[64,384]{1,0:T(8,128)S(1)}, f32[64,384]{1,0:T(8,128)S(1)}, u32[]{:S(2)}, u32[]{:S(2)}) collective-permute-start(f32[64,384]{1,0:T(8,128)S(1)} %get-tuple-element.28.own1_ref), channel_id=1, source_target_pairs={{0,4},{4,0},{1,5},{5,1},{2,6},{6,2},{3,7},{7,3},{8,12},{12,8},{9,1... | collective-permute-start | bytes 294920 | tf_op jit(solution)/shard_map/ppermute | solution.py:560
  12.1 2.6 %copy-start = (f32[512,1024]{1,0:T(8,128)}, f32[512,1024]{1,0:T(8,128)S(1)}, u32[]{:S(2)}) copy-start(f32[512,1024]{1,0:T(8,128)S(1)} %shard_map.65.second_ref.field1_ref) | copy-start | bytes 6291460
  12.2 2.6 %copy-start.2 = (f32[7,1,64,64]{3,2,1,0:T(8,128)S(1)}, f32[7,1,64,64]{3,2,1,0:T(8,128)}, u32[]{:S(2)}) copy-start(f32[7,1,64,64]{3,2,1,0:T(8,128)} %link_ref.3) | copy-start | bytes 344068
  12.2 2.6 %copy-start.4 = (s32[7,128]{1,0:T(8,128)S(1)}, s32[7,128]{1,0:T(8,128)}, u32[]{:S(2)}) copy-start(s32[7,128]{1,0:T(8,128)} %ranks_ref.5) | copy-start | bytes 10756
  18.9 6.1 %collective-permute-start.3 = (f32[9,32,128]{2,1,0:T(8,128)S(1)}, f32[9,32,128]{2,1,0:T(8,128)S(1)}, u32[]{:S(2)}, u32[]{:S(2)}) collective-permute-start(f32[9,32,128]{2,1,0:T(8,128)S(1)} %slice.77), channel_id=1, source_target_pairs={{0,8},{8,0},{16,24},{24,16},{32,40},{40,32},{48,56},{56,48},{1,9},... | collective-permute-start | bytes 442376 | tf_op jit(solution)/shard_map/ppermute | solution.py:560
  25.1 7.8 %collective-permute-start.4 = (f32[6,32,128]{2,1,0:T(8,128)S(1)}, f32[6,32,128]{2,1,0:T(8,128)S(1)}, u32[]{:S(2)}, u32[]{:S(2)}) collective-permute-start(f32[6,32,128]{2,1,0:T(8,128)S(1)} %slice_add_fusion), channel_id=1, source_target_pairs={{0,16},{8,24},{16,0},{24,8},{32,48},{40,56},{48,32},{56,40},{1,17}... | collective-permute-start | bytes 294920 | tf_op jit(solution)/shard_map/ppermute | solution.py:560
  32.9 7.5 %collective-permute-start.5 = (f32[4,32,128]{2,1,0:T(8,128)S(1)}, f32[4,32,128]{2,1,0:T(8,128)S(1)}, u32[]{:S(2)}, u32[]{:S(2)}) collective-permute-start(f32[4,32,128]{2,1,0:T(8,128)S(1)} %slice_add_fusion.1), channel_id=1, source_target_pairs={{0,56},{8,48},{16,40},{24,32},{32,24},{40,16},{48,8},{56,0},{1,57}... | collective-permute-start | bytes 196616 | tf_op jit(solution)/shard_map/ppermute | solution.py:560
  40.4 3.9 %collective-permute-start.6 = (f32[2,32,128]{2,1,0:T(8,128)S(1)}, f32[2,32,128]{2,1,0:T(8,128)S(1)}, u32[]{:S(2)}, u32[]{:S(2)}) collective-permute-start(f32[2,32,128]{2,1,0:T(8,128)S(1)} %slice_add_fusion.2), channel_id=1, source_target_pairs={{0,64},{64,0},{128,192},{192,128},{1,65},{65,1},{129,193},{193,129... | collective-permute-start | bytes 98312 | tf_op jit(solution)/shard_map/ppermute | solution.py:560
  44.3 2.4 %collective-permute-start.7 = (f32[9,32,128]{2,1,0:T(8,128)S(1)}, f32[9,32,128]{2,1,0:T(8,128)S(1)}, u32[]{:S(2)}, u32[]{:S(2)}) collective-permute-start(f32[9,32,128]{2,1,0:T(8,128)S(1)} %constant_dynamic-update-slice_fusion.near_ref), channel_id=1, source_target_pairs={{0,4},{4,0},{1,5},{5,1},{2,6},{6,2},{3,7},{7,3},{8,12},{12,8},{9,1... | collective-permute-start | bytes 442376 | tf_op jit(solution)/shard_map/ppermute | solution.py:560
  53.7 1.8 %collective-permute-start.8 = (f32[5,128,128]{2,1,0:T(8,128)S(1)}, f32[5,128,128]{2,1,0:T(8,128)S(1)}, u32[]{:S(2)}, u32[]{:S(2)}) collective-permute-start(f32[5,128,128]{2,1,0:T(8,128)S(1)} %get-tuple-element.40), channel_id=1, source_target_pairs={{0,4},{4,0},{1,5},{5,1},{2,6},{6,2},{3,7},{7,3},{8,12},{12,8},{9,1... | collective-permute-start | bytes 983048 | tf_op jit(solution)/shard_map/ppermute | solution.py:560
  93.9 5.9 %collective-permute-start.11 = (f32[32,16,128]{2,1,0:T(8,128)S(1)}, f32[32,16,128]{2,1,0:T(8,128)S(1)}, u32[]{:S(2)}, u32[]{:S(2)}) collective-permute-start(f32[32,16,128]{2,1,0:T(8,128)S(1)} %all_to_all.11.near_ref), channel_id=1, source_target_pairs={{0,4},{4,0},{1,5},{5,1},{2,6},{6,2},{3,7},{7,3},{8,12},{12,8},{9,1... | collective-permute-start | bytes 786440 | tf_op jit(solution)/shard_map/ppermute | solution.py:560
  93.9 4.6 %collective-permute-start.9 = (f32[128,128]{1,0:T(8,128)S(1)}, f32[128,128]{1,0:T(8,128)S(1)}, u32[]{:S(2)}, u32[]{:S(2)}) collective-permute-start(f32[128,128]{1,0:T(8,128)S(1)} %two.1), channel_id=1, source_target_pairs={{0,8},{8,0},{16,24},{24,16},{32,40},{40,32},{48,56},{56,48},{1,9},... | collective-permute-start | bytes 196616 | tf_op jit(solution)/shard_map/ppermute | solution.py:560
  95.7 2.8 %collective-permute-start.1 = (f32[2,128,128]{2,1,0:T(8,128)S(1)}, f32[2,128,128]{2,1,0:T(8,128)S(1)}, u32[]{:S(2)}, u32[]{:S(2)}) collective-permute-start(f32[2,128,128]{2,1,0:T(8,128)S(1)} %get-tuple-element.34), channel_id=1, source_target_pairs={{0,4},{4,0},{1,5},{5,1},{2,6},{6,2},{3,7},{7,3},{8,12},{12,8},{9,1... | collective-permute-start | bytes 393224 | tf_op jit(solution)/shard_map/ppermute | solution.py:560
  98.5 1.3 %collective-permute-start.10 = (f32[128,128]{1,0:T(8,128)S(1)}, f32[128,128]{1,0:T(8,128)S(1)}, u32[]{:S(2)}, u32[]{:S(2)}) collective-permute-start(f32[128,128]{1,0:T(8,128)S(1)} %collective-permute-done.9.near2_ref), channel_id=1, source_target_pairs={{0,4},{4,0},{1,5},{5,1},{2,6},{6,2},{3,7},{7,3},{8,12},{12,8},{9,1... | collective-permute-start | bytes 196616 | tf_op jit(solution)/shard_map/ppermute | solution.py:560
